TPU v7x, 8 devices: a whole 2x2x1 slice. The times are simulated.
8 devices in a mesh: depth: 2 (over z, y), col: 2 (over x), row: 2 (over core).
Axes of the slice: x: 2, y: 2, z: 1, core: 2. Of those that a mesh axis runs over, the one named last changes fastest.
Arguments:
- weight: bfloat16 [6144, 6144], P(('row', 'depth'), 'col')
- rhs_stack: bfloat16 [3, 6144, 4096], P(None, ('row', 'depth'), 'col')
Outputs:
- output: bfloat16 [3, 6144, 4096], P(None, ('row', 'depth'), 'col')
All inputs are finite; a program needn't handle non-finite values.
Results may differ from a plain program's by a relative error of at most 0.001.
Values are sent between devices in bfloat16 or wider.
A program may use at most 1 GiB of HBM per device.

v0:
```python
import jax
import jax.numpy as jnp
from jax import lax
from jax.sharding import PartitionSpec as P

ALL_AXES = ("depth", "col", "row")


def solution(mesh):
    depth_size = mesh.shape["depth"]
    col_size = mesh.shape["col"]
    row_size = mesh.shape["row"]
    group_size = row_size // col_size
    layer_steps = row_size // depth_size
    all_coords = [(layer_idx, col_idx, row_idx) for layer_idx in range(depth_size) for col_idx in range(col_size) for row_idx in range(row_size)]

    def linear_index(coords):
        layer_idx, col_idx, row_idx = coords
        return (layer_idx * col_size + col_idx) * row_size + row_idx

    def a_source(coords, extra):
        layer_idx, col_idx, row_idx = coords
        block_shift = (row_idx + layer_idx * layer_steps) // group_size
        return linear_index((layer_idx, (col_idx + block_shift + extra) % col_size, row_idx))

    def x_source(coords, piece_idx):
        layer_idx, col_idx, row_idx = coords
        src_row = (row_idx + col_idx * group_size + piece_idx + layer_idx * layer_steps) % row_size
        return linear_index((layer_idx, col_idx, src_row))

    perm_a_near = [(a_source(coords, 0), linear_index(coords)) for coords in all_coords]
    perm_a_next = [(a_source(coords, 1), linear_index(coords)) for coords in all_coords]
    perm_x_pieces = [[(x_source(coords, piece_idx), linear_index(coords)) for coords in all_coords] for piece_idx in range(group_size)]
    perm_col_shift = [(col_idx, (col_idx - 1) % col_size) for col_idx in range(col_size)]
    perm_row_shift = [(row_idx, (row_idx - 1) % row_size) for row_idx in range(row_size)]

    def local_product(w_local, x_local):
        rhs_count = x_local.shape[0]
        slice_rows = x_local.shape[1]
        block_cols = x_local.shape[2] // group_size
        w_layer = lax.all_gather(w_local, "depth", axis=0, tiled=True)
        block_rows = w_layer.shape[0]
        x_split = jnp.transpose(x_local.reshape(rhs_count, slice_rows, group_size, block_cols), (2, 1, 0, 3))
        x_layer = lax.all_gather(x_split, "depth", axis=1, tiled=True)
        layer_idx = lax.axis_index("depth")
        row_idx = lax.axis_index("row")
        offset = (row_idx + layer_idx * layer_steps) % group_size
        w_near = lax.ppermute(w_layer, ALL_AXES, perm_a_near)
        if group_size > 1:
            w_next = lax.ppermute(w_layer, ALL_AXES, perm_a_next)
            w_pair = jnp.concatenate([w_near, w_next], axis=1).reshape(block_rows, 2 * group_size, block_rows)
            w_start = lax.dynamic_slice_in_dim(w_pair, offset, group_size, axis=1)
        else:
            w_start = w_near.reshape(block_rows, 1, block_rows)
        w_blocks = jnp.transpose(w_start, (1, 0, 2))
        x_blocks = jnp.stack([lax.ppermute(x_layer[piece_idx], ALL_AXES, perm_x_pieces[piece_idx]) for piece_idx in range(group_size)], axis=0)
        partial_sum = jnp.einsum("tik,tkrm->tirm", w_blocks, x_blocks, preferred_element_type=jnp.float32)
        for step_idx in range(1, layer_steps):
            w_recv = lax.ppermute(w_blocks[0], "col", perm_col_shift)
            w_blocks = jnp.concatenate([w_blocks[1:], w_recv[None]], axis=0)
            x_blocks = lax.ppermute(x_blocks, "row", perm_row_shift)
            partial_sum = partial_sum + jnp.einsum("tik,tkrm->tirm", w_blocks, x_blocks, preferred_element_type=jnp.float32)
        reduced = lax.psum_scatter(partial_sum, "depth", scatter_dimension=1, tiled=True)
        rounded = reduced.astype(jnp.bfloat16)
        return jnp.transpose(rounded, (2, 1, 0, 3)).reshape(rhs_count, slice_rows, group_size * block_cols)

    return jax.shard_map(local_product, mesh=mesh, in_specs=(P(("row", "depth"), "col"), P(None, ("row", "depth"), "col")), out_specs=P(None, ("row", "depth"), "col"), check_vma=False)
```

profile of v0, /device:TPU:0, one launch (start us, length us, event | category | flops | bytes accessed | tf_op | source)
XLA Modules:
  0.0 1909.1 jit_solution(11525060951702554951)
XLA Ops:
  6.5 0.0 all-gather.5.cloned.1.call-start
  6.5 0.7 all-gather.5.cloned.1.call-update
  7.3 0.0 all-gather.3.cloned.1.call-start
  7.3 0.7 all-gather.3.cloned.1.call-update
  8.0 0.0 reduce-scatter.2.cloned.1.call-start
  8.1 438.1 %all-gather.5.cloned.1.call-done = bf16[1,3072,3,2048]{3,1,2,0:T(8,128)(2,1)} async-done(((bf16[1,1536,3,2048]{3,1,2,0:T(8,128)(2,1)}), bf16[1,3072,3,2048]{3,1,2,0:T(8,128)(2,1)}) %all-gather.5.cloned.1.call-update) | async-done | bytes 37748752 | tf_op jit(solution)/shard_map/all_gather | solution.py:44
  446.1 284.5 %collective-permute-start.1 = (bf16[3072,3,2048]{2,0,1:T(8,128)(2,1)}, bf16[3072,3,2048]{2,0,1:T(8,128)(2,1)}, u32[]{:S(2)}, u32[]{:S(2)}) collective-permute-start(bf16[3072,3,2048]{2,0,1:T(8,128)(2,1)} %bitcast.15), channel_id=1, source_target_pairs={{0,0},{1,1},{3,2},{2,3},{5,4},{4,5},{6,6},{7,7}} | collective-permute-start | bytes 113246216 | tf_op jit(solution)/shard_map/ppermute | solution.py:56
  730.7 0.0 all-gather.3.cloned.1.call-done
  730.7 143.0 %collective-permute-start = (bf16[3072,3072]{1,0:T(8,128)(2,1)}, bf16[3072,3072]{1,0:T(8,128)(2,1)}, u32[]{:S(2)}, u32[]{:S(2)}) collective-permute-start(bf16[3072,3072]{1,0:T(8,128)(2,1)} %all-gather.3.cloned.1.call-done), channel_id=1, source_target_pairs={{0,0},{3,1},{2,2},{1,3},{6,4},{5,5},{4,6},{7,7}} | collective-permute-start | bytes 56623112 | tf_op jit(solution)/shard_map/ppermute | solution.py:48
  873.7 0.0 collective-permute-done
  873.7 0.0 collective-permute-done.1
  873.7 127.8 %convolution_bitcast_fusion = f32[1,3072,3,2048]{3,1,2,0:T(8,128)} fusion(bf16[3072,3,2048]{2,0,1:T(8,128)(2,1)} %collective-permute-done.1, bf16[3072,3072]{1,0:T(8,128)(2,1)} %collective-permute-done), kind=kOutput, calls=%fused_computation | convolution fusion | flops 115964116992 | bytes 132120576 | tf_op jit(solution)/shard_map/tik,tkrm->tirm/dot_general | solution.py:57
  1001.5 0.0 reduce-scatter.2.cloned.1.call-update
  1001.5 880.4 %reduce-scatter.2.cloned.1.call-done = f32[1,1536,3,2048]{3,1,2,0:T(8,128)} async-done(((f32[1,3072,3,2048]{3,1,2,0:T(8,128)}), f32[1,1536,3,2048]{3,1,2,0:T(8,128)}) %reduce-scatter.2.cloned.1.call-update) | async-done | bytes 37748752 | tf_op jit(solution)/shard_map/reduce_scatter | solution.py:63
  1881.9 20.7 %convert_bitcast_fusion = bf16[3,1536,2048]{2,1,0:T(8,128)(2,1)} fusion(f32[1,1536,3,2048]{3,1,2,0:T(8,128)} %reduce-scatter.2.cloned.1.call-done), kind=kLoop, calls=%fused_computation.2 | loop fusion | flops 9437184 | bytes 56623104 | tf_op jit(solution)/shard_map/reshape | solution.py:65
Async XLA Ops:
  6.5 439.6 %all-gather.5.cloned.1.call-start = ((), (), s32[]{:S(2)}) async-start(), calls=%async_computation.2 | async-start | bytes 56623104 | tf_op jit(solution)/shard_map/all_gather | solution.py:44
  7.3 723.4 %all-gather.3.cloned.1.call-start = ((), (), s32[]{:S(2)}) async-start(), calls=%async_computation.1 | async-start | bytes 28311552 | tf_op jit(solution)/shard_map/all_gather | solution.py:41
  8.0 1873.9 %reduce-scatter.2.cloned.1.call-start = ((), (), s32[]{:S(2)}) async-start(), calls=%async_computation.3 | async-start | bytes 113246208 | tf_op jit(solution)/shard_map/reduce_scatter | solution.py:63
  446.1 427.6 %collective-permute-start.1 = (bf16[3072,3,2048]{2,0,1:T(8,128)(2,1)}, bf16[3072,3,2048]{2,0,1:T(8,128)(2,1)}, u32[]{:S(2)}, u32[]{:S(2)}) collective-permute-start(bf16[3072,3,2048]{2,0,1:T(8,128)(2,1)} %bitcast.15), channel_id=1, source_target_pairs={{0,0},{1,1},{3,2},{2,3},{5,4},{4,5},{6,6},{7,7}} | collective-permute-start | bytes 113246216 | tf_op jit(solution)/shard_map/ppermute | solution.py:56
  730.7 143.0 %collective-permute-start = (bf16[3072,3072]{1,0:T(8,128)(2,1)}, bf16[3072,3072]{1,0:T(8,128)(2,1)}, u32[]{:S(2)}, u32[]{:S(2)}) collective-permute-start(bf16[3072,3072]{1,0:T(8,128)(2,1)} %all-gather.3.cloned.1.call-done), channel_id=1, source_target_pairs={{0,0},{3,1},{2,2},{1,3},{6,4},{5,5},{4,6},{7,7}} | collective-permute-start | bytes 56623112 | tf_op jit(solution)/shard_map/ppermute | solution.py:48
Sparse Core Ops, SparseCore 0:
  8.8 437.2 all-gather.4
  447.6 221.9 all-gather.2
  1001.7 880.2 reduce-scatter.1
where the time goes:
time: 1940 us; the launch traced here: 1910 us
  waiting for transfers between devices  1320 us (68%)
  starting transfers between devices  428 us (22%)
  matrix products  128 us (7%)
  other arithmetic  20.7 us (1%)
    reduce_scatter x1, waiting for transfers between devices, local_product(): lax.psum_scatter(partial_sum, 'depth', scatter_dimension=1, tiled=True)  880 us
    all_gather x1, waiting for transfers between devices, local_product(): x_layer = lax.all_gather(x_split, 'depth', axis=1, tiled=True)  438 us
    ppermute x1, starting transfers between devices, local_product(): lax.ppermute(x_layer[piece_idx], ALL_AXES, perm_x_pieces[piece_idx])  285 us
    ppermute x1, starting transfers between devices, local_product(): w_near = lax.ppermute(w_layer, ALL_AXES, perm_a_near)  143 us
    dot_general x1, matrix products, local_product(): jnp.einsum('tik,tkrm->tirm', w_blocks, x_blocks, preferred_element_type=j...  128 us
  transfers between devices with their start and end apart: 5, of which 2 were waited for; matrix products, arithmetic and copies ran while one was open for 0% of the time, Pallas kernels for 0%

commit v1 on v0

v1 whole, which is shorter than its diff:
```python
import functools

import jax
import jax.numpy as jnp
from jax import lax
from jax.experimental import pallas as pl
from jax.experimental.pallas import tpu as pltpu
from jax.sharding import PartitionSpec as P


SWAP = [(0, 1), (1, 0)]
CHUNKS = (
    (0, 0, 512, 0, 1536),
    (0, 512, 1536, 0, 1536),
    (1, 0, 1024, 0, 1536),
    (1, 1024, 1024, 0, 1536),
    (2, 0, 512, 0, 1536),
    (2, 512, 512, 0, 1536),
    (2, 1024, 512, 0, 1536),
    (2, 1536, 256, 0, 1536),
    (2, 1792, 256, 0, 768),
    (2, 1792, 256, 768, 768),
)
LATE = 4
TAIL = 8
TILE_ROWS = 512
TILE_COLS = 512


def product_kernel(plan, *refs):
    tiles, flips, windows, k_start, k_rows, has_base, has_prev, width, tile_cols = plan
    n_tiles, n_pieces = len(tiles), len(flips)
    a_own, a_far = refs[0], refs[1 : 1 + n_tiles]
    pieces = refs[1 + n_tiles : 1 + n_tiles + n_pieces]
    rest = refs[1 + n_tiles + n_pieces :]
    base_ref = rest[0] if has_base else None
    out_ref, a_all, x_all, a_sems, x_sems = rest[has_base + has_prev :]
    slice_rows = a_own.shape[1] // 2
    layer_idx = lax.axis_index("depth")
    cross = lax.rem(lax.axis_index("col") + lax.axis_index("row"), 2)
    m, n = pl.program_id(0), pl.program_id(1)
    layers = sorted({flip_layer for _, flip_layer in flips})
    n_layers = len(layers)
    col_tiles = width // tile_cols

    def a_copy(side, tile):
        if side == 0:
            source = a_own.at[pl.ds(tiles[tile] * TILE_ROWS, TILE_ROWS)]
        else:
            source = a_far[tile]
        if n_layers == 1:
            start = lax.rem(layer_idx + layers[0], 2) * slice_rows + k_start
            source = source.at[:, pl.ds(pl.multiple_of(start, 128), k_rows)]
        return pltpu.make_async_copy(source, a_all.at[side, pl.ds(tile * TILE_ROWS, TILE_ROWS)], a_sems.at[side, tile])

    def x_copy(idx, tile):
        flip_row, flip_layer = flips[idx]
        slot = lax.rem(cross + flip_row, 2) * n_layers
        if n_layers == 2:
            slot = slot + lax.rem(layer_idx + flip_layer, 2)
        source = pieces[idx]
        start = tile * tile_cols
        if windows[idx] is not None:
            rhs_idx, offset = windows[idx]
            source = source.at[rhs_idx]
            start = start + offset
        return pltpu.make_async_copy(
            source.at[:, pl.ds(start, tile_cols)],
            x_all.at[slot, :, pl.ds(tile * tile_cols, tile_cols)],
            x_sems.at[slot, tile],
        )

    def x_wait(side, tile):
        for layer in range(n_layers):
            slot = side * n_layers + layer
            block = x_all.at[slot, :, pl.ds(tile * tile_cols, tile_cols)]
            pltpu.make_async_copy(block, block, x_sems.at[slot, tile]).wait()

    def x_start(side, tile):
        for idx, (flip_row, _) in enumerate(flips):
            @pl.when(lax.rem(cross + flip_row, 2) == side)
            def _():
                x_copy(idx, tile).start()

    groups = [(0, col, side) for col in range(col_tiles) for side in range(2)]
    groups += [(tile, 0, side) for tile in range(1, n_tiles) for side in range(2)]

    def group_start(index):
        if index < len(groups):
            tile, col, side = groups[index]
            if col == 0:
                a_copy(side, tile).start()
            if tile == 0:
                x_start(side, col)

    def group_wait(index):
        tile, col, side = groups[index]
        if col == 0:
            a_copy(side, tile).wait()
        if tile == 0:
            x_wait(side, col)

    row_range = pl.ds(pl.multiple_of(m * TILE_ROWS, TILE_ROWS), TILE_ROWS)
    col_range = pl.ds(pl.multiple_of(n * tile_cols, tile_cols), tile_cols)
    total = base_ref[...] if has_base else None
    for side in range(2):
        for index, (tile, col, group_side) in enumerate(groups):
            if group_side == side:
                @pl.when((m == tile) & (n == col))
                def _():
                    if index == 0:
                        group_start(0)
                    group_wait(index)
                    if index == 0:
                        group_start(1)
                    group_start(index + 2)

        x_side = x_all[pl.ds(side * n_layers, n_layers), :, col_range].reshape(n_layers * k_rows, tile_cols)
        term = jnp.dot(a_all[side, row_range], x_side, preferred_element_type=jnp.float32)
        total = term if total is None else total + term
    if len(out_ref.shape) == 3:
        out_ref[0] = total.astype(out_ref.dtype)
    else:
        out_ref[...] = total


def product(a_own, a_far, pieces, flips, windows, k_range, width, tiles=(0, 1, 2), base=None, base_start=0, prev=None, out=None):
    rows, half = a_own.shape
    k_start, k_rows = k_range
    any_spec = pl.BlockSpec(memory_space=pl.ANY)
    tile_cols = min(TILE_COLS, width)
    n_layers = len({flip_layer for _, flip_layer in flips})
    operands = [a_own, *(a_far[tile] for tile in tiles), *pieces]
    in_specs = [any_spec] * len(operands)
    first = tiles[0]
    if base is not None:
        operands.append(base)
        in_specs.append(pl.BlockSpec((TILE_ROWS, tile_cols), lambda m, n: (first + m, base_start // tile_cols + n)))
    aliases = {}
    if prev is not None:
        aliases = {len(operands): 0}
        operands.append(prev)
        in_specs.append(any_spec)
    if out is None:
        out_shape = jax.ShapeDtypeStruct((rows, width), jnp.float32)
        out_spec = pl.BlockSpec((TILE_ROWS, tile_cols), lambda m, n: (first + m, n))
    else:
        y_shape, rhs_idx, start = out
        out_shape = jax.ShapeDtypeStruct(y_shape, jnp.bfloat16)
        out_spec = pl.BlockSpec((1, TILE_ROWS, tile_cols), lambda m, n: (rhs_idx, first + m, start // tile_cols + n))
    plan = (tuple(tiles), tuple(flips), tuple(windows), k_start, k_rows, base is not None, prev is not None, width, tile_cols)
    tile_rows = len(tiles) * TILE_ROWS
    vmem = 4 * n_layers * k_rows * (tile_rows + width) + 16 * TILE_ROWS * tile_cols + (8 << 20)
    return pl.pallas_call(
        functools.partial(product_kernel, plan),
        grid=(len(tiles), width // tile_cols),
        out_shape=out_shape,
        in_specs=in_specs,
        out_specs=out_spec,
        scratch_shapes=[
            pltpu.VMEM((2, tile_rows, n_layers * k_rows), jnp.bfloat16),
            pltpu.VMEM((2 * n_layers, k_rows, width), jnp.bfloat16),
            pltpu.SemaphoreType.DMA((2, len(tiles))),
            pltpu.SemaphoreType.DMA((2 * n_layers, width // tile_cols)),
        ],
        input_output_aliases=aliases,
        cost_estimate=pl.CostEstimate(flops=4 * tile_rows * n_layers * k_rows * width, bytes_accessed=4 * tile_rows * half, transcendentals=0),
        compiler_params=pltpu.CompilerParams(dimension_semantics=("arbitrary", "arbitrary"), vmem_limit_bytes=vmem),
        name="product",
    )(*operands)


def tail_kernel(target, *refs):
    a_deep, a_both, x_deep, x_both, base = refs[:5]
    rest = refs[5:]
    total = base[...] + jnp.dot(a_deep[...], x_deep[...], preferred_element_type=jnp.float32)
    total = total + jnp.dot(a_both[...], x_both[...], preferred_element_type=jnp.float32)
    if target is None:
        rest[0][...] = total
        return
    y_ref, stage, sem = rest[1:]
    rhs_idx, start = target
    stage[...] = total.astype(stage.dtype)
    copy = pltpu.make_async_copy(stage, y_ref.at[rhs_idx, :, pl.ds(start, stage.shape[1])], sem)
    copy.start()
    copy.wait()


def tail_product(a_deep, a_both, x_deep, x_both, base, prev=None, target=None):
    vmem_spec = pl.BlockSpec(memory_space=pltpu.VMEM)
    any_spec = pl.BlockSpec(memory_space=pl.ANY)
    operands = [a_deep, a_both, x_deep, x_both, base]
    in_specs = [vmem_spec] * 5
    common = dict(name="tail", compiler_params=pltpu.CompilerParams(vmem_limit_bytes=24 << 20), cost_estimate=pl.CostEstimate(flops=4 * a_deep.size * x_deep.shape[1], bytes_accessed=4 * a_deep.size, transcendentals=0))
    if target is None:
        return pl.pallas_call(functools.partial(tail_kernel, None), out_shape=jax.ShapeDtypeStruct(base.shape, base.dtype), in_specs=in_specs, out_specs=vmem_spec, **common)(*operands)
    return pl.pallas_call(
        functools.partial(tail_kernel, target),
        out_shape=jax.ShapeDtypeStruct(prev.shape, prev.dtype),
        in_specs=in_specs + [any_spec],
        out_specs=any_spec,
        scratch_shapes=[pltpu.VMEM(base.shape, jnp.bfloat16), pltpu.SemaphoreType.DMA],
        input_output_aliases={5: 0},
        **common,
    )(*operands, prev)


OWN, DEEP, PEER, BOTH = (0, 0), (0, 1), (1, 0), (1, 1)


def solution(mesh):
    def permute(value, axis):
        return lax.ppermute(value, axis, SWAP)

    def body(w_local, x_local):
        y_shape = x_local.shape
        slice_rows = y_shape[1]
        n_row_tiles = w_local.shape[0] // TILE_ROWS

        def piece_of(x, chunk):
            rhs_idx, start, width, k_start, k_rows = chunk
            return x[rhs_idx, k_start : k_start + k_rows, start : start + width]

        first = piece_of(x_local, CHUNKS[0])
        first, x_rest, w_rest = lax.optimization_barrier((first, x_local, w_local))
        w_first, w_rest = lax.optimization_barrier((w_rest[:TILE_ROWS], w_rest))
        sends = [first] + [piece_of(x_rest, chunk) for chunk in CHUNKS[1:]]
        deep = [permute(piece, "depth") for piece in sends]
        w_sends = [w_first] + [w_rest[tile * TILE_ROWS : (tile + 1) * TILE_ROWS] for tile in range(1, n_row_tiles)]
        w_far = [permute(piece, "col") for piece in w_sends]
        x_row = permute(x_rest, "row")

        def full(idx, relay, y, tiles):
            rhs_idx, start, width, _, _ = CHUNKS[idx]
            window = (rhs_idx, start)
            return product(w_local, w_far, (x_local, deep[idx], x_row, relay), (OWN, DEEP, PEER, BOTH), (window, None, window, None), (0, slice_rows), width, tiles=tiles, prev=y, out=(y_shape, rhs_idx, start))

        def local(y, x_row, rhs_idx, start, width, tiles, prev=None):
            x_row, y = lax.optimization_barrier((x_row, y))
            window = (rhs_idx, start)
            base = product(w_local, w_far, (x_local, x_row), (OWN, PEER), (window, window), (0, slice_rows), width, tiles=tiles, prev=prev)
            return lax.optimization_barrier((y, base))

        late_rhs, late_start = CHUNKS[LATE][0], CHUNKS[LATE][1]
        main_width = sum(chunk[2] for chunk in CHUNKS[LATE : TAIL - 1])

        relay0 = permute(deep[0], "row")
        y = full(0, relay0, None, (0,))
        y, base = local(y, x_row, late_rhs, late_start, main_width, (0,))
        y = full(0, relay0, y, (1,))
        piece, y = lax.optimization_barrier((deep[1], y))
        relay1 = permute(piece, "row")
        y = full(1, relay1, y, (0, 1))
        y, base = local(y, x_row, late_rhs, late_start, main_width, (1,), prev=base)
        y = full(0, relay0, y, (2,))
        y = full(1, relay1, y, (2,))
        layer_idx = lax.axis_index("depth")
        cross = lax.rem(lax.axis_index("col") + lax.axis_index("row"), 2)

        def tail_weight(flip_row, k_start, k_rows):
            start = lax.rem(layer_idx + 1, 2) * slice_rows + k_start
            own = lax.dynamic_slice_in_dim(w_local, start, k_rows, axis=1)
            far = jnp.concatenate([lax.dynamic_slice_in_dim(tile, start, k_rows, axis=1) for tile in w_far], axis=0)
            return jnp.where(lax.rem(cross + flip_row, 2) == 0, own, far)

        tail_weights = None
        for idx in range(2, len(CHUNKS)):
            rhs_idx, start, width, _, _ = CHUNKS[idx]
            piece, y = lax.optimization_barrier((deep[idx], y))
            relay = permute(piece, "row")
            if idx < LATE:
                y = full(idx, relay, y, (0, 1, 2))
            elif idx < TAIL:
                part, offset = (base, start - late_start) if idx < TAIL - 1 else (base_last, 0)
                y = product(w_local, w_far, (piece, relay), (DEEP, BOTH), (None, None), (0, slice_rows), width, base=part, base_start=offset, prev=y, out=(y_shape, rhs_idx, start))
            elif idx < len(CHUNKS) - 1:
                base_tail = tail_product(*tail_weights[idx - TAIL], piece, relay, base_tail)
            else:
                y = tail_product(*tail_weights[idx - TAIL], piece, relay, base_tail, prev=y, target=(rhs_idx, start))
            if idx == LATE - 1:
                y, base = local(y, x_row, late_rhs, late_start, main_width, (2,), prev=base)
            if idx == LATE:
                for rhs_idx, start, width, _, _ in (CHUNKS[TAIL - 1], CHUNKS[TAIL]):
                    y, part = local(y, x_row, rhs_idx, start, width, (0, 1, 2))
                    base_last, base_tail = (part, None) if start == CHUNKS[TAIL - 1][1] else (base_last, part)
            if idx == TAIL - 3:
                tail_weights = [(tail_weight(0, *chunk[3:]), tail_weight(1, *chunk[3:])) for chunk in CHUNKS[TAIL:]]
                y, tail_weights = lax.optimization_barrier((y, tail_weights))
        return y

    return jax.shard_map(body, mesh=mesh, in_specs=(P(("row", "depth"), "col"), P(None, ("row", "depth"), "col")), out_specs=P(None, ("row", "depth"), "col"), check_vma=False)
```

time: 1940 us -> 522 us (0.27); the launches traced: 1910 us -> 521 us
  waiting for transfers between devices: 1320 us -> 235 us
  starting transfers between devices: 428 us -> 17.6 us
  Pallas kernels: 0 us -> 213 us
  matrix products: 128 us -> 0 us
  local copies, waits for them, and re-layouts: 0 us -> 50.9 us
    reduce_scatter x1 -> x0, waiting for transfers between devices: 880 us -> none  [local_product(): lax.psum_scatter(partial_sum, 'depth', scatter_dimension=1, tiled=True)]
    all_gather x2 -> x0, waiting for transfers between devices: 438 us -> none  [the longest x1 438 us: local_product(): x_layer = lax.all_gather(x_split, 'depth', axis=1, tiled=True)]
    ppermute x2 -> x24, starting transfers between devices: 428 us -> 17.6 us  [permute(): return lax.ppermute(value, axis, SWAP)]
    ppermute x2 -> x24, waiting for transfers between devices: 0.01 us -> 235 us  [permute(): return lax.ppermute(value, axis, SWAP)]
    pallas_call x0 -> x18, Pallas kernels: none -> 213 us  [the longest x16 210 us: product(): pl.pallas_call(functools.partial(product_kernel, plan), grid=(len(tiles),...]
    dot_general x1 -> x0, matrix products: 128 us -> none  [local_product(): jnp.einsum('tik,tkrm->tirm', w_blocks, x_blocks, preferred_element_type=j...]
    unnamed x0 -> x62, local copies, waits for them, and re-layouts: none -> 23.4 us
    squeeze x0 -> x6, local copies, waits for them, and re-layouts: none -> 20.9 us  [piece_of(): return x[rhs_idx, k_start:k_start + k_rows, start:start + width]]
  transfers between devices with their start and end apart: 5 -> 24, of which waited for: 2 -> 13; matrix products, arithmetic and copies ran while one was open for 0% -> 6% of each run, Pallas kernels for 0% -> 40%
where the time goes in v1:
time: 522 us; the launch traced here: 521 us
  waiting for transfers between devices  235 us (45%)
  Pallas kernels  213 us (41%)
  local copies, waits for them, and re-layouts  50.9 us (10%)
  starting transfers between devices  17.6 us (3%)
    ppermute x24, waiting for transfers between devices, permute(): return lax.ppermute(value, axis, SWAP)  235 us
    pallas_call x16, Pallas kernels, product(): pl.pallas_call(functools.partial(product_kernel, plan), grid=(len(tiles),...  210 us
    unnamed x62, local copies, waits for them, and re-layouts  23.4 us
    squeeze x6, local copies, waits for them, and re-layouts, piece_of(): return x[rhs_idx, k_start:k_start + k_rows, start:start + width]  20.9 us
    ppermute x24, starting transfers between devices, permute(): return lax.ppermute(value, axis, SWAP)  17.6 us
  transfers between devices with their start and end apart: 24, of which 13 were waited for; matrix products, arithmetic and copies ran while one was open for 6% of the time, Pallas kernels for 40%

profile of v1, /device:TPU:0, one launch (start us, length us, event | category | flops | bytes accessed | tf_op | source)
XLA Modules:
  0.0 521.4 jit_solution(9446772100615689503)
XLA Ops:
  0.0 1.5 slice_bitcast_fusion.6
  1.5 0.9 collective-permute-start.4
  2.4 5.1 slice_bitcast_fusion
  7.5 2.6 collective-permute-start.8
  10.3 1.5 collective-permute-start
  11.9 1.5 collective-permute-start.9
  13.4 3.1 fusion
  16.5 0.5 collective-permute-start.1
  17.0 129.3 %collective-permute-done.9.refs_3_ = bf16[1536,512]{1,0:T(8,128)(2,1)S(1)} collective-permute-done((bf16[1536,512]{1,0:T(8,128)(2,1)S(1)}, bf16[1536,512]{1,0:T(8,128)(2,1)S(1)}, u32[]{:S(2)}, u32[]{:S(2)}) %collective-permute-start.9) | collective-permute-done | bytes 1572896 | tf_op jit(solution)/shard_map/ppermute | solution.py:213
  146.4 3.4 collective-permute-done.10.refs_5_
  149.8 7.8 %product.16.refs_6_ = bf16[3,1536,2048]{2,1,0:T(8,128)(2,1)} custom-call(bf16[1536,3072]{1,0:T(8,128)(2,1)S(1)} %copy-done, bf16[512,3072]{1,0:T(8,128)(2,1)S(1)} %collective-permute-done.refs_1_, bf16[3,1536,2048]{2,1,0:T(8,128)(2,1)} %refs_4_.7, bf16[1536,512]{1,0:T(8,128)(2,1)S(1)} %collective-permute-done.9.refs_3_, ...), custom_call_target="tpu_custom_call" | custom-call | flops 3221225472 | bytes 6291456 | tf_op jit(solution)/shard_map/product/pallas_call | solution.py:154
  157.6 9.3 %product.17.refs_4_ = f32[1536,1536]{1,0:T(8,128)S(1)} custom-call(bf16[1536,3072]{1,0:T(8,128)(2,1)S(1)} %copy-done, bf16[512,3072]{1,0:T(8,128)(2,1)S(1)} %collective-permute-done.refs_1_, bf16[3,1536,2048]{2,1,0:T(8,128)(2,1)} %refs_4_.7, bf16[3,1536,2048]{2,1,0:T(8,128)(2,1)} %collective-permute-done.4.refs_4_.refs_3_.refs_5_.refs_6_), custom_call_target="tpu_custom_call" | custom-call | flops 4831838208 | bytes 6291456 | tf_op jit(solution)/shard_map/product/pallas_call | solution.py:154
  167.0 3.6 copy-done.7
  170.6 8.4 %product.18.refs_7_ = bf16[3,1536,2048]{2,1,0:T(8,128)(2,1)} custom-call(bf16[1536,3072]{1,0:T(8,128)(2,1)S(1)} %copy-done, bf16[512,3072]{1,0:T(8,128)(2,1)S(1)} %collective-permute-done.1.refs_1_.refs_2_, bf16[3,1536,2048]{2,1,0:T(8,128)(2,1)} %refs_4_.7, bf16[1536,512]{1,0:T(8,128)(2,1)S(1)} %collective-permute-done.9.refs_3_, ...), custom_call_target="tpu_custom_call", output_to_operand_aliasing={{}: (6, {})} | custom-call | flops 3221225472 | bytes 6291456 | tf_op jit(solution)/shard_map/product/pallas_call | solution.py:154
  179.2 1.7 collective-permute-start.2
  180.9 6.4 %slice_bitcast_fusion.1 = (bf16[1536,1024]{1,0:T(8,128)(2,1)}, bf16[1536,1024]{1,0:T(8,128)(2,1)}) fusion(bf16[3,1536,2048]{2,1,0:T(8,128)(2,1)} %refs_4_.7), kind=kLoop, calls=%fused_computation.1 | loop fusion | bytes 12582912 | tf_op jit(solution)/shard_map/squeeze | solution.py:222
  187.2 1.7 collective-permute-start.7
  189.0 28.5 %product.19.refs_6_ = bf16[3,1536,2048]{2,1,0:T(8,128)(2,1)} custom-call(bf16[1536,3072]{1,0:T(8,128)(2,1)} %refs_0_.31, bf16[512,3072]{1,0:T(8,128)(2,1)S(1)} %copy-done.2, bf16[512,3072]{1,0:T(8,128)(2,1)S(1)} %copy-done.5, bf16[3,1536,2048]{2,1,0:T(8,128)(2,1)} %refs_4_.7, ...), custom_call_target="tpu_custom_call", output_to_operand_aliasing={{}: (7, {})} | custom-call | flops 19327352832 | bytes 12582912 | tf_op jit(solution)/shard_map/product/pallas_call | solution.py:154
  217.5 3.7 copy-done.8
  221.2 9.4 %product.20.refs_4_ = f32[1536,1536]{1,0:T(8,128)S(1)} custom-call(bf16[1536,3072]{1,0:T(8,128)(2,1)S(1)} %bitcast.21, bf16[512,3072]{1,0:T(8,128)(2,1)S(1)} %copy-done.5, bf16[3,1536,2048]{2,1,0:T(8,128)(2,1)} %refs_4_.7, bf16[3,1536,2048]{2,1,0:T(8,128)(2,1)} %collective-permute-done.4.refs_4_.refs_3_.refs_5_.refs_6_, ...), custom_call_target="tpu_custom_call", output_to_operand_aliasing={{}: (4, {})} | custom-call | flops 4831838208 | bytes 6291456 | tf_op jit(solution)/shard_map/product/pallas_call | solution.py:154
  230.6 3.6 copy-done.9
  234.2 15.7 %collective-permute-done.2.refs_1_.refs_3_ = bf16[512,3072]{1,0:T(8,128)(2,1)} collective-permute-done((bf16[512,3072]{1,0:T(8,128)(2,1)}, bf16[512,3072]{1,0:T(8,128)(2,1)}, u32[]{:S(2)}, u32[]{:S(2)}) %collective-permute-start.2) | collective-permute-done | bytes 3145760 | tf_op jit(solution)/shard_map/ppermute | solution.py:213
  249.9 8.2 %product.21.refs_6_ = bf16[3,1536,2048]{2,1,0:T(8,128)(2,1)} custom-call(bf16[1536,3072]{1,0:T(8,128)(2,1)S(1)} %bitcast.21, bf16[512,3072]{1,0:T(8,128)(2,1)} %collective-permute-done.2.refs_1_.refs_3_, bf16[3,1536,2048]{2,1,0:T(8,128)(2,1)} %refs_4_.7, bf16[1536,512]{1,0:T(8,128)(2,1)S(1)} %collective-permute-done.9.refs_3_, ...), custom_call_target="tpu_custom_call", output_to_operand_aliasing={{}: (6, {})} | custom-call | flops 3221225472 | bytes 6291456 | tf_op jit(solution)/shard_map/product/pallas_call | solution.py:154
  258.1 18.3 %product.22.refs_8_ = bf16[3,1536,2048]{2,1,0:T(8,128)(2,1)} custom-call(bf16[1536,3072]{1,0:T(8,128)(2,1)} %refs_0_.31, bf16[512,3072]{1,0:T(8,128)(2,1)} %collective-permute-done.2.refs_1_.refs_3_, bf16[3,1536,2048]{2,1,0:T(8,128)(2,1)} %refs_4_.7, bf16[1536,1536]{1,0:T(8,128)(2,1)S(1)} %collective-permute-done.8.refs_4_.refs_3_, ...), custom_call_target="tpu_custom_call", output_to_operand_aliasing={{}: (6, {})} | custom-call | flops 9663676416 | bytes 6291456 | tf_op jit(solution)/shard_map/product/pallas_call | solution.py:154
  276.4 1.8 collective-permute-start.6
  278.2 4.1 collective-permute-done.12.refs_7_
  282.3 1.7 copy-done.19
  284.0 29.0 %product.23.refs_8_ = bf16[3,1536,2048]{2,1,0:T(8,128)(2,1)} custom-call(bf16[1536,3072]{1,0:T(8,128)(2,1)} %refs_0_.31, bf16[512,3072]{1,0:T(8,128)(2,1)S(1)} %copy-done.3, bf16[512,3072]{1,0:T(8,128)(2,1)S(1)} %copy-done.5, bf16[512,3072]{1,0:T(8,128)(2,1)} %collective-permute-done.2.refs_1_.refs_3_, ...), custom_call_target="tpu_custom_call", output_to_operand_aliasing={{}: (8, {})} | custom-call | flops 19327352832 | bytes 18874368 | tf_op jit(solution)/shard_map/product/pallas_call | solution.py:154
  313.0 34.0 %collective-permute-done.6.refs_5_ = bf16[1536,1024]{1,0:T(8,128)(2,1)S(1)} collective-permute-done((bf16[1536,1024]{1,0:T(8,128)(2,1)S(1)}, bf16[1536,1024]{1,0:T(8,128)(2,1)S(1)}, u32[]{:S(2)}, u32[]{:S(2)}) %collective-permute-start.6) | collective-permute-done | bytes 3145760 | tf_op jit(solution)/shard_map/ppermute | solution.py:213
  347.0 5.6 %slice_bitcast_fusion.3 = (bf16[1536,512]{1,0:T(8,128)(2,1)}, bf16[1536,512]{1,0:T(8,128)(2,1)S(1)}, bf16[1536,512]{1,0:T(8,128)(2,1)}) fusion(bf16[3,1536,2048]{2,1,0:T(8,128)(2,1)} %refs_4_.7), kind=kLoop, calls=%fused_computation.9 | loop fusion | bytes 9437184 | tf_op jit(solution)/shard_map/squeeze | solution.py:222
  352.5 1.8 collective-permute-start.5
  354.3 29.0 %product.24.refs_7_ = bf16[3,1536,2048]{2,1,0:T(8,128)(2,1)} custom-call(bf16[1536,3072]{1,0:T(8,128)(2,1)} %refs_0_.31, bf16[512,3072]{1,0:T(8,128)(2,1)S(1)} %copy-done.3, bf16[512,3072]{1,0:T(8,128)(2,1)S(1)} %copy-done.5, bf16[512,3072]{1,0:T(8,128)(2,1)} %collective-permute-done.2.refs_1_.refs_3_, ...), custom_call_target="tpu_custom_call", output_to_operand_aliasing={{}: (8, {})} | custom-call | flops 19327352832 | bytes 18874368 | tf_op jit(solution)/shard_map/product/pallas_call | solution.py:154
  383.3 3.7 copy-done.10
  387.0 10.2 %product.25.refs_6_ = f32[1536,1536]{1,0:T(8,128)S(1)} custom-call(bf16[1536,3072]{1,0:T(8,128)(2,1)S(1)} %bitcast.23, bf16[512,3072]{1,0:T(8,128)(2,1)} %collective-permute-done.2.refs_1_.refs_3_, bf16[3,1536,2048]{2,1,0:T(8,128)(2,1)} %refs_4_.7, ...), custom_call_target="tpu_custom_call", output_to_operand_aliasing={{}: (4, {})} | custom-call | flops 4831838208 | bytes 6291456 | tf_op jit(solution)/shard_map/product/pallas_call | solution.py:154
  397.2 3.6 copy-done.11
  400.8 0.5 collective-permute-start.3
  401.2 2.9 collective-permute-done.14.refs_5_
  404.2 9.1 %product.26.refs_7_ = bf16[3,1536,2048]{2,1,0:T(8,128)(2,1)} custom-call(bf16[1536,3072]{1,0:T(8,128)(2,1)S(1)} %bitcast.23, bf16[512,3072]{1,0:T(8,128)(2,1)S(1)} %copy-done.3, bf16[512,3072]{1,0:T(8,128)(2,1)S(1)} %copy-done.5, bf16[512,3072]{1,0:T(8,128)(2,1)} %collective-permute-done.2.refs_1_.refs_3_, ...), custom_call_target="tpu_custom_call", output_to_operand_aliasing={{}: (7, {})} | custom-call | flops 4831838208 | bytes 18874368 | tf_op jit(solution)/shard_map/product/pallas_call | solution.py:154
  413.3 6.7 %product.27.refs_6_ = f32[1536,256]{1,0:T(8,128)S(1)} custom-call(bf16[1536,3072]{1,0:T(8,128)(2,1)S(1)} %bitcast.23, bf16[512,3072]{1,0:T(8,128)(2,1)S(1)} %copy-done.3, bf16[512,3072]{1,0:T(8,128)(2,1)S(1)} %copy-done.5, bf16[512,3072]{1,0:T(8,128)(2,1)} %collective-permute-done.2.refs_1_.refs_3_, bf16[3,1536,2048]{2,1,0:T(8,128)(2,1)} %refs_4_.7, ...), custom_call_target="tpu_custom_call" | custom-call | flops 2415919104 | bytes 18874368 | tf_op jit(solution)/shard_map/product/pallas_call | solution.py:154
  420.1 1.1 copy-done.16
  421.2 6.7 %product.28.refs_4_ = f32[1536,256]{1,0:T(8,128)S(1)} custom-call(bf16[1536,3072]{1,0:T(8,128)(2,1)S(1)} %bitcast.23, bf16[512,3072]{1,0:T(8,128)(2,1)S(1)} %copy-done.3, bf16[512,3072]{1,0:T(8,128)(2,1)S(1)} %copy-done.5, bf16[512,3072]{1,0:T(8,128)(2,1)} %collective-permute-done.2.refs_1_.refs_3_, bf16[3,1536,2048]{2,1,0:T(8,128)(2,1)} %refs_4_.7, ...), custom_call_target="tpu_custom_call" | custom-call | flops 2415919104 | bytes 18874368 | tf_op jit(solution)/shard_map/product/pallas_call | solution.py:154
  427.9 1.2 copy-done.14
  429.1 8.6 %collective-permute-done.3.refs_4_ = bf16[1536,512]{1,0:T(8,128)(2,1)} collective-permute-done((bf16[1536,512]{1,0:T(8,128)(2,1)S(1)}, bf16[1536,512]{1,0:T(8,128)(2,1)}, u32[]{:S(2)}, u32[]{:S(2)}) %collective-permute-start.3) | collective-permute-done | bytes 1572896 | tf_op jit(solution)/shard_map/ppermute | solution.py:213
  437.7 0.4 collective-permute-start.19
  438.1 1.5 constant_dynamic-slice_fusion.1
  439.6 1.6 constant_dynamic-slice_fusion
  441.5 3.7 broadcast_select_fusion
  445.6 1.0 copy-done.6
  446.5 10.6 %product.29.refs_7_ = bf16[3,1536,2048]{2,1,0:T(8,128)(2,1)} custom-call(bf16[1536,3072]{1,0:T(8,128)(2,1)S(1)} %bitcast.25, bf16[512,3072]{1,0:T(8,128)(2,1)S(1)} %copy-done.3, bf16[512,3072]{1,0:T(8,128)(2,1)S(1)} %copy-done.6, bf16[512,3072]{1,0:T(8,128)(2,1)} %collective-permute-done.2.refs_1_.refs_3_, ...), custom_call_target="tpu_custom_call", output_to_operand_aliasing={{}: (7, {})} | custom-call | flops 4831838208 | bytes 18874368 | tf_op jit(solution)/shard_map/product/pallas_call | solution.py:154
  457.2 17.7 %collective-permute-done.19.refs_4_ = bf16[1536,512]{1,0:T(8,128)(2,1)} collective-permute-done((bf16[1536,512]{1,0:T(8,128)(2,1)}, bf16[1536,512]{1,0:T(8,128)(2,1)}, u32[]{:S(2)}, u32[]{:S(2)}) %collective-permute-start.19) | collective-permute-done | bytes 1572896 | tf_op jit(solution)/shard_map/ppermute | solution.py:213
  474.8 1.2 slice_bitcast_fusion.7
  476.0 0.5 collective-permute-start.18
  476.5 2.0 collective-permute-done.20.refs_5_
  478.4 10.4 %product.30.refs_7_ = bf16[3,1536,2048]{2,1,0:T(8,128)(2,1)} custom-call(bf16[1536,3072]{1,0:T(8,128)(2,1)S(1)} %bitcast.25, bf16[512,3072]{1,0:T(8,128)(2,1)S(1)} %copy-done.3, bf16[512,3072]{1,0:T(8,128)(2,1)S(1)} %copy-done.6, bf16[512,3072]{1,0:T(8,128)(2,1)} %collective-permute-done.2.refs_1_.refs_3_, ...), custom_call_target="tpu_custom_call", output_to_operand_aliasing={{}: (7, {})} | custom-call | flops 4831838208 | bytes 18874368 | tf_op jit(solution)/shard_map/product/pallas_call | solution.py:154
  488.9 7.1 %collective-permute-done.18.refs_4_ = bf16[1536,256]{1,0:T(8,128)(2,1)S(1)} collective-permute-done((bf16[1536,256]{1,0:T(8,128)(2,1)S(1)}, bf16[1536,256]{1,0:T(8,128)(2,1)S(1)}, u32[]{:S(2)}, u32[]{:S(2)}) %collective-permute-start.18) | collective-permute-done | bytes 786464 | tf_op jit(solution)/shard_map/ppermute | solution.py:213
  496.0 1.2 slice_bitcast_fusion.8
  497.2 0.5 collective-permute-start.17
  497.6 1.6 collective-permute-start.16
  499.2 7.8 %product.31.refs_5_ = bf16[3,1536,2048]{2,1,0:T(8,128)(2,1)} custom-call(bf16[1536,3072]{1,0:T(8,128)(2,1)S(1)} %bitcast.25, bf16[512,3072]{1,0:T(8,128)(2,1)S(1)} %copy-done.3, bf16[512,3072]{1,0:T(8,128)(2,1)S(1)} %copy-done.6, bf16[512,3072]{1,0:T(8,128)(2,1)} %collective-permute-done.2.refs_1_.refs_3_, ...), custom_call_target="tpu_custom_call", output_to_operand_aliasing={{}: (7, {})} | custom-call | flops 2415919104 | bytes 18874368 | tf_op jit(solution)/shard_map/product/pallas_call | solution.py:154
  507.1 2.1 collective-permute-done.17.refs_2_
  509.2 8.0 %collective-permute-done.16.refs_2_ = bf16[768,256]{1,0:T(8,128)(2,1)S(1)} collective-permute-done((bf16[768,256]{1,0:T(8,128)(2,1)S(1)}, bf16[768,256]{1,0:T(8,128)(2,1)S(1)}, u32[]{:S(2)}, u32[]{:S(2)}) %collective-permute-start.16) | collective-permute-done | bytes 393248 | tf_op jit(solution)/shard_map/ppermute | solution.py:213
  517.2 1.4 tail.2.refs_4_
  518.6 0.3 collective-permute-done.22.refs_3_
  518.9 2.3 tail.3
  (79 shorter events, 1.0 us)
Async XLA Ops:
  1.5 8.6 %copy-start = (bf16[1536,3072]{1,0:T(8,128)(2,1)S(1)}, bf16[1536,3072]{1,0:T(8,128)(2,1)}, u32[]{:S(2)}) copy-start(bf16[1536,3072]{1,0:T(8,128)(2,1)} %refs_0_.31) | copy-start | bytes 28311556
  1.5 148.2 %collective-permute-start.4 = (bf16[3,1536,2048]{2,1,0:T(8,128)(2,1)}, bf16[3,1536,2048]{2,1,0:T(8,128)(2,1)}, u32[]{:S(2)}, u32[]{:S(2)}) collective-permute-start(bf16[3,1536,2048]{2,1,0:T(8,128)(2,1)} %refs_4_.7), channel_id=1, source_target_pairs={{0,1},{1,0},{2,3},{3,2},{4,5},{5,4},{6,7},{7,6}} | collective-permute-start | bytes 56623112 | tf_op jit(solution)/shard_map/ppermute | solution.py:213
  7.5 171.5 %collective-permute-start.8 = (bf16[1536,1536]{1,0:T(8,128)(2,1)}, bf16[1536,1536]{1,0:T(8,128)(2,1)S(1)}, u32[]{:S(2)}, u32[]{:S(2)}) collective-permute-start(bf16[1536,1536]{1,0:T(8,128)(2,1)} %slice_bitcast_fusion), channel_id=1, source_target_pairs={{0,4},{4,0},{1,5},{5,1},{2,6},{6,2},{3,7},{7,3}} | collective-permute-start | bytes 14155784 | tf_op jit(solution)/shard_map/ppermute | solution.py:213
  10.3 136.0 %collective-permute-start = (bf16[512,3072]{1,0:T(8,128)(2,1)S(1)}, bf16[512,3072]{1,0:T(8,128)(2,1)S(1)}, u32[]{:S(2)}, u32[]{:S(2)}) collective-permute-start(bf16[512,3072]{1,0:T(8,128)(2,1)S(1)} %slice.40), channel_id=1, source_target_pairs={{0,2},{2,0},{1,3},{3,1},{4,6},{6,4},{5,7},{7,5}} | collective-permute-start | bytes 9437192 | tf_op jit(solution)/shard_map/ppermute | solution.py:213
  11.9 134.5 %collective-permute-start.9 = (bf16[1536,512]{1,0:T(8,128)(2,1)S(1)}, bf16[1536,512]{1,0:T(8,128)(2,1)S(1)}, u32[]{:S(2)}, u32[]{:S(2)}) collective-permute-start(bf16[1536,512]{1,0:T(8,128)(2,1)S(1)} %slice_bitcast_fusion.6), channel_id=1, source_target_pairs={{0,4},{4,0},{1,5},{5,1},{2,6},{6,2},{3,7},{7,3}} | collective-permute-start | bytes 4718600 | tf_op jit(solution)/shard_map/ppermute | solution.py:213
  16.5 154.1 %collective-permute-start.1 = (bf16[512,3072]{1,0:T(8,128)(2,1)}, bf16[512,3072]{1,0:T(8,128)(2,1)S(1)}, u32[]{:S(2)}, u32[]{:S(2)}) collective-permute-start(bf16[512,3072]{1,0:T(8,128)(2,1)} %get-tuple-element.115), channel_id=1, source_target_pairs={{0,2},{2,0},{1,3},{3,1},{4,6},{6,4},{5,7},{7,5}} | collective-permute-start | bytes 9437192 | tf_op jit(solution)/shard_map/ppermute | solution.py:213
  146.3 3.4 collective-permute-start.10
  146.4 11.3 %copy-start.1 = (bf16[512,3072]{1,0:T(8,128)(2,1)}, bf16[512,3072]{1,0:T(8,128)(2,1)S(1)}, u32[]{:S(2)}) copy-start(bf16[512,3072]{1,0:T(8,128)(2,1)S(1)} %collective-permute-done.refs_1_) | copy-start | bytes 9437188
  149.8 20.8 %copy-start.12 = (bf16[1536,512]{1,0:T(8,128)(2,1)}, bf16[1536,512]{1,0:T(8,128)(2,1)S(1)}, u32[]{:S(2)}) copy-start(bf16[1536,512]{1,0:T(8,128)(2,1)S(1)} %collective-permute-done.10.refs_5_) | copy-start | bytes 4718596
  167.0 3.6 copy-start.7
  170.6 8.4 %copy-start.4 = (bf16[512,3072]{1,0:T(8,128)(2,1)}, bf16[512,3072]{1,0:T(8,128)(2,1)S(1)}, u32[]{:S(2)}) copy-start(bf16[512,3072]{1,0:T(8,128)(2,1)S(1)} %collective-permute-done.1.refs_1_.refs_2_) | copy-start | bytes 9437188
  179.0 10.0 %collective-permute-start.11 = (bf16[1536,1536]{1,0:T(8,128)(2,1)S(1)}, bf16[1536,1536]{1,0:T(8,128)(2,1)}, u32[]{:S(2)}, u32[]{:S(2)}) collective-permute-start(bf16[1536,1536]{1,0:T(8,128)(2,1)S(1)} %collective-permute-done.8.refs_4_.refs_3_), channel_id=1, source_target_pairs={{0,1},{1,0},{2,3},{3,2},{4,5},{5,4},{6,7},{7,6}} | collective-permute-start | bytes 14155784 | tf_op jit(solution)/shard_map/ppermute | solution.py:213
  179.2 9.8 %copy-start.2 = (bf16[512,3072]{1,0:T(8,128)(2,1)S(1)}, bf16[512,3072]{1,0:T(8,128)(2,1)}, u32[]{:S(2)}) copy-start(bf16[512,3072]{1,0:T(8,128)(2,1)} %copy-done.1) | copy-start | bytes 9437188
  179.2 9.8 %copy-start.5 = (bf16[512,3072]{1,0:T(8,128)(2,1)S(1)}, bf16[512,3072]{1,0:T(8,128)(2,1)}, u32[]{:S(2)}) copy-start(bf16[512,3072]{1,0:T(8,128)(2,1)} %copy-done.4) | copy-start | bytes 9437188
  179.2 70.7 %collective-permute-start.2 = (bf16[512,3072]{1,0:T(8,128)(2,1)}, bf16[512,3072]{1,0:T(8,128)(2,1)}, u32[]{:S(2)}, u32[]{:S(2)}) collective-permute-start(bf16[512,3072]{1,0:T(8,128)(2,1)} %get-tuple-element.114), channel_id=1, source_target_pairs={{0,2},{2,0},{1,3},{3,1},{4,6},{6,4},{5,7},{7,5}} | collective-permute-start | bytes 9437192 | tf_op jit(solution)/shard_map/ppermute | solution.py:213
  180.9 36.6 %slice-start = ((s8[9437184]{0:T(1024)(128)(4,1)}), s8[4194304]{0:T(1024)(128)(4,1)S(1)}, s32[]{:S(2)}) async-start(s8[9437184]{0:T(1024)(128)(4,1)} %bitcast.20), calls=%async_computation | async-start | bytes 8388608
  187.2 30.3 %slice-start.1 = ((s8[9437184]{0:T(1024)(128)(4,1)}), s8[4194304]{0:T(1024)(128)(4,1)S(1)}, s32[]{:S(2)}) async-start(s8[9437184]{0:T(1024)(128)(4,1)} %bitcast.20), calls=%async_computation.1 | async-start | bytes 8388608
  187.2 30.3 %slice-start.2 = ((s8[9437184]{0:T(1024)(128)(4,1)}), s8[1048576]{0:T(1024)(128)(4,1)S(1)}, s32[]{:S(2)}) async-start(s8[9437184]{0:T(1024)(128)(4,1)} %bitcast.20), calls=%async_computation.2 | async-start | bytes 2097152
  187.2 89.2 %collective-permute-start.7 = (bf16[1536,1024]{1,0:T(8,128)(2,1)}, bf16[1536,1024]{1,0:T(8,128)(2,1)}, u32[]{:S(2)}, u32[]{:S(2)}) collective-permute-start(bf16[1536,1024]{1,0:T(8,128)(2,1)} %get-tuple-element.106), channel_id=1, source_target_pairs={{0,4},{4,0},{1,5},{5,1},{2,6},{6,2},{3,7},{7,3}} | collective-permute-start | bytes 9437192 | tf_op jit(solution)/shard_map/ppermute | solution.py:213
  217.5 3.7 copy-start.8
  221.2 28.7 %copy-start.13 = (bf16[1536,512]{1,0:T(8,128)(2,1)S(1)}, bf16[1536,512]{1,0:T(8,128)(2,1)}, u32[]{:S(2)}) copy-start(bf16[1536,512]{1,0:T(8,128)(2,1)} %copy-done.12) | copy-start | bytes 4718596
  230.6 3.6 copy-start.9
  258.1 18.4 %copy-start.20 = (bf16[1536,1024]{1,0:T(8,128)(2,1)S(1)}, bf16[1536,1024]{1,0:T(8,128)(2,1)}, u32[]{:S(2)}) copy-start(bf16[1536,1024]{1,0:T(8,128)(2,1)} %get-tuple-element.107) | copy-start | bytes 9437188
  258.1 25.9 %copy-start.3 = (bf16[512,3072]{1,0:T(8,128)(2,1)S(1)}, bf16[512,3072]{1,0:T(8,128)(2,1)}, u32[]{:S(2)}) copy-start(bf16[512,3072]{1,0:T(8,128)(2,1)} %copy-done.1) | copy-start | bytes 9437188
  276.4 5.9 %collective-permute-start.12 = (bf16[1536,1024]{1,0:T(8,128)(2,1)}, bf16[1536,1024]{1,0:T(8,128)(2,1)S(1)}, u32[]{:S(2)}, u32[]{:S(2)}) collective-permute-start(bf16[1536,1024]{1,0:T(8,128)(2,1)} %collective-permute-done.7.refs_5_), channel_id=1, source_target_pairs={{0,1},{1,0},{2,3},{3,2},{4,5},{5,4},{6,7},{7,6}} | collective-permute-start | bytes 9437192 | tf_op jit(solution)/shard_map/ppermute | solution.py:213
  276.4 70.5 %collective-permute-start.6 = (bf16[1536,1024]{1,0:T(8,128)(2,1)S(1)}, bf16[1536,1024]{1,0:T(8,128)(2,1)S(1)}, u32[]{:S(2)}, u32[]{:S(2)}) collective-permute-start(bf16[1536,1024]{1,0:T(8,128)(2,1)S(1)} %copy-done.20), channel_id=1, source_target_pairs={{0,4},{4,0},{1,5},{5,1},{2,6},{6,2},{3,7},{7,3}} | collective-permute-start | bytes 9437192 | tf_op jit(solution)/shard_map/ppermute | solution.py:213
  282.3 1.7 copy-start.19
  346.9 5.6 %copy-start.18 = (bf16[1536,1024]{1,0:T(8,128)(2,1)}, bf16[1536,1024]{1,0:T(8,128)(2,1)S(1)}, u32[]{:S(2)}) copy-start(bf16[1536,1024]{1,0:T(8,128)(2,1)S(1)} %collective-permute-done.6.refs_5_) | copy-start | bytes 9437188
  346.9 7.3 %collective-permute-start.13 = (bf16[1536,1024]{1,0:T(8,128)(2,1)S(1)}, bf16[1536,1024]{1,0:T(8,128)(2,1)}, u32[]{:S(2)}, u32[]{:S(2)}) collective-permute-start(bf16[1536,1024]{1,0:T(8,128)(2,1)S(1)} %collective-permute-done.6.refs_5_), channel_id=1, source_target_pairs={{0,1},{1,0},{2,3},{3,2},{4,5},{5,4},{6,7},{7,6}} | collective-permute-start | bytes 9437192 | tf_op jit(solution)/shard_map/ppermute | solution.py:213
  347.0 36.3 %slice-start.3 = ((s8[9437184]{0:T(1024)(128)(4,1)}), s8[4194304]{0:T(1024)(128)(4,1)S(1)}, s32[]{:S(2)}) async-start(s8[9437184]{0:T(1024)(128)(4,1)} %bitcast.22), calls=%async_computation.3 | async-start | bytes 8388608
  352.5 30.8 %slice-start.4 = ((s8[9437184]{0:T(1024)(128)(4,1)}), s8[4194304]{0:T(1024)(128)(4,1)S(1)}, s32[]{:S(2)}) async-start(s8[9437184]{0:T(1024)(128)(4,1)} %bitcast.22), calls=%async_computation.4 | async-start | bytes 8388608
  352.5 30.8 %slice-start.5 = ((s8[9437184]{0:T(1024)(128)(4,1)}), s8[1048576]{0:T(1024)(128)(4,1)S(1)}, s32[]{:S(2)}) async-start(s8[9437184]{0:T(1024)(128)(4,1)} %bitcast.22), calls=%async_computation.5 | async-start | bytes 2097152
  352.5 48.3 %collective-permute-start.5 = (bf16[1536,512]{1,0:T(8,128)(2,1)S(1)}, bf16[1536,512]{1,0:T(8,128)(2,1)S(1)}, u32[]{:S(2)}, u32[]{:S(2)}) collective-permute-start(bf16[1536,512]{1,0:T(8,128)(2,1)S(1)} %get-tuple-element.102), channel_id=1, source_target_pairs={{0,4},{4,0},{1,5},{5,1},{2,6},{6,2},{3,7},{7,3}} | collective-permute-start | bytes 4718600 | tf_op jit(solution)/shard_map/ppermute | solution.py:213
  383.3 3.7 copy-start.10
  387.0 13.8 %copy-start.21 = (bf16[1536,512]{1,0:T(8,128)(2,1)S(1)}, bf16[1536,512]{1,0:T(8,128)(2,1)}, u32[]{:S(2)}) copy-start(bf16[1536,512]{1,0:T(8,128)(2,1)} %get-tuple-element.103) | copy-start | bytes 4718596
  397.2 3.6 copy-start.11
  400.8 3.4 collective-permute-start.14
  400.8 36.9 %collective-permute-start.3 = (bf16[1536,512]{1,0:T(8,128)(2,1)S(1)}, bf16[1536,512]{1,0:T(8,128)(2,1)}, u32[]{:S(2)}, u32[]{:S(2)}) collective-permute-start(bf16[1536,512]{1,0:T(8,128)(2,1)S(1)} %copy-done.21), channel_id=1, source_target_pairs={{0,4},{4,0},{1,5},{5,1},{2,6},{6,2},{3,7},{7,3}} | collective-permute-start | bytes 4718600 | tf_op jit(solution)/shard_map/ppermute | solution.py:213
  420.1 1.1 copy-start.16
  427.9 1.2 copy-start.14
  437.7 7.5 %collective-permute-start.15 = (bf16[1536,512]{1,0:T(8,128)(2,1)}, bf16[1536,512]{1,0:T(8,128)(2,1)}, u32[]{:S(2)}, u32[]{:S(2)}) collective-permute-start(bf16[1536,512]{1,0:T(8,128)(2,1)} %collective-permute-done.3.refs_4_), channel_id=1, source_target_pairs={{0,1},{1,0},{2,3},{3,2},{4,5},{5,4},{6,7},{7,6}} | collective-permute-start | bytes 4718600 | tf_op jit(solution)/shard_map/ppermute | solution.py:213
  437.7 37.1 %collective-permute-start.19 = (bf16[1536,512]{1,0:T(8,128)(2,1)}, bf16[1536,512]{1,0:T(8,128)(2,1)}, u32[]{:S(2)}, u32[]{:S(2)}) collective-permute-start(bf16[1536,512]{1,0:T(8,128)(2,1)} %get-tuple-element.101), channel_id=1, source_target_pairs={{0,4},{4,0},{1,5},{5,1},{2,6},{6,2},{3,7},{7,3}} | collective-permute-start | bytes 4718600 | tf_op jit(solution)/shard_map/ppermute | solution.py:213
  439.6 5.6 %slice-start.6 = ((s8[9437184]{0:T(1024)(128)(4,1)}), s8[4194304]{0:T(1024)(128)(4,1)S(1)}, s32[]{:S(2)}) async-start(s8[9437184]{0:T(1024)(128)(4,1)} %bitcast.24), calls=%async_computation.6 | async-start | bytes 8388608
  441.5 3.9 slice-start.7
  441.5 4.1 slice-start.8
  441.5 5.0 copy-start.6
  474.8 3.6 collective-permute-start.20
  476.0 23.2 %copy-start.17 = (f32[1536,256]{1,0:T(8,128)S(1)}, f32[1536,256]{1,0:T(8,128)}, u32[]{:S(2)}) copy-start(f32[1536,256]{1,0:T(8,128)} %copy-done.16) | copy-start | bytes 4718596
  476.0 20.0 %collective-permute-start.18 = (bf16[1536,256]{1,0:T(8,128)(2,1)S(1)}, bf16[1536,256]{1,0:T(8,128)(2,1)S(1)}, u32[]{:S(2)}, u32[]{:S(2)}) collective-permute-start(bf16[1536,256]{1,0:T(8,128)(2,1)S(1)} %slice_bitcast_fusion.7), channel_id=1, source_target_pairs={{0,4},{4,0},{1,5},{5,1},{2,6},{6,2},{3,7},{7,3}} | collective-permute-start | bytes 2359304 | tf_op jit(solution)/shard_map/ppermute | solution.py:213
  496.0 3.2 collective-permute-start.21
  497.2 12.0 %collective-permute-start.17 = (bf16[768,256]{1,0:T(8,128)(2,1)S(1)}, bf16[768,256]{1,0:T(8,128)(2,1)S(1)}, u32[]{:S(2)}, u32[]{:S(2)}) collective-permute-start(bf16[768,256]{1,0:T(8,128)(2,1)S(1)} %get-tuple-element.104), channel_id=1, source_target_pairs={{0,4},{4,0},{1,5},{5,1},{2,6},{6,2},{3,7},{7,3}} | collective-permute-start | bytes 1179656 | tf_op jit(solution)/shard_map/ppermute | solution.py:213
  497.6 19.5 %copy-start.15 = (f32[1536,256]{1,0:T(8,128)S(1)}, f32[1536,256]{1,0:T(8,128)}, u32[]{:S(2)}) copy-start(f32[1536,256]{1,0:T(8,128)} %copy-done.14) | copy-start | bytes 4718596
  497.6 19.5 %collective-permute-start.16 = (bf16[768,256]{1,0:T(8,128)(2,1)S(1)}, bf16[768,256]{1,0:T(8,128)(2,1)S(1)}, u32[]{:S(2)}, u32[]{:S(2)}) collective-permute-start(bf16[768,256]{1,0:T(8,128)(2,1)S(1)} %get-tuple-element.105), channel_id=1, source_target_pairs={{0,4},{4,0},{1,5},{5,1},{2,6},{6,2},{3,7},{7,3}} | collective-permute-start | bytes 1179656 | tf_op jit(solution)/shard_map/ppermute | solution.py:213
  509.2 8.0 %collective-permute-start.23 = (bf16[768,256]{1,0:T(8,128)(2,1)S(1)}, bf16[768,256]{1,0:T(8,128)(2,1)S(1)}, u32[]{:S(2)}, u32[]{:S(2)}) collective-permute-start(bf16[768,256]{1,0:T(8,128)(2,1)S(1)} %collective-permute-done.17.refs_2_), channel_id=1, source_target_pairs={{0,1},{1,0},{2,3},{3,2},{4,5},{5,4},{6,7},{7,6}} | collective-permute-start | bytes 1179656 | tf_op jit(solution)/shard_map/ppermute | solution.py:213
  517.1 1.7 collective-permute-start.22

commit v2 on v1

--- a/solution.py
+++ b/solution.py
@@ -18,13 +18,14 @@
     (2, 512, 512, 0, 1536),
     (2, 1024, 512, 0, 1536),
     (2, 1536, 256, 0, 1536),
+    (2, 1792, 256, 768, 768),
     (2, 1792, 256, 0, 768),
-    (2, 1792, 256, 768, 768),
 )
+SEND_ORDER = (9, 0, 1, 2, 3, 4, 5, 6, 7, 8)
 LATE = 4
-TAIL = 8
 TILE_ROWS = 512
 TILE_COLS = 512
+LOCAL_VMEM = 58 << 20
 
 
 def product_kernel(plan, *refs):
@@ -124,7 +125,7 @@
         out_ref[...] = total
 
 
-def product(a_own, a_far, pieces, flips, windows, k_range, width, tiles=(0, 1, 2), base=None, base_start=0, prev=None, out=None):
+def product(a_own, a_far, pieces, flips, windows, k_range, width, tiles=(0, 1, 2), vmem=None, base=None, base_start=0, prev=None, out=None):
     rows, half = a_own.shape
     k_start, k_rows = k_range
     any_spec = pl.BlockSpec(memory_space=pl.ANY)
@@ -150,7 +151,7 @@
         out_spec = pl.BlockSpec((1, TILE_ROWS, tile_cols), lambda m, n: (rhs_idx, first + m, start // tile_cols + n))
     plan = (tuple(tiles), tuple(flips), tuple(windows), k_start, k_rows, base is not None, prev is not None, width, tile_cols)
     tile_rows = len(tiles) * TILE_ROWS
-    vmem = 4 * n_layers * k_rows * (tile_rows + width) + 16 * TILE_ROWS * tile_cols + (8 << 20)
+    vmem = vmem or 4 * n_layers * k_rows * (tile_rows + width) + 16 * TILE_ROWS * tile_cols + (8 << 20)
     return pl.pallas_call(
         functools.partial(product_kernel, plan),
         grid=(len(tiles), width // tile_cols),
@@ -170,37 +171,88 @@
     )(*operands)
 
 
-def tail_kernel(target, *refs):
-    a_deep, a_both, x_deep, x_both, base = refs[:5]
-    rest = refs[5:]
-    total = base[...] + jnp.dot(a_deep[...], x_deep[...], preferred_element_type=jnp.float32)
-    total = total + jnp.dot(a_both[...], x_both[...], preferred_element_type=jnp.float32)
-    if target is None:
-        rest[0][...] = total
-        return
-    y_ref, stage, sem = rest[1:]
-    rhs_idx, start = target
-    stage[...] = total.astype(stage.dtype)
-    copy = pltpu.make_async_copy(stage, y_ref.at[rhs_idx, :, pl.ds(start, stage.shape[1])], sem)
-    copy.start()
-    copy.wait()
-
-
-def tail_product(a_deep, a_both, x_deep, x_both, base, prev=None, target=None):
+def weight_kernel(layer_flip, *refs):
+    a_own, a_far, out_ref, sems = refs[0], refs[1:-2], refs[-2], refs[-1]
+    slice_rows = out_ref.shape[2]
+    start = pl.multiple_of(lax.rem(lax.axis_index("depth") + layer_flip, 2) * slice_rows, slice_rows)
+    copies = [pltpu.make_async_copy(a_own.at[:, pl.ds(start, slice_rows)], out_ref.at[0], sems.at[0])]
+    for tile, ref in enumerate(a_far):
+        block = out_ref.at[1, pl.ds(tile * TILE_ROWS, TILE_ROWS)]
+        copies.append(pltpu.make_async_copy(ref.at[:, pl.ds(start, slice_rows)], block, sems.at[tile + 1]))
+    for copy in copies:
+        copy.start()
+    for copy in copies:
+        copy.wait()
+
+
+def late_weights(a_own, a_far):
+    rows, half = a_own.shape
+    any_spec = pl.BlockSpec(memory_space=pl.ANY)
+    return pl.pallas_call(
+        functools.partial(weight_kernel, 1),
+        out_shape=jax.ShapeDtypeStruct((2, rows, half // 2), jnp.bfloat16),
+        in_specs=[any_spec] * (1 + len(a_far)),
+        out_specs=pl.BlockSpec(memory_space=pltpu.VMEM),
+        scratch_shapes=[pltpu.SemaphoreType.DMA((1 + len(a_far),))],
+        cost_estimate=pl.CostEstimate(flops=2 * rows * half * 256, bytes_accessed=4 * rows * half, transcendentals=0),
+        compiler_params=pltpu.CompilerParams(vmem_limit_bytes=16 << 20),
+        name="late_weights",
+    )(a_own, *a_far)
+
+
+def late_kernel(k_start, base_start, target, *refs):
+    weights, x_deep, x_both, base = refs[:4]
+    rest = refs[4:]
+    k_rows, width = x_deep.shape
+    cross = lax.rem(lax.axis_index("col") + lax.axis_index("row"), 2)
+    k_range = pl.ds(k_start, k_rows)
+
+    def row_tile(tile, carry):
+        row_range = pl.ds(pl.multiple_of(tile * TILE_ROWS, TILE_ROWS), TILE_ROWS)
+        total = base[row_range, pl.ds(base_start, width)]
+        total = total + jnp.dot(weights[cross, row_range, k_range], x_deep[...], preferred_element_type=jnp.float32)
+        total = total + jnp.dot(weights[1 - cross, row_range, k_range], x_both[...], preferred_element_type=jnp.float32)
+        if target is None:
+            rest[0][row_range] = total
+        else:
+            y_ref, stage, sems = rest[1:]
+            stage[row_range] = total.astype(stage.dtype)
+            out_copy(tile, y_ref, stage, sems).start()
+        return carry
+
+    def out_copy(tile, y_ref, stage, sems):
+        rhs_idx, start = target
+        row_range = pl.ds(pl.multiple_of(tile * TILE_ROWS, TILE_ROWS), TILE_ROWS)
+        return pltpu.make_async_copy(stage.at[row_range], y_ref.at[rhs_idx, row_range, pl.ds(start, width)], sems.at[tile])
+
+    tiles = weights.shape[1] // TILE_ROWS
+    lax.fori_loop(0, tiles, row_tile, 0)
+    if target is not None:
+        for tile in range(tiles):
+            out_copy(tile, *rest[1:]).wait()
+
+
+def late_product(weights, x_deep, x_both, base, base_start, k_start, prev=None, target=None):
     vmem_spec = pl.BlockSpec(memory_space=pltpu.VMEM)
     any_spec = pl.BlockSpec(memory_space=pl.ANY)
-    operands = [a_deep, a_both, x_deep, x_both, base]
-    in_specs = [vmem_spec] * 5
-    common = dict(name="tail", compiler_params=pltpu.CompilerParams(vmem_limit_bytes=24 << 20), cost_estimate=pl.CostEstimate(flops=4 * a_deep.size * x_deep.shape[1], bytes_accessed=4 * a_deep.size, transcendentals=0))
+    rows, width = weights.shape[1], x_deep.shape[1]
+    operands = [weights, x_deep, x_both, base]
+    in_specs = [vmem_spec] * 4
+    common = dict(
+        name="late",
+        compiler_params=pltpu.CompilerParams(vmem_limit_bytes=28 << 20),
+        cost_estimate=pl.CostEstimate(flops=4 * rows * x_deep.size, bytes_accessed=4 * x_deep.size, transcendentals=0),
+    )
+    body = functools.partial(late_kernel, k_start, base_start, target)
     if target is None:
-        return pl.pallas_call(functools.partial(tail_kernel, None), out_shape=jax.ShapeDtypeStruct(base.shape, base.dtype), in_specs=in_specs, out_specs=vmem_spec, **common)(*operands)
+        return pl.pallas_call(body, out_shape=jax.ShapeDtypeStruct((rows, width), jnp.float32), in_specs=in_specs, out_specs=vmem_spec, **common)(*operands)
     return pl.pallas_call(
-        functools.partial(tail_kernel, target),
+        body,
         out_shape=jax.ShapeDtypeStruct(prev.shape, prev.dtype),
         in_specs=in_specs + [any_spec],
         out_specs=any_spec,
-        scratch_shapes=[pltpu.VMEM(base.shape, jnp.bfloat16), pltpu.SemaphoreType.DMA],
-        input_output_aliases={5: 0},
+        scratch_shapes=[pltpu.VMEM((rows, width), jnp.bfloat16), pltpu.SemaphoreType.DMA((rows // TILE_ROWS,))],
+        input_output_aliases={4: 0},
         **common,
     )(*operands, prev)
 
@@ -221,11 +273,14 @@
             rhs_idx, start, width, k_start, k_rows = chunk
             return x[rhs_idx, k_start : k_start + k_rows, start : start + width]
 
-        first = piece_of(x_local, CHUNKS[0])
-        first, x_rest, w_rest = lax.optimization_barrier((first, x_local, w_local))
-        w_first, w_rest = lax.optimization_barrier((w_rest[:TILE_ROWS], w_rest))
-        sends = [first] + [piece_of(x_rest, chunk) for chunk in CHUNKS[1:]]
-        deep = [permute(piece, "depth") for piece in sends]
+        sends = {SEND_ORDER[0]: piece_of(x_local, CHUNKS[SEND_ORDER[0]])}
+        sends[SEND_ORDER[0]], x_rest = lax.optimization_barrier((sends[SEND_ORDER[0]], x_local))
+        second = piece_of(x_rest, CHUNKS[SEND_ORDER[1]])
+        sends[SEND_ORDER[1]], x_rest, w_rest = lax.optimization_barrier((second, x_rest, w_local))
+        w_first, x_rest, w_rest = lax.optimization_barrier((w_rest[:TILE_ROWS], x_rest, w_rest))
+        for idx in SEND_ORDER[2:]:
+            sends[idx] = piece_of(x_rest, CHUNKS[idx])
+        deep = {idx: permute(sends[idx], "depth") for idx in SEND_ORDER}
         w_sends = [w_first] + [w_rest[tile * TILE_ROWS : (tile + 1) * TILE_ROWS] for tile in range(1, n_row_tiles)]
         w_far = [permute(piece, "col") for piece in w_sends]
         x_row = permute(x_rest, "row")
@@ -238,12 +293,14 @@
         def local(y, x_row, rhs_idx, start, width, tiles, prev=None):
             x_row, y = lax.optimization_barrier((x_row, y))
             window = (rhs_idx, start)
-            base = product(w_local, w_far, (x_local, x_row), (OWN, PEER), (window, window), (0, slice_rows), width, tiles=tiles, prev=prev)
+            base = product(w_local, w_far, (x_local, x_row), (OWN, PEER), (window, window), (0, slice_rows), width, tiles=tiles, prev=prev, vmem=LOCAL_VMEM)
             return lax.optimization_barrier((y, base))
 
+        count = len(CHUNKS)
         late_rhs, late_start = CHUNKS[LATE][0], CHUNKS[LATE][1]
-        main_width = sum(chunk[2] for chunk in CHUNKS[LATE : TAIL - 1])
-
+        main_width = sum(chunk[2] for chunk in CHUNKS[LATE : count - 3])
+
+        relay_tail = permute(deep[count - 1], "row")
         relay0 = permute(deep[0], "row")
         y = full(0, relay0, None, (0,))
         y, base = local(y, x_row, late_rhs, late_start, main_width, (0,))
@@ -254,38 +311,26 @@
         y, base = local(y, x_row, late_rhs, late_start, main_width, (1,), prev=base)
         y = full(0, relay0, y, (2,))
         y = full(1, relay1, y, (2,))
-        layer_idx = lax.axis_index("depth")
-        cross = lax.rem(lax.axis_index("col") + lax.axis_index("row"), 2)
-
-        def tail_weight(flip_row, k_start, k_rows):
-            start = lax.rem(layer_idx + 1, 2) * slice_rows + k_start
-            own = lax.dynamic_slice_in_dim(w_local, start, k_rows, axis=1)
-            far = jnp.concatenate([lax.dynamic_slice_in_dim(tile, start, k_rows, axis=1) for tile in w_far], axis=0)
-            return jnp.where(lax.rem(cross + flip_row, 2) == 0, own, far)
-
-        tail_weights = None
-        for idx in range(2, len(CHUNKS)):
-            rhs_idx, start, width, _, _ = CHUNKS[idx]
+        for idx in range(2, count - 1):
+            rhs_idx, start, _, k_start, _ = CHUNKS[idx]
             piece, y = lax.optimization_barrier((deep[idx], y))
             relay = permute(piece, "row")
             if idx < LATE:
                 y = full(idx, relay, y, (0, 1, 2))
-            elif idx < TAIL:
-                part, offset = (base, start - late_start) if idx < TAIL - 1 else (base_last, 0)
-                y = product(w_local, w_far, (piece, relay), (DEEP, BOTH), (None, None), (0, slice_rows), width, base=part, base_start=offset, prev=y, out=(y_shape, rhs_idx, start))
-            elif idx < len(CHUNKS) - 1:
-                base_tail = tail_product(*tail_weights[idx - TAIL], piece, relay, base_tail)
             else:
-                y = tail_product(*tail_weights[idx - TAIL], piece, relay, base_tail, prev=y, target=(rhs_idx, start))
+                part, offset = (base, start - late_start) if idx < count - 3 else (base_last, 0) if idx == count - 3 else (base_tail, 0)
+                y = late_product(weights, piece, relay, part, offset, k_start, prev=y, target=(rhs_idx, start))
             if idx == LATE - 1:
                 y, base = local(y, x_row, late_rhs, late_start, main_width, (2,), prev=base)
-            if idx == LATE:
-                for rhs_idx, start, width, _, _ in (CHUNKS[TAIL - 1], CHUNKS[TAIL]):
-                    y, part = local(y, x_row, rhs_idx, start, width, (0, 1, 2))
-                    base_last, base_tail = (part, None) if start == CHUNKS[TAIL - 1][1] else (base_last, part)
-            if idx == TAIL - 3:
-                tail_weights = [(tail_weight(0, *chunk[3:]), tail_weight(1, *chunk[3:])) for chunk in CHUNKS[TAIL:]]
-                y, tail_weights = lax.optimization_barrier((y, tail_weights))
+                w_gate, y = lax.optimization_barrier((w_local, y))
+                weights = late_weights(w_gate, w_far)
+                y, weights = lax.optimization_barrier((y, weights))
+            if idx == LATE + 1:
+                y, base_last = local(y, x_row, *CHUNKS[count - 3][:3], (0, 1, 2))
+                y, base_tail = local(y, x_row, *CHUNKS[count - 1][:3], (0, 1, 2))
+                piece, y = lax.optimization_barrier((deep[count - 1], y))
+                base_tail = late_product(weights, piece, relay_tail, base_tail, 0, CHUNKS[count - 1][3])
+                y, base_tail = lax.optimization_barrier((y, base_tail))
         return y
 
     return jax.shard_map(body, mesh=mesh, in_specs=(P(("row", "depth"), "col"), P(None, ("row", "depth"), "col")), out_specs=P(None, ("row", "depth"), "col"), check_vma=False)

time: 522 us -> 567 us (1.086)
  waiting for transfers between devices: 235 us -> 283 us
  local copies, waits for them, and re-layouts: 50.9 us -> 58.3 us
    ppermute x24, waiting for transfers between devices: 235 us -> 283 us  [permute(): return lax.ppermute(value, axis, SWAP)]
    pallas_call x16 -> x12, Pallas kernels: 210 us -> 179 us  [product(): pl.pallas_call(functools.partial(product_kernel, plan), grid=(len(tiles),...]
    pallas_call x2 -> x7, Pallas kernels: 3.74 us -> 29.5 us  [the longest x5 24.7 us: late_product(): pl.pallas_call(body, out_shape=jax.ShapeDtypeStruct(prev.shape, prev.dtyp...]
    unnamed x62 -> x50, local copies, waits for them, and re-layouts: 23.4 us -> 30.3 us
    squeeze x6 -> x7, local copies, waits for them, and re-layouts: 20.9 us -> 22.5 us  [piece_of(): return x[rhs_idx, k_start:k_start + k_rows, start:start + width]]
  transfers between devices with their start and end apart: 24 -> 24, of which waited for: 13 -> 13; matrix products, arithmetic and copies ran while one was open for 6% -> 4% of each run, Pallas kernels for 40% -> 36%
where the time goes in v2:
time: 567 us; the launch traced here: 566 us
  waiting for transfers between devices  283 us (50%)
  Pallas kernels  208 us (37%)
  local copies, waits for them, and re-layouts  58.3 us (10%)
  starting transfers between devices  15.9 us (3%)
    ppermute x24, waiting for transfers between devices, permute(): return lax.ppermute(value, axis, SWAP)  283 us
    pallas_call x12, Pallas kernels, product(): pl.pallas_call(functools.partial(product_kernel, plan), grid=(len(tiles),...  179 us
    unnamed x50, local copies, waits for them, and re-layouts  30.3 us
    pallas_call x5, Pallas kernels, late_product(): pl.pallas_call(body, out_shape=jax.ShapeDtypeStruct(prev.shape, prev.dtyp...  24.7 us
    squeeze x7, local copies, waits for them, and re-layouts, piece_of(): return x[rhs_idx, k_start:k_start + k_rows, start:start + width]  22.5 us
    ppermute x24, starting transfers between devices, permute(): return lax.ppermute(value, axis, SWAP)  15.9 us
  transfers between devices with their start and end apart: 24, of which 13 were waited for; matrix products, arithmetic and copies ran while one was open for 4% of the time, Pallas kernels for 36%

profile of v2, /device:TPU:0, one launch (start us, length us, event | category | flops | bytes accessed | tf_op | source)
XLA Modules:
  0.0 566.3 jit_solution(1600425578419531659)
XLA Ops:
  0.0 1.8 slice_bitcast_fusion.9
  1.8 1.7 slice_bitcast_fusion.6
  3.5 2.2 slice.41
  5.7 0.9 collective-permute-start
  6.6 4.8 slice_bitcast_fusion
  11.4 2.6 collective-permute-start.6
  14.0 1.5 collective-permute-start.1
  15.5 0.5 collective-permute-start.7
  16.0 3.2 fusion
  19.3 131.0 %collective-permute-done.7.refs_3_ = bf16[1536,512]{1,0:T(8,128)(2,1)S(1)} collective-permute-done((bf16[1536,512]{1,0:T(8,128)(2,1)S(1)}, bf16[1536,512]{1,0:T(8,128)(2,1)S(1)}, u32[]{:S(2)}, u32[]{:S(2)}) %collective-permute-start.7) | collective-permute-done | bytes 1572896 | tf_op jit(solution)/shard_map/ppermute | solution.py:265
  150.3 3.4 collective-permute-done.8.refs_5_
  153.7 7.5 %product.12.refs_6_ = bf16[3,1536,2048]{2,1,0:T(8,128)(2,1)} custom-call(bf16[1536,3072]{1,0:T(8,128)(2,1)S(1)} %bitcast.21, bf16[512,3072]{1,0:T(8,128)(2,1)S(1)} %collective-permute-done.1.refs_1_, bf16[3,1536,2048]{2,1,0:T(8,128)(2,1)} %refs_4_.7, bf16[1536,512]{1,0:T(8,128)(2,1)S(1)} %collective-permute-done.7.refs_3_, ...), custom_call_target="tpu_custom_call" | custom-call | flops 3221225472 | bytes 6291456 | tf_op jit(solution)/shard_map/product/pallas_call | solution.py:155
  161.2 1.1 copy-done.11
  162.3 11.2 %product.13.refs_4_ = f32[1536,1536]{1,0:T(8,128)} custom-call(bf16[1536,3072]{1,0:T(8,128)(2,1)} %refs_0_.24, bf16[512,3072]{1,0:T(8,128)(2,1)} %copy-done.7, bf16[3,1536,2048]{2,1,0:T(8,128)(2,1)} %refs_4_.7, bf16[3,1536,2048]{2,1,0:T(8,128)(2,1)} %collective-permute-done.refs_4_.refs_3_.refs_5_.refs_6_), custom_call_target="tpu_custom_call" | custom-call | flops 4831838208 | bytes 6291456 | tf_op jit(solution)/shard_map/product/pallas_call | solution.py:155
  173.6 3.7 copy-done
  177.3 1.4 copy-done.12
  178.7 8.2 %product.14.refs_7_ = bf16[3,1536,2048]{2,1,0:T(8,128)(2,1)} custom-call(bf16[1536,3072]{1,0:T(8,128)(2,1)S(1)} %copy-done, bf16[512,3072]{1,0:T(8,128)(2,1)} %collective-permute-done.2.refs_1_.refs_2_, bf16[3,1536,2048]{2,1,0:T(8,128)(2,1)} %refs_4_.7, bf16[1536,512]{1,0:T(8,128)(2,1)S(1)} %collective-permute-done.7.refs_3_, ...), custom_call_target="tpu_custom_call", output_to_operand_aliasing={{}: (6, {})} | custom-call | flops 3221225472 | bytes 6291456 | tf_op jit(solution)/shard_map/product/pallas_call | solution.py:155
  187.0 1.8 collective-permute-start.3
  188.8 6.2 %slice_bitcast_fusion.1 = (bf16[1536,1024]{1,0:T(8,128)(2,1)}, bf16[1536,1024]{1,0:T(8,128)(2,1)}) fusion(bf16[3,1536,2048]{2,1,0:T(8,128)(2,1)} %refs_4_.7), kind=kLoop, calls=%fused_computation.1 | loop fusion | bytes 12582912 | tf_op jit(solution)/shard_map/squeeze | solution.py:274
  195.0 1.5 collective-permute-start.5
  196.5 2.2 copy-done.9
  198.7 28.8 %product.15.refs_6_ = bf16[3,1536,2048]{2,1,0:T(8,128)(2,1)} custom-call(bf16[1536,3072]{1,0:T(8,128)(2,1)} %refs_0_.24, bf16[512,3072]{1,0:T(8,128)(2,1)S(1)} %copy-done.8, bf16[512,3072]{1,0:T(8,128)(2,1)} %collective-permute-done.2.refs_1_.refs_2_, bf16[3,1536,2048]{2,1,0:T(8,128)(2,1)} %refs_4_.7, ...), custom_call_target="tpu_custom_call", output_to_operand_aliasing={{}: (7, {})} | custom-call | flops 19327352832 | bytes 12582912 | tf_op jit(solution)/shard_map/product/pallas_call | solution.py:155
  227.5 11.2 %product.16.refs_4_ = f32[1536,1536]{1,0:T(8,128)} custom-call(bf16[1536,3072]{1,0:T(8,128)(2,1)} %refs_0_.24, bf16[512,3072]{1,0:T(8,128)(2,1)} %collective-permute-done.2.refs_1_.refs_2_, bf16[3,1536,2048]{2,1,0:T(8,128)(2,1)} %refs_4_.7, ...), custom_call_target="tpu_custom_call", output_to_operand_aliasing={{}: (4, {})} | custom-call | flops 4831838208 | bytes 6291456 | tf_op jit(solution)/shard_map/product/pallas_call | solution.py:155
  238.7 19.1 %collective-permute-done.3.refs_1_.refs_3_ = bf16[512,3072]{1,0:T(8,128)(2,1)} collective-permute-done((bf16[512,3072]{1,0:T(8,128)(2,1)}, bf16[512,3072]{1,0:T(8,128)(2,1)}, u32[]{:S(2)}, u32[]{:S(2)}) %collective-permute-start.3) | collective-permute-done | bytes 3145760 | tf_op jit(solution)/shard_map/ppermute | solution.py:265
  257.8 3.7 copy-done.1
  261.5 1.4 copy-done.13
  262.9 8.5 %product.17.refs_6_ = bf16[3,1536,2048]{2,1,0:T(8,128)(2,1)} custom-call(bf16[1536,3072]{1,0:T(8,128)(2,1)S(1)} %copy-done.1, bf16[512,3072]{1,0:T(8,128)(2,1)} %collective-permute-done.3.refs_1_.refs_3_, bf16[3,1536,2048]{2,1,0:T(8,128)(2,1)} %refs_4_.7, bf16[1536,512]{1,0:T(8,128)(2,1)S(1)} %collective-permute-done.7.refs_3_, ...), custom_call_target="tpu_custom_call", output_to_operand_aliasing={{}: (6, {})} | custom-call | flops 3221225472 | bytes 6291456 | tf_op jit(solution)/shard_map/product/pallas_call | solution.py:155
  271.4 17.8 %product.18.refs_8_ = bf16[3,1536,2048]{2,1,0:T(8,128)(2,1)} custom-call(bf16[1536,3072]{1,0:T(8,128)(2,1)} %refs_0_.24, bf16[512,3072]{1,0:T(8,128)(2,1)} %collective-permute-done.3.refs_1_.refs_3_, bf16[3,1536,2048]{2,1,0:T(8,128)(2,1)} %refs_4_.7, bf16[1536,1536]{1,0:T(8,128)(2,1)} %collective-permute-done.6.refs_4_.refs_3_, ...), custom_call_target="tpu_custom_call", output_to_operand_aliasing={{}: (6, {})} | custom-call | flops 9663676416 | bytes 6291456 | tf_op jit(solution)/shard_map/product/pallas_call | solution.py:155
  289.3 1.7 collective-permute-start.4
  291.0 4.1 collective-permute-done.10.refs_7_
  295.1 1.6 copy-done.18
  296.8 28.8 %product.19.refs_8_ = bf16[3,1536,2048]{2,1,0:T(8,128)(2,1)} custom-call(bf16[1536,3072]{1,0:T(8,128)(2,1)} %refs_0_.24, bf16[512,3072]{1,0:T(8,128)(2,1)S(1)} %copy-done.8, bf16[512,3072]{1,0:T(8,128)(2,1)} %collective-permute-done.2.refs_1_.refs_2_, bf16[512,3072]{1,0:T(8,128)(2,1)} %collective-permute-done.3.refs_1_.refs_3_, ...), custom_call_target="tpu_custom_call", output_to_operand_aliasing={{}: (8, {})} | custom-call | flops 19327352832 | bytes 18874368 | tf_op jit(solution)/shard_map/product/pallas_call | solution.py:155
  325.6 34.2 %collective-permute-done.4.refs_5_ = bf16[1536,1024]{1,0:T(8,128)(2,1)S(1)} collective-permute-done((bf16[1536,1024]{1,0:T(8,128)(2,1)S(1)}, bf16[1536,1024]{1,0:T(8,128)(2,1)S(1)}, u32[]{:S(2)}, u32[]{:S(2)}) %collective-permute-start.4) | collective-permute-done | bytes 3145760 | tf_op jit(solution)/shard_map/ppermute | solution.py:265
  359.8 5.7 %slice_bitcast_fusion.3 = (bf16[1536,512]{1,0:T(8,128)(2,1)}, bf16[1536,512]{1,0:T(8,128)(2,1)}, bf16[1536,512]{1,0:T(8,128)(2,1)}) fusion(bf16[3,1536,2048]{2,1,0:T(8,128)(2,1)} %refs_4_.7), kind=kLoop, calls=%fused_computation.3 | loop fusion | bytes 9437184 | tf_op jit(solution)/shard_map/squeeze | solution.py:274
  365.5 1.7 collective-permute-start.17
  367.3 1.7 copy-done.17
  369.0 28.8 %product.20.refs_4_ = bf16[3,1536,2048]{2,1,0:T(8,128)(2,1)} custom-call(bf16[1536,3072]{1,0:T(8,128)(2,1)} %refs_0_.24, bf16[512,3072]{1,0:T(8,128)(2,1)S(1)} %copy-done.8, bf16[512,3072]{1,0:T(8,128)(2,1)} %collective-permute-done.2.refs_1_.refs_2_, bf16[512,3072]{1,0:T(8,128)(2,1)} %collective-permute-done.3.refs_1_.refs_3_, ...), custom_call_target="tpu_custom_call", output_to_operand_aliasing={{}: (8, {})} | custom-call | flops 19327352832 | bytes 18874368 | tf_op jit(solution)/shard_map/product/pallas_call | solution.py:155
  397.8 11.3 %product.21.refs_3_ = f32[1536,1536]{1,0:T(8,128)} custom-call(bf16[1536,3072]{1,0:T(8,128)(2,1)} %refs_0_.24, bf16[512,3072]{1,0:T(8,128)(2,1)} %collective-permute-done.3.refs_1_.refs_3_, bf16[3,1536,2048]{2,1,0:T(8,128)(2,1)} %refs_4_.7, ...), custom_call_target="tpu_custom_call", output_to_operand_aliasing={{}: (4, {})} | custom-call | flops 4831838208 | bytes 6291456 | tf_op jit(solution)/shard_map/product/pallas_call | solution.py:155
  409.1 3.7 copy-done.2
  412.8 3.1 late_weights.1.refs_0_
  416.3 3.0 collective-permute-done.18.refs_2_
  419.3 1.0 copy-done.5
  420.3 6.2 %late.6.refs_4_ = bf16[3,1536,2048]{2,1,0:T(8,128)(2,1)} custom-call(bf16[2,1536,1536]{2,1,0:T(8,128)(2,1)S(1)} %late_weights.1.refs_0_, bf16[1536,512]{1,0:T(8,128)(2,1)S(1)} %collective-permute-done.17.refs_1_, bf16[1536,512]{1,0:T(8,128)(2,1)S(1)} %collective-permute-done.18.refs_2_, f32[1536,1536]{1,0:T(8,128)S(1)} %copy-done.5, ...), custom_call_target="tpu_custom_call", output_to_operand_aliasing={{}: (4, {})} | custom-call | flops 4831838208 | bytes 3145728 | tf_op jit(solution)/shard_map/late/pallas_call | solution.py:249
  426.5 26.2 %collective-permute-done.16.refs_1_ = bf16[1536,512]{1,0:T(8,128)(2,1)S(1)} collective-permute-done((bf16[1536,512]{1,0:T(8,128)(2,1)S(1)}, bf16[1536,512]{1,0:T(8,128)(2,1)S(1)}, u32[]{:S(2)}, u32[]{:S(2)}) %collective-permute-start.16) | collective-permute-done | bytes 1572896 | tf_op jit(solution)/shard_map/ppermute | solution.py:265
  453.0 1.7 collective-permute-start.15
  454.7 43.4 %collective-permute-done.15.refs_1_ = bf16[768,256]{1,0:T(8,128)(2,1)S(1)} collective-permute-done((bf16[768,256]{1,0:T(8,128)(2,1)S(1)}, bf16[768,256]{1,0:T(8,128)(2,1)S(1)}, u32[]{:S(2)}, u32[]{:S(2)}) %collective-permute-start.15) | collective-permute-done | bytes 393248 | tf_op jit(solution)/shard_map/ppermute | solution.py:265
  498.2 6.2 %late.7.refs_4_ = bf16[3,1536,2048]{2,1,0:T(8,128)(2,1)} custom-call(bf16[2,1536,1536]{2,1,0:T(8,128)(2,1)S(1)} %late_weights.1.refs_0_, bf16[1536,512]{1,0:T(8,128)(2,1)S(1)} %collective-permute-done.16.refs_1_, bf16[1536,512]{1,0:T(8,128)(2,1)S(1)} %collective-permute-done.19.refs_2_, f32[1536,1536]{1,0:T(8,128)S(1)} %copy-done.5, ...), custom_call_target="tpu_custom_call", output_to_operand_aliasing={{}: (4, {})} | custom-call | flops 4831838208 | bytes 3145728 | tf_op jit(solution)/shard_map/late/pallas_call | solution.py:249
  504.4 8.3 %product.22.refs_3_ = f32[1536,256]{1,0:T(8,128)} custom-call(bf16[1536,3072]{1,0:T(8,128)(2,1)} %refs_0_.24, bf16[512,3072]{1,0:T(8,128)(2,1)} %copy-done.7, bf16[512,3072]{1,0:T(8,128)(2,1)} %collective-permute-done.2.refs_1_.refs_2_, bf16[512,3072]{1,0:T(8,128)(2,1)} %collective-permute-done.3.refs_1_.refs_3_, bf16[3,1536,2048]{2,1,0:T(8,128)(2,1)} %refs_4_.7, ...), custom_call_target="tpu_custom_call" | custom-call | flops 2415919104 | bytes 18874368 | tf_op jit(solution)/shard_map/product/pallas_call | solution.py:155
  512.6 8.5 %product.23.refs_3_ = f32[1536,256]{1,0:T(8,128)} custom-call(bf16[1536,3072]{1,0:T(8,128)(2,1)} %refs_0_.24, bf16[512,3072]{1,0:T(8,128)(2,1)} %copy-done.7, bf16[512,3072]{1,0:T(8,128)(2,1)} %collective-permute-done.2.refs_1_.refs_2_, bf16[512,3072]{1,0:T(8,128)(2,1)} %collective-permute-done.3.refs_1_.refs_3_, bf16[3,1536,2048]{2,1,0:T(8,128)(2,1)} %refs_4_.7, ...), custom_call_target="tpu_custom_call" | custom-call | flops 2415919104 | bytes 18874368 | tf_op jit(solution)/shard_map/product/pallas_call | solution.py:155
  521.2 3.7 copy-done.4
  524.9 1.4 copy-done.15
  526.3 1.7 late.8.refs_3_
  528.0 0.4 collective-permute-start.21
  528.4 1.3 slice_bitcast_fusion.7
  530.0 1.4 collective-permute-done.21.refs_2_
  531.4 3.7 copy-done.6
  535.1 6.2 %late.9.refs_4_ = bf16[3,1536,2048]{2,1,0:T(8,128)(2,1)} custom-call(bf16[2,1536,1536]{2,1,0:T(8,128)(2,1)S(1)} %copy-done.4, bf16[1536,512]{1,0:T(8,128)(2,1)S(1)} %collective-permute-done.14.refs_1_, bf16[1536,512]{1,0:T(8,128)(2,1)S(1)} %collective-permute-done.21.refs_2_, f32[1536,1536]{1,0:T(8,128)S(1)} %copy-done.6, ...), custom_call_target="tpu_custom_call", output_to_operand_aliasing={{}: (4, {})} | custom-call | flops 4831838208 | bytes 3145728 | tf_op jit(solution)/shard_map/late/pallas_call | solution.py:249
  541.3 8.0 %collective-permute-done.13.refs_1_ = bf16[1536,256]{1,0:T(8,128)(2,1)S(1)} collective-permute-done((bf16[1536,256]{1,0:T(8,128)(2,1)S(1)}, bf16[1536,256]{1,0:T(8,128)(2,1)S(1)}, u32[]{:S(2)}, u32[]{:S(2)}) %collective-permute-start.13) | collective-permute-done | bytes 786464 | tf_op jit(solution)/shard_map/ppermute | solution.py:265
  549.3 1.0 slice_bitcast_fusion.8
  550.7 0.9 collective-permute-done.22.refs_2_
  551.6 3.7 late.10.refs_4_
  555.3 6.6 %collective-permute-done.12.refs_1_ = bf16[768,256]{1,0:T(8,128)(2,1)S(1)} collective-permute-done((bf16[768,256]{1,0:T(8,128)(2,1)S(1)}, bf16[768,256]{1,0:T(8,128)(2,1)S(1)}, u32[]{:S(2)}, u32[]{:S(2)}) %collective-permute-start.12) | collective-permute-done | bytes 393248 | tf_op jit(solution)/shard_map/ppermute | solution.py:265
  561.9 1.7 collective-permute-done.23.refs_2_
  563.6 2.5 late.11
  (63 shorter events, 1.6 us)
Async XLA Ops:
  1.8 14.2 %slice-start = ((s8[9437184]{0:T(1024)(128)(4,1)}), s8[4194304]{0:T(1024)(128)(4,1)S(1)}, s32[]{:S(2)}) async-start(s8[9437184]{0:T(1024)(128)(4,1)} %bitcast.20), calls=%async_computation | async-start | bytes 8388608
  3.5 12.5 %slice-start.1 = ((s8[9437184]{0:T(1024)(128)(4,1)}), s8[4194304]{0:T(1024)(128)(4,1)S(1)}, s32[]{:S(2)}) async-start(s8[9437184]{0:T(1024)(128)(4,1)} %bitcast.20), calls=%async_computation.1 | async-start | bytes 8388608
  5.7 10.3 %slice-start.2 = ((s8[9437184]{0:T(1024)(128)(4,1)}), s8[1048576]{0:T(1024)(128)(4,1)S(1)}, s32[]{:S(2)}) async-start(s8[9437184]{0:T(1024)(128)(4,1)} %bitcast.20), calls=%async_computation.2 | async-start | bytes 2097152
  5.7 148.0 %collective-permute-start = (bf16[3,1536,2048]{2,1,0:T(8,128)(2,1)}, bf16[3,1536,2048]{2,1,0:T(8,128)(2,1)}, u32[]{:S(2)}, u32[]{:S(2)}) collective-permute-start(bf16[3,1536,2048]{2,1,0:T(8,128)(2,1)} %refs_4_.7), channel_id=1, source_target_pairs={{0,1},{1,0},{2,3},{3,2},{4,5},{5,4},{6,7},{7,6}} | collective-permute-start | bytes 56623112 | tf_op jit(solution)/shard_map/ppermute | solution.py:265
  11.4 175.5 %collective-permute-start.6 = (bf16[1536,1536]{1,0:T(8,128)(2,1)}, bf16[1536,1536]{1,0:T(8,128)(2,1)}, u32[]{:S(2)}, u32[]{:S(2)}) collective-permute-start(bf16[1536,1536]{1,0:T(8,128)(2,1)} %slice_bitcast_fusion), channel_id=1, source_target_pairs={{0,4},{4,0},{1,5},{5,1},{2,6},{6,2},{3,7},{7,3}} | collective-permute-start | bytes 14155784 | tf_op jit(solution)/shard_map/ppermute | solution.py:265
  14.0 136.3 %collective-permute-start.1 = (bf16[512,3072]{1,0:T(8,128)(2,1)S(1)}, bf16[512,3072]{1,0:T(8,128)(2,1)S(1)}, u32[]{:S(2)}, u32[]{:S(2)}) collective-permute-start(bf16[512,3072]{1,0:T(8,128)(2,1)S(1)} %slice.41), channel_id=1, source_target_pairs={{0,2},{2,0},{1,3},{3,1},{4,6},{6,4},{5,7},{7,5}} | collective-permute-start | bytes 9437192 | tf_op jit(solution)/shard_map/ppermute | solution.py:265
  15.5 134.8 %collective-permute-start.7 = (bf16[1536,512]{1,0:T(8,128)(2,1)S(1)}, bf16[1536,512]{1,0:T(8,128)(2,1)S(1)}, u32[]{:S(2)}, u32[]{:S(2)}) collective-permute-start(bf16[1536,512]{1,0:T(8,128)(2,1)S(1)} %slice_bitcast_fusion.6), channel_id=1, source_target_pairs={{0,4},{4,0},{1,5},{5,1},{2,6},{6,2},{3,7},{7,3}} | collective-permute-start | bytes 4718600 | tf_op jit(solution)/shard_map/ppermute | solution.py:265
  19.3 154.3 %collective-permute-start.2 = (bf16[512,3072]{1,0:T(8,128)(2,1)}, bf16[512,3072]{1,0:T(8,128)(2,1)}, u32[]{:S(2)}, u32[]{:S(2)}) collective-permute-start(bf16[512,3072]{1,0:T(8,128)(2,1)} %get-tuple-element.115), channel_id=1, source_target_pairs={{0,2},{2,0},{1,3},{3,1},{4,6},{6,4},{5,7},{7,5}} | collective-permute-start | bytes 9437192 | tf_op jit(solution)/shard_map/ppermute | solution.py:265
  150.3 3.4 collective-permute-start.8
  150.3 10.9 %copy-start.7 = (bf16[512,3072]{1,0:T(8,128)(2,1)}, bf16[512,3072]{1,0:T(8,128)(2,1)S(1)}, u32[]{:S(2)}) copy-start(bf16[512,3072]{1,0:T(8,128)(2,1)S(1)} %collective-permute-done.1.refs_1_) | copy-start | bytes 9437188
  161.2 1.1 copy-start.11
  173.6 3.7 copy-start
  177.3 1.4 copy-start.12
  186.9 9.6 %collective-permute-start.9 = (bf16[1536,1536]{1,0:T(8,128)(2,1)}, bf16[1536,1536]{1,0:T(8,128)(2,1)S(1)}, u32[]{:S(2)}, u32[]{:S(2)}) collective-permute-start(bf16[1536,1536]{1,0:T(8,128)(2,1)} %collective-permute-done.6.refs_4_.refs_3_), channel_id=1, source_target_pairs={{0,1},{1,0},{2,3},{3,2},{4,5},{5,4},{6,7},{7,6}} | collective-permute-start | bytes 14155784 | tf_op jit(solution)/shard_map/ppermute | solution.py:265
  187.0 11.7 %copy-start.8 = (bf16[512,3072]{1,0:T(8,128)(2,1)S(1)}, bf16[512,3072]{1,0:T(8,128)(2,1)}, u32[]{:S(2)}) copy-start(bf16[512,3072]{1,0:T(8,128)(2,1)} %copy-done.7) | copy-start | bytes 9437188
  187.0 70.8 %collective-permute-start.3 = (bf16[512,3072]{1,0:T(8,128)(2,1)}, bf16[512,3072]{1,0:T(8,128)(2,1)}, u32[]{:S(2)}, u32[]{:S(2)}) collective-permute-start(bf16[512,3072]{1,0:T(8,128)(2,1)} %get-tuple-element.114), channel_id=1, source_target_pairs={{0,2},{2,0},{1,3},{3,1},{4,6},{6,4},{5,7},{7,5}} | collective-permute-start | bytes 9437192 | tf_op jit(solution)/shard_map/ppermute | solution.py:265
  195.0 94.3 %collective-permute-start.5 = (bf16[1536,1024]{1,0:T(8,128)(2,1)}, bf16[1536,1024]{1,0:T(8,128)(2,1)}, u32[]{:S(2)}, u32[]{:S(2)}) collective-permute-start(bf16[1536,1024]{1,0:T(8,128)(2,1)} %get-tuple-element.112), channel_id=1, source_target_pairs={{0,4},{4,0},{1,5},{5,1},{2,6},{6,2},{3,7},{7,3}} | collective-permute-start | bytes 9437192 | tf_op jit(solution)/shard_map/ppermute | solution.py:265
  196.5 2.2 copy-start.9
  257.8 3.7 copy-start.1
  261.5 1.4 copy-start.13
  262.9 8.5 %copy-start.10 = (bf16[1536,1536]{1,0:T(8,128)(2,1)S(1)}, bf16[1536,1536]{1,0:T(8,128)(2,1)}, u32[]{:S(2)}) copy-start(bf16[1536,1536]{1,0:T(8,128)(2,1)} %copy-done.9) | copy-start | bytes 14155780
  271.4 17.9 %copy-start.19 = (bf16[1536,1024]{1,0:T(8,128)(2,1)S(1)}, bf16[1536,1024]{1,0:T(8,128)(2,1)}, u32[]{:S(2)}) copy-start(bf16[1536,1024]{1,0:T(8,128)(2,1)} %get-tuple-element.113) | copy-start | bytes 9437188
  289.2 5.9 %collective-permute-start.10 = (bf16[1536,1024]{1,0:T(8,128)(2,1)}, bf16[1536,1024]{1,0:T(8,128)(2,1)S(1)}, u32[]{:S(2)}, u32[]{:S(2)}) collective-permute-start(bf16[1536,1024]{1,0:T(8,128)(2,1)} %collective-permute-done.5.refs_5_), channel_id=1, source_target_pairs={{0,1},{1,0},{2,3},{3,2},{4,5},{5,4},{6,7},{7,6}} | collective-permute-start | bytes 9437192 | tf_op jit(solution)/shard_map/ppermute | solution.py:265
  289.3 70.5 %collective-permute-start.4 = (bf16[1536,1024]{1,0:T(8,128)(2,1)S(1)}, bf16[1536,1024]{1,0:T(8,128)(2,1)S(1)}, u32[]{:S(2)}, u32[]{:S(2)}) collective-permute-start(bf16[1536,1024]{1,0:T(8,128)(2,1)S(1)} %copy-done.19), channel_id=1, source_target_pairs={{0,4},{4,0},{1,5},{5,1},{2,6},{6,2},{3,7},{7,3}} | collective-permute-start | bytes 9437192 | tf_op jit(solution)/shard_map/ppermute | solution.py:265
  295.1 1.6 copy-start.18
  359.8 5.7 %copy-start.16 = (bf16[1536,1024]{1,0:T(8,128)(2,1)}, bf16[1536,1024]{1,0:T(8,128)(2,1)S(1)}, u32[]{:S(2)}) copy-start(bf16[1536,1024]{1,0:T(8,128)(2,1)S(1)} %collective-permute-done.4.refs_5_) | copy-start | bytes 9437188
  359.8 7.5 %collective-permute-start.11 = (bf16[1536,1024]{1,0:T(8,128)(2,1)S(1)}, bf16[1536,1024]{1,0:T(8,128)(2,1)S(1)}, u32[]{:S(2)}, u32[]{:S(2)}) collective-permute-start(bf16[1536,1024]{1,0:T(8,128)(2,1)S(1)} %collective-permute-done.4.refs_5_), channel_id=1, source_target_pairs={{0,1},{1,0},{2,3},{3,2},{4,5},{5,4},{6,7},{7,6}} | collective-permute-start | bytes 9437192 | tf_op jit(solution)/shard_map/ppermute | solution.py:265
  365.5 50.3 %collective-permute-start.17 = (bf16[1536,512]{1,0:T(8,128)(2,1)}, bf16[1536,512]{1,0:T(8,128)(2,1)S(1)}, u32[]{:S(2)}, u32[]{:S(2)}) collective-permute-start(bf16[1536,512]{1,0:T(8,128)(2,1)} %get-tuple-element.109), channel_id=1, source_target_pairs={{0,4},{4,0},{1,5},{5,1},{2,6},{6,2},{3,7},{7,3}} | collective-permute-start | bytes 4718600 | tf_op jit(solution)/shard_map/ppermute | solution.py:265
  367.3 1.7 copy-start.17
  409.1 3.7 copy-start.2
  412.7 3.2 copy-start.20
  412.7 7.6 %copy-start.5 = (f32[1536,1536]{1,0:T(8,128)S(1)}, f32[1536,1536]{1,0:T(8,128)}, u32[]{:S(2)}) copy-start(f32[1536,1536]{1,0:T(8,128)} %product.21.refs_3_) | copy-start | bytes 28311556
  415.9 82.3 %copy-start.3 = (bf16[2,1536,1536]{2,1,0:T(8,128)(2,1)}, bf16[2,1536,1536]{2,1,0:T(8,128)(2,1)S(1)}, u32[]{:S(2)}) copy-start(bf16[2,1536,1536]{2,1,0:T(8,128)(2,1)S(1)} %late_weights.1.refs_0_) | copy-start | bytes 28311556
  415.9 3.4 collective-permute-start.18
  415.9 37.1 %copy-start.21 = (bf16[768,256]{1,0:T(8,128)(2,1)S(1)}, bf16[768,256]{1,0:T(8,128)(2,1)}, u32[]{:S(2)}) copy-start(bf16[768,256]{1,0:T(8,128)(2,1)} %slice_bitcast_fusion.9) | copy-start | bytes 1179652
  415.9 36.8 %collective-permute-start.16 = (bf16[1536,512]{1,0:T(8,128)(2,1)S(1)}, bf16[1536,512]{1,0:T(8,128)(2,1)S(1)}, u32[]{:S(2)}, u32[]{:S(2)}) collective-permute-start(bf16[1536,512]{1,0:T(8,128)(2,1)S(1)} %copy-done.20), channel_id=1, source_target_pairs={{0,4},{4,0},{1,5},{5,1},{2,6},{6,2},{3,7},{7,3}} | collective-permute-start | bytes 4718600 | tf_op jit(solution)/shard_map/ppermute | solution.py:265
  452.7 45.5 %collective-permute-start.19 = (bf16[1536,512]{1,0:T(8,128)(2,1)S(1)}, bf16[1536,512]{1,0:T(8,128)(2,1)S(1)}, u32[]{:S(2)}, u32[]{:S(2)}) collective-permute-start(bf16[1536,512]{1,0:T(8,128)(2,1)S(1)} %collective-permute-done.16.refs_1_), channel_id=1, source_target_pairs={{0,1},{1,0},{2,3},{3,2},{4,5},{5,4},{6,7},{7,6}} | collective-permute-start | bytes 4718600 | tf_op jit(solution)/shard_map/ppermute | solution.py:265
  452.7 75.3 %collective-permute-start.14 = (bf16[1536,512]{1,0:T(8,128)(2,1)}, bf16[1536,512]{1,0:T(8,128)(2,1)S(1)}, u32[]{:S(2)}, u32[]{:S(2)}) collective-permute-start(bf16[1536,512]{1,0:T(8,128)(2,1)} %get-tuple-element.111), channel_id=1, source_target_pairs={{0,4},{4,0},{1,5},{5,1},{2,6},{6,2},{3,7},{7,3}} | collective-permute-start | bytes 4718600 | tf_op jit(solution)/shard_map/ppermute | solution.py:265
  453.0 45.1 %collective-permute-start.15 = (bf16[768,256]{1,0:T(8,128)(2,1)S(1)}, bf16[768,256]{1,0:T(8,128)(2,1)S(1)}, u32[]{:S(2)}, u32[]{:S(2)}) collective-permute-start(bf16[768,256]{1,0:T(8,128)(2,1)S(1)} %copy-done.21), channel_id=1, source_target_pairs={{0,4},{4,0},{1,5},{5,1},{2,6},{6,2},{3,7},{7,3}} | collective-permute-start | bytes 1179656 | tf_op jit(solution)/shard_map/ppermute | solution.py:265
  498.2 23.0 %collective-permute-start.20 = (bf16[768,256]{1,0:T(8,128)(2,1)S(1)}, bf16[768,256]{1,0:T(8,128)(2,1)S(1)}, u32[]{:S(2)}, u32[]{:S(2)}) collective-permute-start(bf16[768,256]{1,0:T(8,128)(2,1)S(1)} %collective-permute-done.15.refs_1_), channel_id=1, source_target_pairs={{0,1},{1,0},{2,3},{3,2},{4,5},{5,4},{6,7},{7,6}} | collective-permute-start | bytes 1179656 | tf_op jit(solution)/shard_map/ppermute | solution.py:265
  521.2 3.7 copy-start.4
  524.9 1.4 copy-start.15
  528.0 3.4 collective-permute-start.21
  528.4 23.2 %copy-start.14 = (f32[1536,256]{1,0:T(8,128)S(1)}, f32[1536,256]{1,0:T(8,128)}, u32[]{:S(2)}) copy-start(f32[1536,256]{1,0:T(8,128)} %product.22.refs_3_) | copy-start | bytes 4718596
  529.7 19.6 %collective-permute-start.13 = (bf16[1536,256]{1,0:T(8,128)(2,1)S(1)}, bf16[1536,256]{1,0:T(8,128)(2,1)S(1)}, u32[]{:S(2)}, u32[]{:S(2)}) collective-permute-start(bf16[1536,256]{1,0:T(8,128)(2,1)S(1)} %slice_bitcast_fusion.7), channel_id=1, source_target_pairs={{0,4},{4,0},{1,5},{5,1},{2,6},{6,2},{3,7},{7,3}} | collective-permute-start | bytes 2359304 | tf_op jit(solution)/shard_map/ppermute | solution.py:265
  531.4 3.7 copy-start.6
  549.3 2.3 collective-permute-start.22
  550.3 11.5 %collective-permute-start.12 = (bf16[768,256]{1,0:T(8,128)(2,1)S(1)}, bf16[768,256]{1,0:T(8,128)(2,1)S(1)}, u32[]{:S(2)}, u32[]{:S(2)}) collective-permute-start(bf16[768,256]{1,0:T(8,128)(2,1)S(1)} %slice_bitcast_fusion.8), channel_id=1, source_target_pairs={{0,4},{4,0},{1,5},{5,1},{2,6},{6,2},{3,7},{7,3}} | collective-permute-start | bytes 1179656 | tf_op jit(solution)/shard_map/ppermute | solution.py:265
  561.9 1.7 collective-permute-start.23

commit v3 on v2

v3 whole, which is shorter than its diff:
```python
import functools

import jax
import jax.numpy as jnp
from jax import lax
from jax.experimental import pallas as pl
from jax.experimental.pallas import tpu as pltpu
from jax.sharding import PartitionSpec as P


SWAP = [(0, 1), (1, 0)]
CHUNKS = {
    "a": (0, 0, 512, 0, 1536),
    "b": (0, 512, 1536, 0, 1536),
    "c": (1, 0, 1024, 0, 1536),
    "d": (1, 1024, 1024, 0, 1536),
    "e": (2, 0, 512, 0, 1536),
    "f": (2, 512, 512, 0, 1536),
    "g": (2, 1024, 256, 0, 1536),
    "h": (2, 1280, 256, 0, 1536),
    "i0": (2, 1536, 256, 0, 768),
    "i1": (2, 1536, 256, 768, 768),
    "j0": (2, 1792, 256, 0, 384),
    "j1": (2, 1792, 256, 384, 640),
    "j2": (2, 1792, 256, 1024, 512),
}
SEND_ORDER = ("j0", "a", "b", "c", "d", "i0", "j1", "e", "f", "g", "h", "i1", "j2")
LATE_COLS = (2, 0, 2048)
TILE_ROWS = 512
TILE_COLS = 512
LOCAL_VMEM = 58 << 20
SMALL_ROWS = 1536


def product_kernel(plan, *refs):
    tiles, flips, windows, k_start, k_rows, has_base, has_prev, width, tile_cols = plan
    n_tiles, n_pieces = len(tiles), len(flips)
    a_own, a_far = refs[0], refs[1 : 1 + n_tiles]
    pieces = refs[1 + n_tiles : 1 + n_tiles + n_pieces]
    rest = refs[1 + n_tiles + n_pieces :]
    base_ref = rest[0] if has_base else None
    outs = rest[has_base + has_prev : -4]
    a_all, x_all, a_sems, x_sems = rest[-4:]
    slice_rows = a_own.shape[1] // 2
    layer_idx = lax.axis_index("depth")
    cross = lax.rem(lax.axis_index("col") + lax.axis_index("row"), 2)
    m, n = pl.program_id(0), pl.program_id(1)
    layers = sorted({flip_layer for _, flip_layer in flips})
    n_layers = len(layers)
    col_tiles = width // tile_cols

    def a_copy(side, tile):
        if side == 0:
            source = a_own.at[pl.ds(tiles[tile] * TILE_ROWS, TILE_ROWS)]
        else:
            source = a_far[tile]
        if n_layers == 1:
            start = lax.rem(layer_idx + layers[0], 2) * slice_rows + k_start
            source = source.at[:, pl.ds(pl.multiple_of(start, 128), k_rows)]
        return pltpu.make_async_copy(source, a_all.at[side, pl.ds(tile * TILE_ROWS, TILE_ROWS)], a_sems.at[side, tile])

    def x_copy(idx, tile):
        flip_row, flip_layer = flips[idx]
        slot = lax.rem(cross + flip_row, 2) * n_layers
        if n_layers == 2:
            slot = slot + lax.rem(layer_idx + flip_layer, 2)
        source = pieces[idx]
        start = tile * tile_cols
        if windows[idx] is not None:
            rhs_idx, offset = windows[idx]
            source = source.at[rhs_idx]
            start = start + offset
        return pltpu.make_async_copy(
            source.at[:, pl.ds(start, tile_cols)],
            x_all.at[slot, :, pl.ds(tile * tile_cols, tile_cols)],
            x_sems.at[slot, tile],
        )

    def x_wait(side, tile):
        for layer in range(n_layers):
            slot = side * n_layers + layer
            block = x_all.at[slot, :, pl.ds(tile * tile_cols, tile_cols)]
            pltpu.make_async_copy(block, block, x_sems.at[slot, tile]).wait()

    def x_start(side, tile):
        for idx, (flip_row, _) in enumerate(flips):
            @pl.when(lax.rem(cross + flip_row, 2) == side)
            def _():
                x_copy(idx, tile).start()

    groups = [(0, col, side) for col in range(col_tiles) for side in range(2)]
    groups += [(tile, 0, side) for tile in range(1, n_tiles) for side in range(2)]

    def group_start(index):
        if index < len(groups):
            tile, col, side = groups[index]
            if col == 0:
                a_copy(side, tile).start()
            if tile == 0:
                x_start(side, col)

    def group_wait(index):
        tile, col, side = groups[index]
        if col == 0:
            a_copy(side, tile).wait()
        if tile == 0:
            x_wait(side, col)

    row_range = pl.ds(pl.multiple_of(m * TILE_ROWS, TILE_ROWS), TILE_ROWS)
    col_range = pl.ds(pl.multiple_of(n * tile_cols, tile_cols), tile_cols)
    total = base_ref[...] if has_base else None
    for side in range(2):
        for index, (tile, col, group_side) in enumerate(groups):
            if group_side == side:
                @pl.when((m == tile) & (n == col))
                def _():
                    if index == 0:
                        group_start(0)
                    group_wait(index)
                    if index == 0:
                        group_start(1)
                    group_start(index + 2)

        x_side = x_all[pl.ds(side * n_layers, n_layers), :, col_range].reshape(n_layers * k_rows, tile_cols)
        term = jnp.dot(a_all[side, row_range], x_side, preferred_element_type=jnp.float32)
        total = term if total is None else total + term
    if len(outs[0].shape) == 3:
        outs[0][0] = total.astype(outs[0].dtype)
    else:
        for col, out_ref in enumerate(outs):
            @pl.when(n == col)
            def _():
                out_ref[...] = total


def product(a_own, a_far, pieces, flips, windows, k_range, width, tiles=(0, 1, 2), vmem=None, base=None, base_start=0, prev=None, out=None):
    rows, half = a_own.shape
    k_start, k_rows = k_range
    any_spec = pl.BlockSpec(memory_space=pl.ANY)
    tile_cols = min(TILE_COLS, width)
    n_layers = len({flip_layer for _, flip_layer in flips})
    operands = [a_own, *(a_far[tile] for tile in tiles), *pieces]
    hbm_spec = pl.BlockSpec(memory_space=pltpu.HBM)
    in_specs = [hbm_spec] * (1 + len(tiles)) + [any_spec if window is None else hbm_spec for window in windows]
    first = tiles[0]
    if base is not None:
        operands.append(base)
        in_specs.append(pl.BlockSpec((TILE_ROWS, tile_cols), lambda m, n: (first + m, base_start // tile_cols + n)))
    prevs = list(prev) if isinstance(prev, (list, tuple)) else [] if prev is None else [prev]
    aliases = {len(operands) + idx: idx for idx in range(len(prevs))}
    operands += prevs
    in_specs += [any_spec] * len(prevs)
    if out is None:
        out_shape = [jax.ShapeDtypeStruct((rows, tile_cols), jnp.float32)] * (width // tile_cols)
        out_spec = [pl.BlockSpec((TILE_ROWS, tile_cols), lambda m, n: (first + m, 0))] * len(out_shape)
    else:
        y_shape, rhs_idx, start = out
        out_shape = jax.ShapeDtypeStruct(y_shape, jnp.bfloat16)
        out_spec = pl.BlockSpec((1, TILE_ROWS, tile_cols), lambda m, n: (rhs_idx, first + m, start // tile_cols + n))
    plan = (tuple(tiles), tuple(flips), tuple(windows), k_start, k_rows, base is not None, len(prevs), width, tile_cols)
    tile_rows = len(tiles) * TILE_ROWS
    vmem = vmem or 4 * n_layers * k_rows * (tile_rows + width) + 16 * TILE_ROWS * tile_cols + (8 << 20)
    return pl.pallas_call(
        functools.partial(product_kernel, plan),
        grid=(len(tiles), width // tile_cols),
        out_shape=out_shape,
        in_specs=in_specs,
        out_specs=out_spec,
        scratch_shapes=[
            pltpu.VMEM((2, tile_rows, n_layers * k_rows), jnp.bfloat16),
            pltpu.VMEM((2 * n_layers, k_rows, width), jnp.bfloat16),
            pltpu.SemaphoreType.DMA((2, len(tiles))),
            pltpu.SemaphoreType.DMA((2 * n_layers, width // tile_cols)),
        ],
        input_output_aliases=aliases,
        cost_estimate=pl.CostEstimate(flops=4 * tile_rows * n_layers * k_rows * width, bytes_accessed=4 * tile_rows * half, transcendentals=0),
        compiler_params=pltpu.CompilerParams(dimension_semantics=("arbitrary", "arbitrary"), vmem_limit_bytes=vmem),
        name="product",
    )(*operands)


def weight_kernel(layer_flip, *refs):
    a_own, a_far, out_ref, sems = refs[0], refs[1:-2], refs[-2], refs[-1]
    slice_rows = out_ref.shape[2]
    start = pl.multiple_of(lax.rem(lax.axis_index("depth") + layer_flip, 2) * slice_rows, slice_rows)
    copies = [pltpu.make_async_copy(a_own.at[:, pl.ds(start, slice_rows)], out_ref.at[0], sems.at[0])]
    for tile, ref in enumerate(a_far):
        block = out_ref.at[1, pl.ds(tile * TILE_ROWS, TILE_ROWS)]
        copies.append(pltpu.make_async_copy(ref.at[:, pl.ds(start, slice_rows)], block, sems.at[tile + 1]))
    for copy in copies:
        copy.start()
    for copy in copies:
        copy.wait()


def late_weights(a_own, a_far):
    rows, half = a_own.shape
    any_spec = pl.BlockSpec(memory_space=pl.ANY)
    return pl.pallas_call(
        functools.partial(weight_kernel, 1),
        out_shape=jax.ShapeDtypeStruct((2, rows, half // 2), jnp.bfloat16),
        in_specs=[pl.BlockSpec(memory_space=pltpu.HBM)] * (1 + len(a_far)),
        out_specs=pl.BlockSpec(memory_space=pltpu.VMEM),
        scratch_shapes=[pltpu.SemaphoreType.DMA((1 + len(a_far),))],
        cost_estimate=pl.CostEstimate(flops=2 * rows * half * 256, bytes_accessed=4 * rows * half, transcendentals=0),
        compiler_params=pltpu.CompilerParams(vmem_limit_bytes=16 << 20),
        name="late_weights",
    )(a_own, *a_far)


def late_kernel(k_start, base_start, target, flips, tile_rows, *refs):
    n_pieces = len(flips)
    weights, pieces, base = refs[0], refs[1 : 1 + n_pieces], refs[1 + n_pieces]
    rest = refs[2 + n_pieces :]
    k_rows, width = pieces[0].shape
    cross = lax.rem(lax.axis_index("col") + lax.axis_index("row"), 2)
    k_range = pl.ds(k_start, k_rows)
    tiles = weights.shape[1] // tile_rows

    def rows_of(tile):
        return pl.ds(pl.multiple_of(tile * tile_rows, tile_rows), tile_rows)

    def out_copy(tile):
        y_ref, stage, sems = rest[1:]
        rhs_idx, start = target
        return pltpu.make_async_copy(stage.at[rows_of(tile)], y_ref.at[rhs_idx, rows_of(tile), pl.ds(start, width)], sems.at[tile])

    def row_tile(tile, carry):
        row_range = rows_of(tile)
        total = base[row_range, pl.ds(base_start, width)]
        for flip, piece in zip(flips, pieces):
            side = lax.rem(cross + flip, 2)
            total = total + jnp.dot(weights[side, row_range, k_range], piece[...], preferred_element_type=jnp.float32)
        if target is None:
            rest[0][row_range] = total
        else:
            stage = rest[2]
            stage[row_range] = total.astype(stage.dtype)
            out_copy(tile).start()
        return carry

    lax.fori_loop(0, tiles, row_tile, 0)
    if target is not None:
        for tile in range(tiles):
            out_copy(tile).wait()


def late_product(weights, pieces, flips, base, base_start, k_start, prev=None, target=None, tile_rows=TILE_ROWS):
    vmem_spec = pl.BlockSpec(memory_space=pltpu.VMEM)
    any_spec = pl.BlockSpec(memory_space=pl.ANY)
    rows, width = weights.shape[1], pieces[0].shape[1]
    operands = [weights, *pieces, base]
    in_specs = [vmem_spec] * len(operands)
    scratch = []
    aliases = {}
    if target is None:
        out_shape, out_spec = jax.ShapeDtypeStruct((rows, width), jnp.float32), vmem_spec
    else:
        out_shape, out_spec = jax.ShapeDtypeStruct(prev.shape, prev.dtype), any_spec
        aliases = {len(operands): 0}
        operands.append(prev)
        in_specs.append(any_spec)
        scratch = [pltpu.VMEM((rows, width), jnp.bfloat16), pltpu.SemaphoreType.DMA((rows // tile_rows,))]
    return pl.pallas_call(
        functools.partial(late_kernel, k_start, base_start, target, flips, tile_rows),
        out_shape=out_shape,
        in_specs=in_specs,
        out_specs=out_spec,
        scratch_shapes=scratch,
        input_output_aliases=aliases,
        name="late",
        compiler_params=pltpu.CompilerParams(vmem_limit_bytes=28 << 20),
        cost_estimate=pl.CostEstimate(flops=2 * rows * len(pieces) * pieces[0].size, bytes_accessed=4 * pieces[0].size, transcendentals=0),
    )(*operands)


OWN, DEEP, PEER, BOTH = (0, 0), (0, 1), (1, 0), (1, 1)


def solution(mesh):
    def permute(value, axis):
        return lax.ppermute(value, axis, SWAP)

    def body(w_local, x_local):
        y_shape = x_local.shape
        slice_rows = y_shape[1]
        n_row_tiles = w_local.shape[0] // TILE_ROWS

        def piece_of(x, chunk):
            rhs_idx, start, width, k_start, k_rows = chunk
            return x[rhs_idx, k_start : k_start + k_rows, start : start + width]

        sends = {SEND_ORDER[0]: piece_of(x_local, CHUNKS[SEND_ORDER[0]])}
        sends[SEND_ORDER[0]], x_rest = lax.optimization_barrier((sends[SEND_ORDER[0]], x_local))
        second = piece_of(x_rest, CHUNKS[SEND_ORDER[1]])
        sends[SEND_ORDER[1]], x_rest, w_rest = lax.optimization_barrier((second, x_rest, w_local))
        w_first, x_rest, w_rest = lax.optimization_barrier((w_rest[:TILE_ROWS], x_rest, w_rest))
        for name in SEND_ORDER[2:]:
            sends[name] = piece_of(x_rest, CHUNKS[name])
        deep = {name: permute(sends[name], "depth") for name in SEND_ORDER}
        w_sends = [w_first] + [w_rest[tile * TILE_ROWS : (tile + 1) * TILE_ROWS] for tile in range(1, n_row_tiles)]
        w_far = [permute(piece, "col") for piece in w_sends]
        x_row = permute(x_rest, "row")

        def full(name, relay, y, tiles):
            rhs_idx, start, width, _, _ = CHUNKS[name]
            window = (rhs_idx, start)
            return product(w_local, w_far, (x_local, deep[name], x_row, relay), (OWN, DEEP, PEER, BOTH), (window, None, window, None), (0, slice_rows), width, tiles=tiles, prev=y, out=(y_shape, rhs_idx, start))

        def local(y, tiles, prev=None):
            rhs_idx, start, width = LATE_COLS
            gated, y = lax.optimization_barrier((x_row, y))
            window = (rhs_idx, start)
            base = product(w_local, w_far, (x_local, gated), (OWN, PEER), (window, window), (0, slice_rows), width, tiles=tiles, prev=prev, vmem=LOCAL_VMEM)
            return lax.optimization_barrier((y, base))

        def relay_after(y, name):
            piece, y = lax.optimization_barrier((deep[name], y))
            return piece, permute(piece, "row"), y

        relay_j0 = permute(deep["j0"], "row")
        relay_a = permute(deep["a"], "row")
        y = full("a", relay_a, None, (0,))
        y, base = local(y, (0,))
        y = full("a", relay_a, y, (1,))
        _, relay, y = relay_after(y, "b")
        y = full("b", relay, y, (0, 1))
        y, base = local(y, (1,), prev=base)
        y = full("a", relay_a, y, (2,))
        y = full("b", relay, y, (2,))
        for name in ("c", "d"):
            _, relay, y = relay_after(y, name)
            y = full(name, relay, y, (0, 1, 2))
        early_i0, relay_i0, y = relay_after(y, "i0")
        early_j1, relay_j1, y = relay_after(y, "j1")
        y, base = local(y, (2,), prev=base)
        w_gate, y = lax.optimization_barrier((w_local, y))
        weights = late_weights(w_gate, w_far)
        y, weights = lax.optimization_barrier((y, weights))

        def base_of(name):
            _, start, _, _, _ = CHUNKS[name]
            return base[start // TILE_COLS], start % TILE_COLS

        def late(name, y):
            piece, relay, y = relay_after(y, name)
            rhs_idx, start, _, k_start, _ = CHUNKS[name]
            return late_product(weights, (piece, relay), (0, 1), *base_of(name), k_start, prev=y, target=(rhs_idx, start))

        def early_part(name, piece, relay, part, part_start):
            return late_product(weights, (piece, relay), (0, 1), part, part_start, CHUNKS[name][3])

        def split_late(name, y, part, part_start, tile_rows=TILE_ROWS):
            piece, relay, y = relay_after(y, name)
            rhs_idx, start, _, k_start, _ = CHUNKS[name]
            part = late_product(weights, (piece,), (0,), part, part_start, k_start, tile_rows=tile_rows)
            return late_product(weights, (relay,), (1,), part, 0, k_start, prev=y, target=(rhs_idx, start), tile_rows=tile_rows)

        part_j = early_part("j0", deep["j0"], relay_j0, *base_of("j0"))
        y, part_j = lax.optimization_barrier((y, part_j))
        y = late("e", y)
        part_i = early_part("i0", early_i0, relay_i0, *base_of("i0"))
        part_j = early_part("j1", early_j1, relay_j1, part_j, 0)
        y, part_i, part_j = lax.optimization_barrier((y, part_i, part_j))
        y = late("f", y)
        for name in ("g", "h"):
            y = split_late(name, y, *base_of(name))
        y = split_late("i1", y, part_i, 0, SMALL_ROWS)
        return split_late("j2", y, part_j, 0, SMALL_ROWS)

    return jax.shard_map(body, mesh=mesh, in_specs=(P(("row", "depth"), "col"), P(None, ("row", "depth"), "col")), out_specs=P(None, ("row", "depth"), "col"), check_vma=False)
```

time: 567 us -> 545 us (0.961)
  waiting for transfers between devices: 283 us -> 264 us
  local copies, waits for them, and re-layouts: 58.3 us -> 49.5 us
  starting transfers between devices: 15.9 us -> 24.1 us
    ppermute x24 -> x30, waiting for transfers between devices: 283 us -> 264 us  [permute(): return lax.ppermute(value, axis, SWAP)]
    unnamed x50 -> x46, local copies, waits for them, and re-layouts: 30.3 us -> 20.8 us
    ppermute x24 -> x30, starting transfers between devices: 15.9 us -> 24.1 us  [permute(): return lax.ppermute(value, axis, SWAP)]
    pallas_call x12 -> x10, Pallas kernels: 179 us -> 173 us  [product(): pl.pallas_call(functools.partial(product_kernel, plan), grid=(len(tiles),...]
    pallas_call x6 -> x13, Pallas kernels: 26.4 us -> 30 us  [late_product(): pl.pallas_call(functools.partial(late_kernel, k_start, base_start, target...]
    squeeze x7 -> x9, local copies, waits for them, and re-layouts: 22.5 us -> 23.3 us  [piece_of(): return x[rhs_idx, k_start:k_start + k_rows, start:start + width]]
  transfers between devices with their start and end apart: 24 -> 30, of which waited for: 13 -> 14; matrix products, arithmetic and copies ran while one was open for 4% -> 4% of each run, Pallas kernels for 36% -> 37%
where the time goes in v3:
time: 545 us; the launch traced here: 544 us
  waiting for transfers between devices  264 us (48%)
  Pallas kernels  205 us (38%)
  local copies, waits for them, and re-layouts  49.5 us (9%)
  starting transfers between devices  24.1 us (4%)
    ppermute x30, waiting for transfers between devices, permute(): return lax.ppermute(value, axis, SWAP)  264 us
    pallas_call x10, Pallas kernels, product(): pl.pallas_call(functools.partial(product_kernel, plan), grid=(len(tiles),...  173 us
    pallas_call x13, Pallas kernels, late_product(): pl.pallas_call(functools.partial(late_kernel, k_start, base_start, target...  30 us
    ppermute x30, starting transfers between devices, permute(): return lax.ppermute(value, axis, SWAP)  24.1 us
    squeeze x9, local copies, waits for them, and re-layouts, piece_of(): return x[rhs_idx, k_start:k_start + k_rows, start:start + width]  23.3 us
    unnamed x46, local copies, waits for them, and re-layouts  20.8 us
  transfers between devices with their start and end apart: 30, of which 14 were waited for; matrix products, arithmetic and copies ran while one was open for 4% of the time, Pallas kernels for 37%

profile of v3, /device:TPU:0, one launch (start us, length us, event | category | flops | bytes accessed | tf_op | source)
XLA Modules:
  0.0 543.9 jit_solution(15920937774250520118)
XLA Ops:
  0.0 1.6 slice_bitcast_fusion.12
  1.6 1.7 slice_bitcast_fusion.5
  3.3 2.2 slice.50
  6.4 4.8 slice_bitcast_fusion
  11.2 2.6 collective-permute-start.8
  13.8 1.5 collective-permute-start.3
  15.8 3.2 fusion
  19.1 131.0 %collective-permute-done.9.refs_3_ = bf16[1536,512]{1,0:T(8,128)(2,1)S(1)} collective-permute-done((bf16[1536,512]{1,0:T(8,128)(2,1)S(1)}, bf16[1536,512]{1,0:T(8,128)(2,1)S(1)}, u32[]{:S(2)}, u32[]{:S(2)}) %collective-permute-start.9) | collective-permute-done | bytes 1572896 | tf_op jit(solution)/shard_map/ppermute | solution.py:282
  150.1 3.4 collective-permute-done.10.refs_5_
  153.5 7.5 %product.10.refs_6_ = bf16[3,1536,2048]{2,1,0:T(8,128)(2,1)} custom-call(bf16[1536,3072]{1,0:T(8,128)(2,1)S(1)} %bitcast.27, bf16[512,3072]{1,0:T(8,128)(2,1)S(1)} %collective-permute-done.3.refs_1_, bf16[3,1536,2048]{2,1,0:T(8,128)(2,1)} %refs_2_.13, bf16[1536,512]{1,0:T(8,128)(2,1)S(1)} %collective-permute-done.9.refs_3_, ...), custom_call_target="tpu_custom_call" | custom-call | flops 3221225472 | bytes 6291456 | tf_op jit(solution)/shard_map/product/pallas_call | solution.py:163
  161.0 1.1 copy-done.11
  162.2 14.6 %product.11 = (f32[1536,512]{1,0:T(8,128)}, f32[1536,512]{1,0:T(8,128)}, f32[1536,512]{1,0:T(8,128)}, f32[1536,512]{1,0:T(8,128)}) custom-call(bf16[1536,3072]{1,0:T(8,128)(2,1)} %refs_0_.20, bf16[512,3072]{1,0:T(8,128)(2,1)} %copy-done.3, bf16[3,1536,2048]{2,1,0:T(8,128)(2,1)} %refs_2_.13, ...), custom_call_target="tpu_custom_call" | custom-call | flops 6442450944 | bytes 6291456 | tf_op jit(solution)/shard_map/product/pallas_call | solution.py:163
  176.8 3.7 copy-done
  180.5 1.4 copy-done.12
  181.9 8.2 %product.12.refs_7_ = bf16[3,1536,2048]{2,1,0:T(8,128)(2,1)} custom-call(bf16[1536,3072]{1,0:T(8,128)(2,1)S(1)} %copy-done, bf16[512,3072]{1,0:T(8,128)(2,1)} %collective-permute-done.4.refs_1_.refs_2_, bf16[3,1536,2048]{2,1,0:T(8,128)(2,1)} %refs_2_.13, bf16[1536,512]{1,0:T(8,128)(2,1)S(1)} %collective-permute-done.9.refs_3_, ...), custom_call_target="tpu_custom_call", output_to_operand_aliasing={{}: (6, {})} | custom-call | flops 3221225472 | bytes 6291456 | tf_op jit(solution)/shard_map/product/pallas_call | solution.py:163
  190.2 1.8 collective-permute-start.5
  192.0 6.3 %slice_bitcast_fusion.1 = (bf16[1536,1024]{1,0:T(8,128)(2,1)}, bf16[1536,1024]{1,0:T(8,128)(2,1)}) fusion(bf16[3,1536,2048]{2,1,0:T(8,128)(2,1)} %refs_2_.13), kind=kLoop, calls=%fused_computation.1 | loop fusion | bytes 12582912 | tf_op jit(solution)/shard_map/squeeze | solution.py:291
  198.3 1.5 collective-permute-start.7
  199.8 2.1 copy-done.9
  202.0 28.8 %product.13.refs_6_ = bf16[3,1536,2048]{2,1,0:T(8,128)(2,1)} custom-call(bf16[1536,3072]{1,0:T(8,128)(2,1)} %refs_0_.20, bf16[512,3072]{1,0:T(8,128)(2,1)S(1)} %copy-done.4, bf16[512,3072]{1,0:T(8,128)(2,1)} %collective-permute-done.4.refs_1_.refs_2_, bf16[3,1536,2048]{2,1,0:T(8,128)(2,1)} %refs_2_.13, ...), custom_call_target="tpu_custom_call", output_to_operand_aliasing={{}: (7, {})} | custom-call | flops 19327352832 | bytes 12582912 | tf_op jit(solution)/shard_map/product/pallas_call | solution.py:163
  230.8 14.7 %product.14 = (f32[1536,512]{1,0:T(8,128)}, f32[1536,512]{1,0:T(8,128)}, f32[1536,512]{1,0:T(8,128)}, f32[1536,512]{1,0:T(8,128)}) custom-call(bf16[1536,3072]{1,0:T(8,128)(2,1)} %refs_0_.20, bf16[512,3072]{1,0:T(8,128)(2,1)} %collective-permute-done.4.refs_1_.refs_2_, ...), custom_call_target="tpu_custom_call", output_to_operand_aliasing={{0}: (4, {}), {1}: (5, {}), {2}: (6, {}), {3}: (7, {})} | custom-call | flops 6442450944 | bytes 6291456 | tf_op jit(solution)/shard_map/product/pallas_call | solution.py:163
  245.5 15.5 %collective-permute-done.5.refs_1_.refs_3_ = bf16[512,3072]{1,0:T(8,128)(2,1)} collective-permute-done((bf16[512,3072]{1,0:T(8,128)(2,1)}, bf16[512,3072]{1,0:T(8,128)(2,1)}, u32[]{:S(2)}, u32[]{:S(2)}) %collective-permute-start.5) | collective-permute-done | bytes 3145760 | tf_op jit(solution)/shard_map/ppermute | solution.py:282
  261.0 3.7 copy-done.1
  264.7 1.4 copy-done.13
  266.1 8.5 %product.15.refs_6_ = bf16[3,1536,2048]{2,1,0:T(8,128)(2,1)} custom-call(bf16[1536,3072]{1,0:T(8,128)(2,1)S(1)} %copy-done.1, bf16[512,3072]{1,0:T(8,128)(2,1)} %collective-permute-done.5.refs_1_.refs_3_, bf16[3,1536,2048]{2,1,0:T(8,128)(2,1)} %refs_2_.13, bf16[1536,512]{1,0:T(8,128)(2,1)S(1)} %collective-permute-done.9.refs_3_, ...), custom_call_target="tpu_custom_call", output_to_operand_aliasing={{}: (6, {})} | custom-call | flops 3221225472 | bytes 6291456 | tf_op jit(solution)/shard_map/product/pallas_call | solution.py:163
  274.6 17.9 %product.16.refs_8_ = bf16[3,1536,2048]{2,1,0:T(8,128)(2,1)} custom-call(bf16[1536,3072]{1,0:T(8,128)(2,1)} %refs_0_.20, bf16[512,3072]{1,0:T(8,128)(2,1)} %collective-permute-done.5.refs_1_.refs_3_, bf16[3,1536,2048]{2,1,0:T(8,128)(2,1)} %refs_2_.13, bf16[1536,1536]{1,0:T(8,128)(2,1)} %collective-permute-done.8.refs_4_.refs_3_, ...), custom_call_target="tpu_custom_call", output_to_operand_aliasing={{}: (6, {})} | custom-call | flops 9663676416 | bytes 6291456 | tf_op jit(solution)/shard_map/product/pallas_call | solution.py:163
  292.6 1.8 collective-permute-start.6
  294.3 4.1 collective-permute-done.12.refs_7_
  298.4 1.7 copy-done.16
  300.1 28.8 %product.17.refs_8_ = bf16[3,1536,2048]{2,1,0:T(8,128)(2,1)} custom-call(bf16[1536,3072]{1,0:T(8,128)(2,1)} %refs_0_.20, bf16[512,3072]{1,0:T(8,128)(2,1)S(1)} %copy-done.4, bf16[512,3072]{1,0:T(8,128)(2,1)} %collective-permute-done.4.refs_1_.refs_2_, bf16[512,3072]{1,0:T(8,128)(2,1)} %collective-permute-done.5.refs_1_.refs_3_, ...), custom_call_target="tpu_custom_call", output_to_operand_aliasing={{}: (8, {})} | custom-call | flops 19327352832 | bytes 18874368 | tf_op jit(solution)/shard_map/product/pallas_call | solution.py:163
  328.9 34.1 %collective-permute-done.6.refs_5_ = bf16[1536,1024]{1,0:T(8,128)(2,1)S(1)} collective-permute-done((bf16[1536,1024]{1,0:T(8,128)(2,1)S(1)}, bf16[1536,1024]{1,0:T(8,128)(2,1)S(1)}, u32[]{:S(2)}, u32[]{:S(2)}) %collective-permute-start.6) | collective-permute-done | bytes 3145760 | tf_op jit(solution)/shard_map/ppermute | solution.py:282
  363.1 1.8 slice_bitcast_fusion.8
  364.8 1.8 collective-permute-start.2
  367.9 1.7 collective-permute-start.20
  369.6 3.7 slice_bitcast_fusion.3
  373.7 14.4 %collective-permute-done.20.refs_1_ = bf16[384,256]{1,0:T(8,128)(2,1)S(1)} collective-permute-done((bf16[384,256]{1,0:T(8,128)(2,1)S(1)}, bf16[384,256]{1,0:T(8,128)(2,1)S(1)}, u32[]{:S(2)}, u32[]{:S(2)}) %collective-permute-start.20) | collective-permute-done | bytes 196640 | tf_op jit(solution)/shard_map/ppermute | solution.py:282
  388.1 1.7 copy-done.15
  389.8 28.8 %product.18.refs_4_ = bf16[3,1536,2048]{2,1,0:T(8,128)(2,1)} custom-call(bf16[1536,3072]{1,0:T(8,128)(2,1)} %refs_0_.20, bf16[512,3072]{1,0:T(8,128)(2,1)S(1)} %copy-done.4, bf16[512,3072]{1,0:T(8,128)(2,1)} %collective-permute-done.4.refs_1_.refs_2_, bf16[512,3072]{1,0:T(8,128)(2,1)} %collective-permute-done.5.refs_1_.refs_3_, ...), custom_call_target="tpu_custom_call", output_to_operand_aliasing={{}: (8, {})} | custom-call | flops 19327352832 | bytes 18874368 | tf_op jit(solution)/shard_map/product/pallas_call | solution.py:163
  418.6 14.7 %product.19 = (f32[1536,512]{1,0:T(8,128)}, f32[1536,512]{1,0:T(8,128)}, f32[1536,512]{1,0:T(8,128)}, f32[1536,512]{1,0:T(8,128)}) custom-call(bf16[1536,3072]{1,0:T(8,128)(2,1)} %refs_0_.20, bf16[512,3072]{1,0:T(8,128)(2,1)} %collective-permute-done.5.refs_1_.refs_3_, ...), custom_call_target="tpu_custom_call", output_to_operand_aliasing={{0}: (4, {}), {1}: (5, {}), {2}: (6, {}), {3}: (7, {})} | custom-call | flops 6442450944 | bytes 6291456 | tf_op jit(solution)/shard_map/product/pallas_call | solution.py:163
  433.3 3.7 copy-done.2
  437.0 2.9 late_weights.1.refs_0_
  439.9 1.3 late.13.refs_3_
  441.3 1.7 collective-permute-start.18
  443.5 1.6 collective-permute-done.24.refs_2_
  445.1 1.7 late.16.refs_2_
  446.8 1.7 late.15.refs_2_
  448.7 6.2 %late.14.refs_4_ = bf16[3,1536,2048]{2,1,0:T(8,128)(2,1)} custom-call(bf16[2,1536,1536]{2,1,0:T(8,128)(2,1)S(1)} %late_weights.1.refs_0_, bf16[1536,512]{1,0:T(8,128)(2,1)S(1)} %collective-permute-done.19.refs_1_, bf16[1536,512]{1,0:T(8,128)(2,1)S(1)} %collective-permute-done.22.refs_2_, f32[1536,512]{1,0:T(8,128)S(1)} %copy-done.7, ...), custom_call_target="tpu_custom_call", output_to_operand_aliasing={{}: (4, {})} | custom-call | flops 4831838208 | bytes 3145728 | tf_op jit(solution)/shard_map/late/pallas_call | solution.py:264
  454.9 23.2 %collective-permute-done.18.refs_1_ = bf16[1536,512]{1,0:T(8,128)(2,1)S(1)} collective-permute-done((bf16[1536,512]{1,0:T(8,128)(2,1)S(1)}, bf16[1536,512]{1,0:T(8,128)(2,1)S(1)}, u32[]{:S(2)}, u32[]{:S(2)}) %collective-permute-start.18) | collective-permute-done | bytes 1572896 | tf_op jit(solution)/shard_map/ppermute | solution.py:282
  478.0 1.5 slice_bitcast_fusion.6
  479.5 1.8 collective-permute-start.17
  481.4 6.2 %late.17.refs_3_ = bf16[3,1536,2048]{2,1,0:T(8,128)(2,1)} custom-call(bf16[2,1536,1536]{2,1,0:T(8,128)(2,1)S(1)} %late_weights.1.refs_0_, bf16[1536,512]{1,0:T(8,128)(2,1)S(1)} %collective-permute-done.18.refs_1_, bf16[1536,512]{1,0:T(8,128)(2,1)S(1)} %collective-permute-done.25.refs_2_, f32[1536,512]{1,0:T(8,128)S(1)} %copy-done.8, ...), custom_call_target="tpu_custom_call", output_to_operand_aliasing={{}: (4, {})} | custom-call | flops 4831838208 | bytes 3145728 | tf_op jit(solution)/shard_map/late/pallas_call | solution.py:264
  487.6 11.9 %collective-permute-done.17.refs_1_ = bf16[1536,256]{1,0:T(8,128)(2,1)S(1)} collective-permute-done((bf16[1536,256]{1,0:T(8,128)(2,1)S(1)}, bf16[1536,256]{1,0:T(8,128)(2,1)S(1)}, u32[]{:S(2)}, u32[]{:S(2)}) %collective-permute-start.17) | collective-permute-done | bytes 786464 | tf_op jit(solution)/shard_map/ppermute | solution.py:282
  499.5 1.7 collective-permute-start.16
  501.2 1.7 late.18.refs_2_
  503.0 2.5 late.19.refs_3_
  505.5 14.0 %collective-permute-done.16.refs_1_ = bf16[1536,256]{1,0:T(8,128)(2,1)S(1)} collective-permute-done((bf16[1536,256]{1,0:T(8,128)(2,1)S(1)}, bf16[1536,256]{1,0:T(8,128)(2,1)S(1)}, u32[]{:S(2)}, u32[]{:S(2)}) %collective-permute-start.16) | collective-permute-done | bytes 786464 | tf_op jit(solution)/shard_map/ppermute | solution.py:282
  519.4 1.7 collective-permute-start.15
  521.2 1.7 late.20.refs_2_
  522.9 2.5 late.21.refs_3_
  525.4 5.6 %collective-permute-done.15.refs_1_ = bf16[768,256]{1,0:T(8,128)(2,1)S(1)} collective-permute-done((bf16[768,256]{1,0:T(8,128)(2,1)S(1)}, bf16[768,256]{1,0:T(8,128)(2,1)S(1)}, u32[]{:S(2)}, u32[]{:S(2)}) %collective-permute-start.15) | collective-permute-done | bytes 393248 | tf_op jit(solution)/shard_map/ppermute | solution.py:282
  531.9 1.8 collective-permute-start.14
  534.5 1.7 late.23.refs_3_
  536.2 4.5 collective-permute-done.14.refs_1_
  542.2 1.5 late.25
  (78 shorter events, 7.3 us)
Async XLA Ops:
  1.6 14.2 %slice-start = ((s8[9437184]{0:T(1024)(128)(4,1)}), s8[4194304]{0:T(1024)(128)(4,1)S(1)}, s32[]{:S(2)}) async-start(s8[9437184]{0:T(1024)(128)(4,1)} %bitcast.26), calls=%async_computation | async-start | bytes 8388608
  3.3 12.5 %slice-start.1 = ((s8[9437184]{0:T(1024)(128)(4,1)}), s8[4194304]{0:T(1024)(128)(4,1)S(1)}, s32[]{:S(2)}) async-start(s8[9437184]{0:T(1024)(128)(4,1)} %bitcast.26), calls=%async_computation.1 | async-start | bytes 8388608
  5.5 10.3 %slice-start.2 = ((s8[9437184]{0:T(1024)(128)(4,1)}), s8[1048576]{0:T(1024)(128)(4,1)S(1)}, s32[]{:S(2)}) async-start(s8[9437184]{0:T(1024)(128)(4,1)} %bitcast.26), calls=%async_computation.2 | async-start | bytes 2097152
  5.6 148.0 %collective-permute-start = (bf16[3,1536,2048]{2,1,0:T(8,128)(2,1)}, bf16[3,1536,2048]{2,1,0:T(8,128)(2,1)}, u32[]{:S(2)}, u32[]{:S(2)}) collective-permute-start(bf16[3,1536,2048]{2,1,0:T(8,128)(2,1)} %refs_2_.13), channel_id=1, source_target_pairs={{0,1},{1,0},{2,3},{3,2},{4,5},{5,4},{6,7},{7,6}} | collective-permute-start | bytes 56623112 | tf_op jit(solution)/shard_map/ppermute | solution.py:282
  11.2 178.9 %collective-permute-start.8 = (bf16[1536,1536]{1,0:T(8,128)(2,1)}, bf16[1536,1536]{1,0:T(8,128)(2,1)}, u32[]{:S(2)}, u32[]{:S(2)}) collective-permute-start(bf16[1536,1536]{1,0:T(8,128)(2,1)} %slice_bitcast_fusion), channel_id=1, source_target_pairs={{0,4},{4,0},{1,5},{5,1},{2,6},{6,2},{3,7},{7,3}} | collective-permute-start | bytes 14155784 | tf_op jit(solution)/shard_map/ppermute | solution.py:282
  13.8 136.3 %collective-permute-start.3 = (bf16[512,3072]{1,0:T(8,128)(2,1)S(1)}, bf16[512,3072]{1,0:T(8,128)(2,1)S(1)}, u32[]{:S(2)}, u32[]{:S(2)}) collective-permute-start(bf16[512,3072]{1,0:T(8,128)(2,1)S(1)} %slice.50), channel_id=1, source_target_pairs={{0,2},{2,0},{1,3},{3,1},{4,6},{6,4},{5,7},{7,5}} | collective-permute-start | bytes 9437192 | tf_op jit(solution)/shard_map/ppermute | solution.py:282
  15.3 134.8 %collective-permute-start.9 = (bf16[1536,512]{1,0:T(8,128)(2,1)S(1)}, bf16[1536,512]{1,0:T(8,128)(2,1)S(1)}, u32[]{:S(2)}, u32[]{:S(2)}) collective-permute-start(bf16[1536,512]{1,0:T(8,128)(2,1)S(1)} %slice_bitcast_fusion.5), channel_id=1, source_target_pairs={{0,4},{4,0},{1,5},{5,1},{2,6},{6,2},{3,7},{7,3}} | collective-permute-start | bytes 4718600 | tf_op jit(solution)/shard_map/ppermute | solution.py:282
  19.0 157.8 %collective-permute-start.4 = (bf16[512,3072]{1,0:T(8,128)(2,1)}, bf16[512,3072]{1,0:T(8,128)(2,1)}, u32[]{:S(2)}, u32[]{:S(2)}) collective-permute-start(bf16[512,3072]{1,0:T(8,128)(2,1)} %get-tuple-element.158), channel_id=1, source_target_pairs={{0,2},{2,0},{1,3},{3,1},{4,6},{6,4},{5,7},{7,5}} | collective-permute-start | bytes 9437192 | tf_op jit(solution)/shard_map/ppermute | solution.py:282
  150.1 3.4 collective-permute-start.10
  150.1 10.9 %copy-start.3 = (bf16[512,3072]{1,0:T(8,128)(2,1)}, bf16[512,3072]{1,0:T(8,128)(2,1)S(1)}, u32[]{:S(2)}) copy-start(bf16[512,3072]{1,0:T(8,128)(2,1)S(1)} %collective-permute-done.3.refs_1_) | copy-start | bytes 9437188
  161.0 1.2 copy-start.11
  176.8 3.7 copy-start
  180.5 1.4 copy-start.12
  190.1 9.7 %collective-permute-start.11 = (bf16[1536,1536]{1,0:T(8,128)(2,1)}, bf16[1536,1536]{1,0:T(8,128)(2,1)S(1)}, u32[]{:S(2)}, u32[]{:S(2)}) collective-permute-start(bf16[1536,1536]{1,0:T(8,128)(2,1)} %collective-permute-done.8.refs_4_.refs_3_), channel_id=1, source_target_pairs={{0,1},{1,0},{2,3},{3,2},{4,5},{5,4},{6,7},{7,6}} | collective-permute-start | bytes 14155784 | tf_op jit(solution)/shard_map/ppermute | solution.py:282
  190.2 11.8 %copy-start.4 = (bf16[512,3072]{1,0:T(8,128)(2,1)S(1)}, bf16[512,3072]{1,0:T(8,128)(2,1)}, u32[]{:S(2)}) copy-start(bf16[512,3072]{1,0:T(8,128)(2,1)} %copy-done.3) | copy-start | bytes 9437188
  190.2 70.8 %collective-permute-start.5 = (bf16[512,3072]{1,0:T(8,128)(2,1)}, bf16[512,3072]{1,0:T(8,128)(2,1)}, u32[]{:S(2)}, u32[]{:S(2)}) collective-permute-start(bf16[512,3072]{1,0:T(8,128)(2,1)} %get-tuple-element.157), channel_id=1, source_target_pairs={{0,2},{2,0},{1,3},{3,1},{4,6},{6,4},{5,7},{7,5}} | collective-permute-start | bytes 9437192 | tf_op jit(solution)/shard_map/ppermute | solution.py:282
  198.3 94.2 %collective-permute-start.7 = (bf16[1536,1024]{1,0:T(8,128)(2,1)}, bf16[1536,1024]{1,0:T(8,128)(2,1)}, u32[]{:S(2)}, u32[]{:S(2)}) collective-permute-start(bf16[1536,1024]{1,0:T(8,128)(2,1)} %get-tuple-element.155), channel_id=1, source_target_pairs={{0,4},{4,0},{1,5},{5,1},{2,6},{6,2},{3,7},{7,3}} | collective-permute-start | bytes 9437192 | tf_op jit(solution)/shard_map/ppermute | solution.py:282
  199.8 2.1 copy-start.9
  261.0 3.7 copy-start.1
  264.7 1.4 copy-start.13
  266.1 8.5 %copy-start.10 = (bf16[1536,1536]{1,0:T(8,128)(2,1)S(1)}, bf16[1536,1536]{1,0:T(8,128)(2,1)}, u32[]{:S(2)}) copy-start(bf16[1536,1536]{1,0:T(8,128)(2,1)} %copy-done.9) | copy-start | bytes 14155780
  274.6 17.9 %copy-start.17 = (bf16[1536,1024]{1,0:T(8,128)(2,1)S(1)}, bf16[1536,1024]{1,0:T(8,128)(2,1)}, u32[]{:S(2)}) copy-start(bf16[1536,1024]{1,0:T(8,128)(2,1)} %get-tuple-element.156) | copy-start | bytes 9437188
  292.5 5.9 %collective-permute-start.12 = (bf16[1536,1024]{1,0:T(8,128)(2,1)}, bf16[1536,1024]{1,0:T(8,128)(2,1)S(1)}, u32[]{:S(2)}, u32[]{:S(2)}) collective-permute-start(bf16[1536,1024]{1,0:T(8,128)(2,1)} %collective-permute-done.7.refs_5_), channel_id=1, source_target_pairs={{0,1},{1,0},{2,3},{3,2},{4,5},{5,4},{6,7},{7,6}} | collective-permute-start | bytes 9437192 | tf_op jit(solution)/shard_map/ppermute | solution.py:282
  292.6 75.3 %copy-start.19 = (bf16[384,256]{1,0:T(8,128)(2,1)S(1)}, bf16[384,256]{1,0:T(8,128)(2,1)}, u32[]{:S(2)}) copy-start(bf16[384,256]{1,0:T(8,128)(2,1)} %slice_bitcast_fusion.12) | copy-start | bytes 589828
  292.6 70.5 %collective-permute-start.6 = (bf16[1536,1024]{1,0:T(8,128)(2,1)S(1)}, bf16[1536,1024]{1,0:T(8,128)(2,1)S(1)}, u32[]{:S(2)}, u32[]{:S(2)}) collective-permute-start(bf16[1536,1024]{1,0:T(8,128)(2,1)S(1)} %copy-done.17), channel_id=1, source_target_pairs={{0,4},{4,0},{1,5},{5,1},{2,6},{6,2},{3,7},{7,3}} | collective-permute-start | bytes 9437192 | tf_op jit(solution)/shard_map/ppermute | solution.py:282
  298.4 1.7 copy-start.16
  363.1 10.3 %copy-start.14 = (bf16[1536,1024]{1,0:T(8,128)(2,1)}, bf16[1536,1024]{1,0:T(8,128)(2,1)S(1)}, u32[]{:S(2)}) copy-start(bf16[1536,1024]{1,0:T(8,128)(2,1)S(1)} %collective-permute-done.6.refs_5_) | copy-start | bytes 9437188
  363.1 25.0 %collective-permute-start.13 = (bf16[1536,1024]{1,0:T(8,128)(2,1)S(1)}, bf16[1536,1024]{1,0:T(8,128)(2,1)S(1)}, u32[]{:S(2)}, u32[]{:S(2)}) collective-permute-start(bf16[1536,1024]{1,0:T(8,128)(2,1)S(1)} %collective-permute-done.6.refs_5_), channel_id=1, source_target_pairs={{0,1},{1,0},{2,3},{3,2},{4,5},{5,4},{6,7},{7,6}} | collective-permute-start | bytes 9437192 | tf_op jit(solution)/shard_map/ppermute | solution.py:282
  364.8 53.8 %collective-permute-start.2 = (bf16[768,256]{1,0:T(8,128)(2,1)S(1)}, bf16[768,256]{1,0:T(8,128)(2,1)S(1)}, u32[]{:S(2)}, u32[]{:S(2)}) collective-permute-start(bf16[768,256]{1,0:T(8,128)(2,1)S(1)} %get-tuple-element.154), channel_id=1, source_target_pairs={{0,4},{4,0},{1,5},{5,1},{2,6},{6,2},{3,7},{7,3}} | collective-permute-start | bytes 1179656 | tf_op jit(solution)/shard_map/ppermute | solution.py:282
  367.6 51.0 %collective-permute-start.1 = (bf16[640,256]{1,0:T(8,128)(2,1)S(1)}, bf16[640,256]{1,0:T(8,128)(2,1)S(1)}, u32[]{:S(2)}, u32[]{:S(2)}) collective-permute-start(bf16[640,256]{1,0:T(8,128)(2,1)S(1)} %slice_bitcast_fusion.10), channel_id=1, source_target_pairs={{0,4},{4,0},{1,5},{5,1},{2,6},{6,2},{3,7},{7,3}} | collective-permute-start | bytes 983048 | tf_op jit(solution)/shard_map/ppermute | solution.py:282
  367.9 20.2 %collective-permute-start.20 = (bf16[384,256]{1,0:T(8,128)(2,1)S(1)}, bf16[384,256]{1,0:T(8,128)(2,1)S(1)}, u32[]{:S(2)}, u32[]{:S(2)}) collective-permute-start(bf16[384,256]{1,0:T(8,128)(2,1)S(1)} %copy-done.19), channel_id=1, source_target_pairs={{0,4},{4,0},{1,5},{5,1},{2,6},{6,2},{3,7},{7,3}} | collective-permute-start | bytes 589832 | tf_op jit(solution)/shard_map/ppermute | solution.py:282
  373.4 67.8 %collective-permute-start.19 = (bf16[1536,512]{1,0:T(8,128)(2,1)}, bf16[1536,512]{1,0:T(8,128)(2,1)S(1)}, u32[]{:S(2)}, u32[]{:S(2)}) collective-permute-start(bf16[1536,512]{1,0:T(8,128)(2,1)} %get-tuple-element.149), channel_id=1, source_target_pairs={{0,4},{4,0},{1,5},{5,1},{2,6},{6,2},{3,7},{7,3}} | collective-permute-start | bytes 4718600 | tf_op jit(solution)/shard_map/ppermute | solution.py:282
  388.1 51.8 %collective-permute-start.21 = (bf16[384,256]{1,0:T(8,128)(2,1)S(1)}, bf16[384,256]{1,0:T(8,128)(2,1)S(1)}, u32[]{:S(2)}, u32[]{:S(2)}) collective-permute-start(bf16[384,256]{1,0:T(8,128)(2,1)S(1)} %collective-permute-done.20.refs_1_), channel_id=1, source_target_pairs={{0,1},{1,0},{2,3},{3,2},{4,5},{5,4},{6,7},{7,6}} | collective-permute-start | bytes 589832 | tf_op jit(solution)/shard_map/ppermute | solution.py:282
  388.1 1.7 copy-start.15
  433.3 3.7 copy-start.2
  437.0 2.9 copy-start.6
  439.8 1.4 copy-start.18
  441.2 7.4 %collective-permute-start.22 = (bf16[1536,512]{1,0:T(8,128)(2,1)S(1)}, bf16[1536,512]{1,0:T(8,128)(2,1)S(1)}, u32[]{:S(2)}, u32[]{:S(2)}) collective-permute-start(bf16[1536,512]{1,0:T(8,128)(2,1)S(1)} %collective-permute-done.19.refs_1_), channel_id=1, source_target_pairs={{0,1},{1,0},{2,3},{3,2},{4,5},{5,4},{6,7},{7,6}} | collective-permute-start | bytes 4718600 | tf_op jit(solution)/shard_map/ppermute | solution.py:282
  441.3 36.8 %collective-permute-start.18 = (bf16[1536,512]{1,0:T(8,128)(2,1)S(1)}, bf16[1536,512]{1,0:T(8,128)(2,1)S(1)}, u32[]{:S(2)}, u32[]{:S(2)}) collective-permute-start(bf16[1536,512]{1,0:T(8,128)(2,1)S(1)} %copy-done.18), channel_id=1, source_target_pairs={{0,4},{4,0},{1,5},{5,1},{2,6},{6,2},{3,7},{7,3}} | collective-permute-start | bytes 4718600 | tf_op jit(solution)/shard_map/ppermute | solution.py:282
  443.0 2.1 collective-permute-start.24
  443.2 3.6 collective-permute-start.23
  446.8 1.9 copy-start.7
  454.8 26.6 %copy-start.8 = (f32[1536,512]{1,0:T(8,128)S(1)}, f32[1536,512]{1,0:T(8,128)}, u32[]{:S(2)}) copy-start(f32[1536,512]{1,0:T(8,128)} %get-tuple-element.136.refs_3_) | copy-start | bytes 9437188
  478.0 3.4 collective-permute-start.25
  479.5 21.7 %copy-start.5 = (f32[1536,512]{1,0:T(8,128)S(1)}, f32[1536,512]{1,0:T(8,128)}, u32[]{:S(2)}) copy-start(f32[1536,512]{1,0:T(8,128)} %get-tuple-element.139.refs_2_) | copy-start | bytes 9437188
  479.5 20.0 %collective-permute-start.17 = (bf16[1536,256]{1,0:T(8,128)(2,1)S(1)}, bf16[1536,256]{1,0:T(8,128)(2,1)S(1)}, u32[]{:S(2)}, u32[]{:S(2)}) collective-permute-start(bf16[1536,256]{1,0:T(8,128)(2,1)S(1)} %get-tuple-element.151), channel_id=1, source_target_pairs={{0,4},{4,0},{1,5},{5,1},{2,6},{6,2},{3,7},{7,3}} | collective-permute-start | bytes 2359304 | tf_op jit(solution)/shard_map/ppermute | solution.py:282
  499.5 3.5 collective-permute-start.26
  499.5 20.0 %collective-permute-start.16 = (bf16[1536,256]{1,0:T(8,128)(2,1)S(1)}, bf16[1536,256]{1,0:T(8,128)(2,1)S(1)}, u32[]{:S(2)}, u32[]{:S(2)}) collective-permute-start(bf16[1536,256]{1,0:T(8,128)(2,1)S(1)} %get-tuple-element.152), channel_id=1, source_target_pairs={{0,4},{4,0},{1,5},{5,1},{2,6},{6,2},{3,7},{7,3}} | collective-permute-start | bytes 2359304 | tf_op jit(solution)/shard_map/ppermute | solution.py:282
  519.4 3.5 collective-permute-start.27
  519.4 11.5 %collective-permute-start.15 = (bf16[768,256]{1,0:T(8,128)(2,1)S(1)}, bf16[768,256]{1,0:T(8,128)(2,1)S(1)}, u32[]{:S(2)}, u32[]{:S(2)}) collective-permute-start(bf16[768,256]{1,0:T(8,128)(2,1)S(1)} %get-tuple-element.153), channel_id=1, source_target_pairs={{0,4},{4,0},{1,5},{5,1},{2,6},{6,2},{3,7},{7,3}} | collective-permute-start | bytes 1179656 | tf_op jit(solution)/shard_map/ppermute | solution.py:282
  531.0 3.5 collective-permute-start.28
  531.9 8.7 %collective-permute-start.14 = (bf16[512,256]{1,0:T(8,128)(2,1)S(1)}, bf16[512,256]{1,0:T(8,128)(2,1)S(1)}, u32[]{:S(2)}, u32[]{:S(2)}) collective-permute-start(bf16[512,256]{1,0:T(8,128)(2,1)S(1)} %slice_bitcast_fusion.11), channel_id=1, source_target_pairs={{0,4},{4,0},{1,5},{5,1},{2,6},{6,2},{3,7},{7,3}} | collective-permute-start | bytes 786440 | tf_op jit(solution)/shard_map/ppermute | solution.py:282
  540.7 1.5 collective-permute-start.29

commit v4 on v3

--- a/solution.py
+++ b/solution.py
@@ -18,13 +18,14 @@
     "f": (2, 512, 512, 0, 1536),
     "g": (2, 1024, 256, 0, 1536),
     "h": (2, 1280, 256, 0, 1536),
-    "i0": (2, 1536, 256, 0, 768),
-    "i1": (2, 1536, 256, 768, 768),
+    "i0": (2, 1536, 256, 0, 1024),
+    "i1": (2, 1536, 256, 1024, 512),
     "j0": (2, 1792, 256, 0, 384),
-    "j1": (2, 1792, 256, 384, 640),
-    "j2": (2, 1792, 256, 1024, 512),
+    "j1": (2, 1792, 256, 384, 768),
+    "j2": (2, 1792, 256, 1152, 384),
 }
-SEND_ORDER = ("j0", "a", "b", "c", "d", "i0", "j1", "e", "f", "g", "h", "i1", "j2")
+SEND_ORDER = ("j0", "a", "b", "c", "d", "i0", "j1", "e", "f", "g", "h")
+SENT_LATE = ("i1", "j2")
 LATE_COLS = (2, 0, 2048)
 TILE_ROWS = 512
 TILE_COLS = 512
@@ -363,6 +364,9 @@
         part_j = early_part("j1", early_j1, relay_j1, part_j, 0)
         y, part_i, part_j = lax.optimization_barrier((y, part_i, part_j))
         y = late("f", y)
+        x_gate, y = lax.optimization_barrier((x_local, y))
+        for name in SENT_LATE:
+            deep[name] = permute(piece_of(x_gate, CHUNKS[name]), "depth")
         for name in ("g", "h"):
             y = split_late(name, y, *base_of(name))
         y = split_late("i1", y, part_i, 0, SMALL_ROWS)

time: 545 us -> 545 us (level)
    squeeze x9 -> x10, local copies, waits for them, and re-layouts: 23.3 us -> 23.9 us  [piece_of(): return x[rhs_idx, k_start:k_start + k_rows, start:start + width]]
where the time goes in v4:
time: 545 us; the launch traced here: 544 us
  waiting for transfers between devices  264 us (48%)
  Pallas kernels  205 us (38%)
  local copies, waits for them, and re-layouts  50.1 us (9%)
  starting transfers between devices  24 us (4%)
    ppermute x30, waiting for transfers between devices, permute(): return lax.ppermute(value, axis, SWAP)  264 us
    pallas_call x10, Pallas kernels, product(): pl.pallas_call(functools.partial(product_kernel, plan), grid=(len(tiles),...  172 us
    pallas_call x13, Pallas kernels, late_product(): pl.pallas_call(functools.partial(late_kernel, k_start, base_start, target...  30 us
    ppermute x30, starting transfers between devices, permute(): return lax.ppermute(value, axis, SWAP)  24 us
    squeeze x10, local copies, waits for them, and re-layouts, piece_of(): return x[rhs_idx, k_start:k_start + k_rows, start:start + width]  23.9 us
    unnamed x46, local copies, waits for them, and re-layouts  20.7 us
  transfers between devices with their start and end apart: 30, of which 14 were waited for; matrix products, arithmetic and copies ran while one was open for 4% of the time, Pallas kernels for 37%

profile of v4, /device:TPU:0, one launch (start us, length us, event | category | flops | bytes accessed | tf_op | source)
XLA Modules:
  0.0 544.5 jit_solution(11209229518527299378)
XLA Ops:
  0.0 1.6 slice_bitcast_fusion.12
  1.6 1.7 slice_bitcast_fusion.5
  3.3 2.2 slice.50
  6.4 4.8 slice_bitcast_fusion
  11.2 2.6 collective-permute-start.8
  13.8 1.5 collective-permute-start.3
  15.8 3.2 fusion
  19.1 131.0 %collective-permute-done.9.refs_3_ = bf16[1536,512]{1,0:T(8,128)(2,1)S(1)} collective-permute-done((bf16[1536,512]{1,0:T(8,128)(2,1)S(1)}, bf16[1536,512]{1,0:T(8,128)(2,1)S(1)}, u32[]{:S(2)}, u32[]{:S(2)}) %collective-permute-start.9) | collective-permute-done | bytes 1572896 | tf_op jit(solution)/shard_map/ppermute | solution.py:283
  150.1 3.4 collective-permute-done.10.refs_5_
  153.5 7.5 %product.10.refs_6_ = bf16[3,1536,2048]{2,1,0:T(8,128)(2,1)} custom-call(bf16[1536,3072]{1,0:T(8,128)(2,1)S(1)} %bitcast.27, bf16[512,3072]{1,0:T(8,128)(2,1)S(1)} %collective-permute-done.3.refs_1_, bf16[3,1536,2048]{2,1,0:T(8,128)(2,1)} %refs_2_.13, bf16[1536,512]{1,0:T(8,128)(2,1)S(1)} %collective-permute-done.9.refs_3_, ...), custom_call_target="tpu_custom_call" | custom-call | flops 3221225472 | bytes 6291456 | tf_op jit(solution)/shard_map/product/pallas_call | solution.py:164
  161.0 1.2 copy-done.11
  162.2 14.6 %product.11 = (f32[1536,512]{1,0:T(8,128)}, f32[1536,512]{1,0:T(8,128)}, f32[1536,512]{1,0:T(8,128)}, f32[1536,512]{1,0:T(8,128)}) custom-call(bf16[1536,3072]{1,0:T(8,128)(2,1)} %refs_0_.20, bf16[512,3072]{1,0:T(8,128)(2,1)} %copy-done.3, bf16[3,1536,2048]{2,1,0:T(8,128)(2,1)} %refs_2_.13, ...), custom_call_target="tpu_custom_call" | custom-call | flops 6442450944 | bytes 6291456 | tf_op jit(solution)/shard_map/product/pallas_call | solution.py:164
  176.8 3.7 copy-done
  180.5 1.4 copy-done.12
  181.9 8.2 %product.12.refs_7_ = bf16[3,1536,2048]{2,1,0:T(8,128)(2,1)} custom-call(bf16[1536,3072]{1,0:T(8,128)(2,1)S(1)} %copy-done, bf16[512,3072]{1,0:T(8,128)(2,1)} %collective-permute-done.4.refs_1_.refs_2_, bf16[3,1536,2048]{2,1,0:T(8,128)(2,1)} %refs_2_.13, bf16[1536,512]{1,0:T(8,128)(2,1)S(1)} %collective-permute-done.9.refs_3_, ...), custom_call_target="tpu_custom_call", output_to_operand_aliasing={{}: (6, {})} | custom-call | flops 3221225472 | bytes 6291456 | tf_op jit(solution)/shard_map/product/pallas_call | solution.py:164
  190.2 1.8 collective-permute-start.5
  192.0 6.3 %slice_bitcast_fusion.1 = (bf16[1536,1024]{1,0:T(8,128)(2,1)}, bf16[1536,1024]{1,0:T(8,128)(2,1)}) fusion(bf16[3,1536,2048]{2,1,0:T(8,128)(2,1)} %refs_2_.13), kind=kLoop, calls=%fused_computation.1 | loop fusion | bytes 12582912 | tf_op jit(solution)/shard_map/squeeze | solution.py:292
  198.3 1.5 collective-permute-start.7
  199.9 2.2 copy-done.9
  202.0 28.8 %product.13.refs_6_ = bf16[3,1536,2048]{2,1,0:T(8,128)(2,1)} custom-call(bf16[1536,3072]{1,0:T(8,128)(2,1)} %refs_0_.20, bf16[512,3072]{1,0:T(8,128)(2,1)S(1)} %copy-done.4, bf16[512,3072]{1,0:T(8,128)(2,1)} %collective-permute-done.4.refs_1_.refs_2_, bf16[3,1536,2048]{2,1,0:T(8,128)(2,1)} %refs_2_.13, ...), custom_call_target="tpu_custom_call", output_to_operand_aliasing={{}: (7, {})} | custom-call | flops 19327352832 | bytes 12582912 | tf_op jit(solution)/shard_map/product/pallas_call | solution.py:164
  230.8 14.7 %product.14 = (f32[1536,512]{1,0:T(8,128)}, f32[1536,512]{1,0:T(8,128)}, f32[1536,512]{1,0:T(8,128)}, f32[1536,512]{1,0:T(8,128)}) custom-call(bf16[1536,3072]{1,0:T(8,128)(2,1)} %refs_0_.20, bf16[512,3072]{1,0:T(8,128)(2,1)} %collective-permute-done.4.refs_1_.refs_2_, ...), custom_call_target="tpu_custom_call", output_to_operand_aliasing={{0}: (4, {}), {1}: (5, {}), {2}: (6, {}), {3}: (7, {})} | custom-call | flops 6442450944 | bytes 6291456 | tf_op jit(solution)/shard_map/product/pallas_call | solution.py:164
  245.5 15.5 %collective-permute-done.5.refs_1_.refs_3_ = bf16[512,3072]{1,0:T(8,128)(2,1)} collective-permute-done((bf16[512,3072]{1,0:T(8,128)(2,1)}, bf16[512,3072]{1,0:T(8,128)(2,1)}, u32[]{:S(2)}, u32[]{:S(2)}) %collective-permute-start.5) | collective-permute-done | bytes 3145760 | tf_op jit(solution)/shard_map/ppermute | solution.py:283
  261.0 3.7 copy-done.1
  264.7 1.4 copy-done.13
  266.1 8.5 %product.15.refs_6_ = bf16[3,1536,2048]{2,1,0:T(8,128)(2,1)} custom-call(bf16[1536,3072]{1,0:T(8,128)(2,1)S(1)} %copy-done.1, bf16[512,3072]{1,0:T(8,128)(2,1)} %collective-permute-done.5.refs_1_.refs_3_, bf16[3,1536,2048]{2,1,0:T(8,128)(2,1)} %refs_2_.13, bf16[1536,512]{1,0:T(8,128)(2,1)S(1)} %collective-permute-done.9.refs_3_, ...), custom_call_target="tpu_custom_call", output_to_operand_aliasing={{}: (6, {})} | custom-call | flops 3221225472 | bytes 6291456 | tf_op jit(solution)/shard_map/product/pallas_call | solution.py:164
  274.6 17.9 %product.16.refs_8_ = bf16[3,1536,2048]{2,1,0:T(8,128)(2,1)} custom-call(bf16[1536,3072]{1,0:T(8,128)(2,1)} %refs_0_.20, bf16[512,3072]{1,0:T(8,128)(2,1)} %collective-permute-done.5.refs_1_.refs_3_, bf16[3,1536,2048]{2,1,0:T(8,128)(2,1)} %refs_2_.13, bf16[1536,1536]{1,0:T(8,128)(2,1)} %collective-permute-done.8.refs_4_.refs_3_, ...), custom_call_target="tpu_custom_call", output_to_operand_aliasing={{}: (6, {})} | custom-call | flops 9663676416 | bytes 6291456 | tf_op jit(solution)/shard_map/product/pallas_call | solution.py:164
  292.6 1.8 collective-permute-start.6
  294.4 4.1 collective-permute-done.12.refs_7_
  298.4 1.7 copy-done.16
  300.1 28.8 %product.17.refs_8_ = bf16[3,1536,2048]{2,1,0:T(8,128)(2,1)} custom-call(bf16[1536,3072]{1,0:T(8,128)(2,1)} %refs_0_.20, bf16[512,3072]{1,0:T(8,128)(2,1)S(1)} %copy-done.4, bf16[512,3072]{1,0:T(8,128)(2,1)} %collective-permute-done.4.refs_1_.refs_2_, bf16[512,3072]{1,0:T(8,128)(2,1)} %collective-permute-done.5.refs_1_.refs_3_, ...), custom_call_target="tpu_custom_call", output_to_operand_aliasing={{}: (8, {})} | custom-call | flops 19327352832 | bytes 18874368 | tf_op jit(solution)/shard_map/product/pallas_call | solution.py:164
  328.9 34.1 %collective-permute-done.6.refs_5_ = bf16[1536,1024]{1,0:T(8,128)(2,1)S(1)} collective-permute-done((bf16[1536,1024]{1,0:T(8,128)(2,1)S(1)}, bf16[1536,1024]{1,0:T(8,128)(2,1)S(1)}, u32[]{:S(2)}, u32[]{:S(2)}) %collective-permute-start.6) | collective-permute-done | bytes 3145760 | tf_op jit(solution)/shard_map/ppermute | solution.py:283
  363.1 1.5 slice_bitcast_fusion.8
  364.5 1.8 collective-permute-start.2
  367.6 1.7 collective-permute-start.16
  369.4 3.7 slice_bitcast_fusion.3
  373.4 18.6 %collective-permute-done.16.refs_1_ = bf16[384,256]{1,0:T(8,128)(2,1)S(1)} collective-permute-done((bf16[384,256]{1,0:T(8,128)(2,1)S(1)}, bf16[384,256]{1,0:T(8,128)(2,1)S(1)}, u32[]{:S(2)}, u32[]{:S(2)}) %collective-permute-start.16) | collective-permute-done | bytes 196640 | tf_op jit(solution)/shard_map/ppermute | solution.py:283
  392.0 1.7 copy-done.15
  393.7 28.8 %product.18.refs_4_ = bf16[3,1536,2048]{2,1,0:T(8,128)(2,1)} custom-call(bf16[1536,3072]{1,0:T(8,128)(2,1)} %refs_0_.20, bf16[512,3072]{1,0:T(8,128)(2,1)S(1)} %copy-done.4, bf16[512,3072]{1,0:T(8,128)(2,1)} %collective-permute-done.4.refs_1_.refs_2_, bf16[512,3072]{1,0:T(8,128)(2,1)} %collective-permute-done.5.refs_1_.refs_3_, ...), custom_call_target="tpu_custom_call", output_to_operand_aliasing={{}: (8, {})} | custom-call | flops 19327352832 | bytes 18874368 | tf_op jit(solution)/shard_map/product/pallas_call | solution.py:164
  422.6 14.7 %product.19 = (f32[1536,512]{1,0:T(8,128)}, f32[1536,512]{1,0:T(8,128)}, f32[1536,512]{1,0:T(8,128)}, f32[1536,512]{1,0:T(8,128)}) custom-call(bf16[1536,3072]{1,0:T(8,128)(2,1)} %refs_0_.20, bf16[512,3072]{1,0:T(8,128)(2,1)} %collective-permute-done.5.refs_1_.refs_3_, ...), custom_call_target="tpu_custom_call", output_to_operand_aliasing={{0}: (4, {}), {1}: (5, {}), {2}: (6, {}), {3}: (7, {})} | custom-call | flops 6442450944 | bytes 6291456 | tf_op jit(solution)/shard_map/product/pallas_call | solution.py:164
  437.2 3.7 copy-done.2
  440.9 2.9 late_weights.1.refs_0_
  443.8 1.3 late.13.refs_3_
  445.2 1.7 collective-permute-start.14
  447.4 2.4 collective-permute-done.20.refs_2_
  449.9 1.7 late.16.refs_2_
  451.6 2.1 late.15.refs_2_
  453.8 6.2 %late.14.refs_4_ = bf16[3,1536,2048]{2,1,0:T(8,128)(2,1)} custom-call(bf16[2,1536,1536]{2,1,0:T(8,128)(2,1)S(1)} %late_weights.1.refs_0_, bf16[1536,512]{1,0:T(8,128)(2,1)S(1)} %collective-permute-done.15.refs_1_, bf16[1536,512]{1,0:T(8,128)(2,1)S(1)} %collective-permute-done.18.refs_2_, f32[1536,512]{1,0:T(8,128)S(1)} %copy-done.7, ...), custom_call_target="tpu_custom_call", output_to_operand_aliasing={{}: (4, {})} | custom-call | flops 4831838208 | bytes 3145728 | tf_op jit(solution)/shard_map/late/pallas_call | solution.py:265
  460.0 21.9 %collective-permute-done.14.refs_1_ = bf16[1536,512]{1,0:T(8,128)(2,1)S(1)} collective-permute-done((bf16[1536,512]{1,0:T(8,128)(2,1)S(1)}, bf16[1536,512]{1,0:T(8,128)(2,1)S(1)}, u32[]{:S(2)}, u32[]{:S(2)}) %collective-permute-start.14) | collective-permute-done | bytes 1572896 | tf_op jit(solution)/shard_map/ppermute | solution.py:283
  482.0 1.5 slice_bitcast_fusion.6
  483.5 1.7 collective-permute-start.25
  485.4 6.2 %late.17.refs_3_ = bf16[3,1536,2048]{2,1,0:T(8,128)(2,1)} custom-call(bf16[2,1536,1536]{2,1,0:T(8,128)(2,1)S(1)} %late_weights.1.refs_0_, bf16[1536,512]{1,0:T(8,128)(2,1)S(1)} %collective-permute-done.14.refs_1_, bf16[1536,512]{1,0:T(8,128)(2,1)S(1)} %collective-permute-done.21.refs_2_, f32[1536,512]{1,0:T(8,128)S(1)} %copy-done.8, ...), custom_call_target="tpu_custom_call", output_to_operand_aliasing={{}: (4, {})} | custom-call | flops 4831838208 | bytes 3145728 | tf_op jit(solution)/shard_map/late/pallas_call | solution.py:265
  491.6 11.9 %collective-permute-done.25.refs_1_ = bf16[1536,256]{1,0:T(8,128)(2,1)S(1)} collective-permute-done((bf16[1536,256]{1,0:T(8,128)(2,1)S(1)}, bf16[1536,256]{1,0:T(8,128)(2,1)S(1)}, u32[]{:S(2)}, u32[]{:S(2)}) %collective-permute-start.25) | collective-permute-done | bytes 786464 | tf_op jit(solution)/shard_map/ppermute | solution.py:283
  503.4 1.7 collective-permute-start.24
  505.2 1.7 late.18.refs_2_
  506.9 2.5 late.19.refs_3_
  509.4 14.0 %collective-permute-done.24.refs_1_ = bf16[1536,256]{1,0:T(8,128)(2,1)S(1)} collective-permute-done((bf16[1536,256]{1,0:T(8,128)(2,1)S(1)}, bf16[1536,256]{1,0:T(8,128)(2,1)S(1)}, u32[]{:S(2)}, u32[]{:S(2)}) %collective-permute-start.24) | collective-permute-done | bytes 786464 | tf_op jit(solution)/shard_map/ppermute | solution.py:283
  524.4 1.7 collective-permute-start.23
  526.1 1.7 late.20.refs_2_
  527.9 2.5 late.21.refs_3_
  530.3 2.8 collective-permute-done.23.refs_1_
  534.0 1.7 collective-permute-start.22
  536.4 1.5 late.23.refs_3_
  537.8 3.5 collective-permute-done.22.refs_1_
  542.8 1.5 late.25
  (79 shorter events, 7.9 us)
Async XLA Ops:
  1.6 14.2 %slice-start = ((s8[9437184]{0:T(1024)(128)(4,1)}), s8[4194304]{0:T(1024)(128)(4,1)S(1)}, s32[]{:S(2)}) async-start(s8[9437184]{0:T(1024)(128)(4,1)} %bitcast.26), calls=%async_computation | async-start | bytes 8388608
  3.3 12.5 %slice-start.1 = ((s8[9437184]{0:T(1024)(128)(4,1)}), s8[4194304]{0:T(1024)(128)(4,1)S(1)}, s32[]{:S(2)}) async-start(s8[9437184]{0:T(1024)(128)(4,1)} %bitcast.26), calls=%async_computation.1 | async-start | bytes 8388608
  5.5 10.3 %slice-start.2 = ((s8[9437184]{0:T(1024)(128)(4,1)}), s8[1048576]{0:T(1024)(128)(4,1)S(1)}, s32[]{:S(2)}) async-start(s8[9437184]{0:T(1024)(128)(4,1)} %bitcast.26), calls=%async_computation.2 | async-start | bytes 2097152
  5.6 148.0 %collective-permute-start = (bf16[3,1536,2048]{2,1,0:T(8,128)(2,1)}, bf16[3,1536,2048]{2,1,0:T(8,128)(2,1)}, u32[]{:S(2)}, u32[]{:S(2)}) collective-permute-start(bf16[3,1536,2048]{2,1,0:T(8,128)(2,1)} %refs_2_.13), channel_id=1, source_target_pairs={{0,1},{1,0},{2,3},{3,2},{4,5},{5,4},{6,7},{7,6}} | collective-permute-start | bytes 56623112 | tf_op jit(solution)/shard_map/ppermute | solution.py:283
  11.2 179.0 %collective-permute-start.8 = (bf16[1536,1536]{1,0:T(8,128)(2,1)}, bf16[1536,1536]{1,0:T(8,128)(2,1)}, u32[]{:S(2)}, u32[]{:S(2)}) collective-permute-start(bf16[1536,1536]{1,0:T(8,128)(2,1)} %slice_bitcast_fusion), channel_id=1, source_target_pairs={{0,4},{4,0},{1,5},{5,1},{2,6},{6,2},{3,7},{7,3}} | collective-permute-start | bytes 14155784 | tf_op jit(solution)/shard_map/ppermute | solution.py:283
  13.8 136.3 %collective-permute-start.3 = (bf16[512,3072]{1,0:T(8,128)(2,1)S(1)}, bf16[512,3072]{1,0:T(8,128)(2,1)S(1)}, u32[]{:S(2)}, u32[]{:S(2)}) collective-permute-start(bf16[512,3072]{1,0:T(8,128)(2,1)S(1)} %slice.50), channel_id=1, source_target_pairs={{0,2},{2,0},{1,3},{3,1},{4,6},{6,4},{5,7},{7,5}} | collective-permute-start | bytes 9437192 | tf_op jit(solution)/shard_map/ppermute | solution.py:283
  15.3 134.8 %collective-permute-start.9 = (bf16[1536,512]{1,0:T(8,128)(2,1)S(1)}, bf16[1536,512]{1,0:T(8,128)(2,1)S(1)}, u32[]{:S(2)}, u32[]{:S(2)}) collective-permute-start(bf16[1536,512]{1,0:T(8,128)(2,1)S(1)} %slice_bitcast_fusion.5), channel_id=1, source_target_pairs={{0,4},{4,0},{1,5},{5,1},{2,6},{6,2},{3,7},{7,3}} | collective-permute-start | bytes 4718600 | tf_op jit(solution)/shard_map/ppermute | solution.py:283
  19.0 157.8 %collective-permute-start.4 = (bf16[512,3072]{1,0:T(8,128)(2,1)}, bf16[512,3072]{1,0:T(8,128)(2,1)}, u32[]{:S(2)}, u32[]{:S(2)}) collective-permute-start(bf16[512,3072]{1,0:T(8,128)(2,1)} %get-tuple-element.160), channel_id=1, source_target_pairs={{0,2},{2,0},{1,3},{3,1},{4,6},{6,4},{5,7},{7,5}} | collective-permute-start | bytes 9437192 | tf_op jit(solution)/shard_map/ppermute | solution.py:283
  150.1 3.4 collective-permute-start.10
  150.1 10.9 %copy-start.3 = (bf16[512,3072]{1,0:T(8,128)(2,1)}, bf16[512,3072]{1,0:T(8,128)(2,1)S(1)}, u32[]{:S(2)}) copy-start(bf16[512,3072]{1,0:T(8,128)(2,1)S(1)} %collective-permute-done.3.refs_1_) | copy-start | bytes 9437188
  161.0 1.2 copy-start.11
  176.8 3.7 copy-start
  180.5 1.4 copy-start.12
  190.2 9.7 %collective-permute-start.11 = (bf16[1536,1536]{1,0:T(8,128)(2,1)}, bf16[1536,1536]{1,0:T(8,128)(2,1)S(1)}, u32[]{:S(2)}, u32[]{:S(2)}) collective-permute-start(bf16[1536,1536]{1,0:T(8,128)(2,1)} %collective-permute-done.8.refs_4_.refs_3_), channel_id=1, source_target_pairs={{0,1},{1,0},{2,3},{3,2},{4,5},{5,4},{6,7},{7,6}} | collective-permute-start | bytes 14155784 | tf_op jit(solution)/shard_map/ppermute | solution.py:283
  190.2 11.8 %copy-start.4 = (bf16[512,3072]{1,0:T(8,128)(2,1)S(1)}, bf16[512,3072]{1,0:T(8,128)(2,1)}, u32[]{:S(2)}) copy-start(bf16[512,3072]{1,0:T(8,128)(2,1)} %copy-done.3) | copy-start | bytes 9437188
  190.2 70.8 %collective-permute-start.5 = (bf16[512,3072]{1,0:T(8,128)(2,1)}, bf16[512,3072]{1,0:T(8,128)(2,1)}, u32[]{:S(2)}, u32[]{:S(2)}) collective-permute-start(bf16[512,3072]{1,0:T(8,128)(2,1)} %get-tuple-element.159), channel_id=1, source_target_pairs={{0,2},{2,0},{1,3},{3,1},{4,6},{6,4},{5,7},{7,5}} | collective-permute-start | bytes 9437192 | tf_op jit(solution)/shard_map/ppermute | solution.py:283
  198.3 94.2 %collective-permute-start.7 = (bf16[1536,1024]{1,0:T(8,128)(2,1)}, bf16[1536,1024]{1,0:T(8,128)(2,1)}, u32[]{:S(2)}, u32[]{:S(2)}) collective-permute-start(bf16[1536,1024]{1,0:T(8,128)(2,1)} %get-tuple-element.157), channel_id=1, source_target_pairs={{0,4},{4,0},{1,5},{5,1},{2,6},{6,2},{3,7},{7,3}} | collective-permute-start | bytes 9437192 | tf_op jit(solution)/shard_map/ppermute | solution.py:283
  199.8 2.2 copy-start.9
  261.0 3.7 copy-start.1
  264.7 1.4 copy-start.13
  266.1 8.5 %copy-start.10 = (bf16[1536,1536]{1,0:T(8,128)(2,1)S(1)}, bf16[1536,1536]{1,0:T(8,128)(2,1)}, u32[]{:S(2)}) copy-start(bf16[1536,1536]{1,0:T(8,128)(2,1)} %copy-done.9) | copy-start | bytes 14155780
  274.6 17.9 %copy-start.17 = (bf16[1536,1024]{1,0:T(8,128)(2,1)S(1)}, bf16[1536,1024]{1,0:T(8,128)(2,1)}, u32[]{:S(2)}) copy-start(bf16[1536,1024]{1,0:T(8,128)(2,1)} %get-tuple-element.158) | copy-start | bytes 9437188
  292.5 5.9 %collective-permute-start.12 = (bf16[1536,1024]{1,0:T(8,128)(2,1)}, bf16[1536,1024]{1,0:T(8,128)(2,1)S(1)}, u32[]{:S(2)}, u32[]{:S(2)}) collective-permute-start(bf16[1536,1024]{1,0:T(8,128)(2,1)} %collective-permute-done.7.refs_5_), channel_id=1, source_target_pairs={{0,1},{1,0},{2,3},{3,2},{4,5},{5,4},{6,7},{7,6}} | collective-permute-start | bytes 9437192 | tf_op jit(solution)/shard_map/ppermute | solution.py:283
  292.6 75.1 %copy-start.19 = (bf16[384,256]{1,0:T(8,128)(2,1)S(1)}, bf16[384,256]{1,0:T(8,128)(2,1)}, u32[]{:S(2)}) copy-start(bf16[384,256]{1,0:T(8,128)(2,1)} %slice_bitcast_fusion.12) | copy-start | bytes 589828
  292.6 70.5 %collective-permute-start.6 = (bf16[1536,1024]{1,0:T(8,128)(2,1)S(1)}, bf16[1536,1024]{1,0:T(8,128)(2,1)S(1)}, u32[]{:S(2)}, u32[]{:S(2)}) collective-permute-start(bf16[1536,1024]{1,0:T(8,128)(2,1)S(1)} %copy-done.17), channel_id=1, source_target_pairs={{0,4},{4,0},{1,5},{5,1},{2,6},{6,2},{3,7},{7,3}} | collective-permute-start | bytes 9437192 | tf_op jit(solution)/shard_map/ppermute | solution.py:283
  298.4 1.7 copy-start.16
  363.1 10.0 %copy-start.14 = (bf16[1536,1024]{1,0:T(8,128)(2,1)}, bf16[1536,1024]{1,0:T(8,128)(2,1)S(1)}, u32[]{:S(2)}) copy-start(bf16[1536,1024]{1,0:T(8,128)(2,1)S(1)} %collective-permute-done.6.refs_5_) | copy-start | bytes 9437188
  363.1 28.9 %collective-permute-start.13 = (bf16[1536,1024]{1,0:T(8,128)(2,1)S(1)}, bf16[1536,1024]{1,0:T(8,128)(2,1)S(1)}, u32[]{:S(2)}, u32[]{:S(2)}) collective-permute-start(bf16[1536,1024]{1,0:T(8,128)(2,1)S(1)} %collective-permute-done.6.refs_5_), channel_id=1, source_target_pairs={{0,1},{1,0},{2,3},{3,2},{4,5},{5,4},{6,7},{7,6}} | collective-permute-start | bytes 9437192 | tf_op jit(solution)/shard_map/ppermute | solution.py:283
  364.5 58.0 %collective-permute-start.2 = (bf16[1024,256]{1,0:T(8,128)(2,1)S(1)}, bf16[1024,256]{1,0:T(8,128)(2,1)S(1)}, u32[]{:S(2)}, u32[]{:S(2)}) collective-permute-start(bf16[1024,256]{1,0:T(8,128)(2,1)S(1)} %slice_bitcast_fusion.8), channel_id=1, source_target_pairs={{0,4},{4,0},{1,5},{5,1},{2,6},{6,2},{3,7},{7,3}} | collective-permute-start | bytes 1572872 | tf_op jit(solution)/shard_map/ppermute | solution.py:283
  367.3 55.2 %collective-permute-start.1 = (bf16[768,256]{1,0:T(8,128)(2,1)S(1)}, bf16[768,256]{1,0:T(8,128)(2,1)S(1)}, u32[]{:S(2)}, u32[]{:S(2)}) collective-permute-start(bf16[768,256]{1,0:T(8,128)(2,1)S(1)} %slice_bitcast_fusion.9), channel_id=1, source_target_pairs={{0,4},{4,0},{1,5},{5,1},{2,6},{6,2},{3,7},{7,3}} | collective-permute-start | bytes 1179656 | tf_op jit(solution)/shard_map/ppermute | solution.py:283
  367.6 24.4 %collective-permute-start.16 = (bf16[384,256]{1,0:T(8,128)(2,1)S(1)}, bf16[384,256]{1,0:T(8,128)(2,1)S(1)}, u32[]{:S(2)}, u32[]{:S(2)}) collective-permute-start(bf16[384,256]{1,0:T(8,128)(2,1)S(1)} %copy-done.19), channel_id=1, source_target_pairs={{0,4},{4,0},{1,5},{5,1},{2,6},{6,2},{3,7},{7,3}} | collective-permute-start | bytes 589832 | tf_op jit(solution)/shard_map/ppermute | solution.py:283
  373.1 72.0 %collective-permute-start.15 = (bf16[1536,512]{1,0:T(8,128)(2,1)}, bf16[1536,512]{1,0:T(8,128)(2,1)S(1)}, u32[]{:S(2)}, u32[]{:S(2)}) collective-permute-start(bf16[1536,512]{1,0:T(8,128)(2,1)} %get-tuple-element.155), channel_id=1, source_target_pairs={{0,4},{4,0},{1,5},{5,1},{2,6},{6,2},{3,7},{7,3}} | collective-permute-start | bytes 4718600 | tf_op jit(solution)/shard_map/ppermute | solution.py:283
  392.0 51.8 %collective-permute-start.17 = (bf16[384,256]{1,0:T(8,128)(2,1)S(1)}, bf16[384,256]{1,0:T(8,128)(2,1)S(1)}, u32[]{:S(2)}, u32[]{:S(2)}) collective-permute-start(bf16[384,256]{1,0:T(8,128)(2,1)S(1)} %collective-permute-done.16.refs_1_), channel_id=1, source_target_pairs={{0,1},{1,0},{2,3},{3,2},{4,5},{5,4},{6,7},{7,6}} | collective-permute-start | bytes 589832 | tf_op jit(solution)/shard_map/ppermute | solution.py:283
  392.0 1.7 copy-start.15
  437.2 3.7 copy-start.2
  440.9 2.9 copy-start.6
  443.8 1.4 copy-start.18
  445.1 8.6 %collective-permute-start.18 = (bf16[1536,512]{1,0:T(8,128)(2,1)S(1)}, bf16[1536,512]{1,0:T(8,128)(2,1)S(1)}, u32[]{:S(2)}, u32[]{:S(2)}) collective-permute-start(bf16[1536,512]{1,0:T(8,128)(2,1)S(1)} %collective-permute-done.15.refs_1_), channel_id=1, source_target_pairs={{0,1},{1,0},{2,3},{3,2},{4,5},{5,4},{6,7},{7,6}} | collective-permute-start | bytes 4718600 | tf_op jit(solution)/shard_map/ppermute | solution.py:283
  445.2 36.8 %collective-permute-start.14 = (bf16[1536,512]{1,0:T(8,128)(2,1)S(1)}, bf16[1536,512]{1,0:T(8,128)(2,1)S(1)}, u32[]{:S(2)}, u32[]{:S(2)}) collective-permute-start(bf16[1536,512]{1,0:T(8,128)(2,1)S(1)} %copy-done.18), channel_id=1, source_target_pairs={{0,4},{4,0},{1,5},{5,1},{2,6},{6,2},{3,7},{7,3}} | collective-permute-start | bytes 4718600 | tf_op jit(solution)/shard_map/ppermute | solution.py:283
  446.9 4.7 collective-permute-start.19
  447.1 2.8 collective-permute-start.20
  451.6 2.2 copy-start.7
  460.0 25.4 %copy-start.8 = (f32[1536,512]{1,0:T(8,128)S(1)}, f32[1536,512]{1,0:T(8,128)}, u32[]{:S(2)}) copy-start(f32[1536,512]{1,0:T(8,128)} %get-tuple-element.138.refs_3_) | copy-start | bytes 9437188
  481.9 3.4 collective-permute-start.21
  483.4 21.7 %copy-start.5 = (f32[1536,512]{1,0:T(8,128)S(1)}, f32[1536,512]{1,0:T(8,128)}, u32[]{:S(2)}) copy-start(f32[1536,512]{1,0:T(8,128)} %get-tuple-element.143.refs_2_) | copy-start | bytes 9437188
  483.5 20.0 %collective-permute-start.25 = (bf16[1536,256]{1,0:T(8,128)(2,1)S(1)}, bf16[1536,256]{1,0:T(8,128)(2,1)S(1)}, u32[]{:S(2)}, u32[]{:S(2)}) collective-permute-start(bf16[1536,256]{1,0:T(8,128)(2,1)S(1)} %get-tuple-element.153), channel_id=1, source_target_pairs={{0,4},{4,0},{1,5},{5,1},{2,6},{6,2},{3,7},{7,3}} | collective-permute-start | bytes 2359304 | tf_op jit(solution)/shard_map/ppermute | solution.py:283
  503.4 3.5 collective-permute-start.26
  503.4 20.0 %collective-permute-start.24 = (bf16[1536,256]{1,0:T(8,128)(2,1)S(1)}, bf16[1536,256]{1,0:T(8,128)(2,1)S(1)}, u32[]{:S(2)}, u32[]{:S(2)}) collective-permute-start(bf16[1536,256]{1,0:T(8,128)(2,1)S(1)} %get-tuple-element.154), channel_id=1, source_target_pairs={{0,4},{4,0},{1,5},{5,1},{2,6},{6,2},{3,7},{7,3}} | collective-permute-start | bytes 2359304 | tf_op jit(solution)/shard_map/ppermute | solution.py:283
  523.4 4.5 collective-permute-start.27
  524.4 8.7 %collective-permute-start.23 = (bf16[512,256]{1,0:T(8,128)(2,1)S(1)}, bf16[512,256]{1,0:T(8,128)(2,1)S(1)}, u32[]{:S(2)}, u32[]{:S(2)}) collective-permute-start(bf16[512,256]{1,0:T(8,128)(2,1)S(1)} %slice_bitcast_fusion.10), channel_id=1, source_target_pairs={{0,4},{4,0},{1,5},{5,1},{2,6},{6,2},{3,7},{7,3}} | collective-permute-start | bytes 786440 | tf_op jit(solution)/shard_map/ppermute | solution.py:283
  533.1 3.3 collective-permute-start.28
  534.0 7.3 %collective-permute-start.22 = (bf16[384,256]{1,0:T(8,128)(2,1)S(1)}, bf16[384,256]{1,0:T(8,128)(2,1)S(1)}, u32[]{:S(2)}, u32[]{:S(2)}) collective-permute-start(bf16[384,256]{1,0:T(8,128)(2,1)S(1)} %slice_bitcast_fusion.11), channel_id=1, source_target_pairs={{0,4},{4,0},{1,5},{5,1},{2,6},{6,2},{3,7},{7,3}} | collective-permute-start | bytes 589832 | tf_op jit(solution)/shard_map/ppermute | solution.py:283
  541.4 1.4 collective-permute-start.29

commit v5 on v4

--- a/solution.py
+++ b/solution.py
@@ -92,6 +92,8 @@
     groups = [(0, col, side) for col in range(col_tiles) for side in range(2)]
     groups += [(tile, 0, side) for tile in range(1, n_tiles) for side in range(2)]
 
+    ahead = len(groups)
+
     def group_start(index):
         if index < len(groups):
             tile, col, side = groups[index]
@@ -118,9 +120,8 @@
                     if index == 0:
                         group_start(0)
                     group_wait(index)
-                    if index == 0:
-                        group_start(1)
-                    group_start(index + 2)
+                    for later in range(index + ahead if index else 1, index + ahead + 1):
+                        group_start(later)
 
         x_side = x_all[pl.ds(side * n_layers, n_layers), :, col_range].reshape(n_layers * k_rows, tile_cols)
         term = jnp.dot(a_all[side, row_range], x_side, preferred_element_type=jnp.float32)

time: 545 us -> 549 us (level)
  transfers between devices with their start and end apart: 30 -> 30, of which waited for: 14 -> 14; matrix products, arithmetic and copies ran while one was open for 4% -> 4% of each run, Pallas kernels for 37% -> 38%
where the time goes in v5:
time: 549 us
  waiting for transfers between devices  264 us (48%)
  Pallas kernels  210 us (38%)
  local copies, waits for them, and re-layouts  50.1 us (9%)
  starting transfers between devices  23.9 us (4%)
    ppermute x30, waiting for transfers between devices, permute(): return lax.ppermute(value, axis, SWAP)  264 us
    pallas_call x10, Pallas kernels, product(): pl.pallas_call(functools.partial(product_kernel, plan), grid=(len(tiles),...  177 us
    pallas_call x13, Pallas kernels, late_product(): pl.pallas_call(functools.partial(late_kernel, k_start, base_start, target...  30 us
    squeeze x10, local copies, waits for them, and re-layouts, piece_of(): return x[rhs_idx, k_start:k_start + k_rows, start:start + width]  23.9 us
    ppermute x30, starting transfers between devices, permute(): return lax.ppermute(value, axis, SWAP)  23.9 us
    unnamed x46, local copies, waits for them, and re-layouts  20.6 us
  transfers between devices with their start and end apart: 30, of which 14 were waited for; matrix products, arithmetic and copies ran while one was open for 4% of the time, Pallas kernels for 38%

profile of v5, /device:TPU:0, one launch (start us, length us, event | category | flops | bytes accessed | tf_op | source)
XLA Modules:
  0.0 548.5 jit_solution(13136732897918259677)
XLA Ops:
  0.0 1.6 slice_bitcast_fusion.12
  1.6 1.7 slice_bitcast_fusion.5
  3.3 2.2 slice.50
  6.4 4.8 slice_bitcast_fusion
  11.2 2.6 collective-permute-start.8
  13.8 1.5 collective-permute-start.3
  15.8 3.2 fusion
  19.1 131.0 %collective-permute-done.9.refs_3_ = bf16[1536,512]{1,0:T(8,128)(2,1)S(1)} collective-permute-done((bf16[1536,512]{1,0:T(8,128)(2,1)S(1)}, bf16[1536,512]{1,0:T(8,128)(2,1)S(1)}, u32[]{:S(2)}, u32[]{:S(2)}) %collective-permute-start.9) | collective-permute-done | bytes 1572896 | tf_op jit(solution)/shard_map/ppermute | solution.py:284
  150.1 3.4 collective-permute-done.10.refs_5_
  153.5 7.5 %product.10.refs_6_ = bf16[3,1536,2048]{2,1,0:T(8,128)(2,1)} custom-call(bf16[1536,3072]{1,0:T(8,128)(2,1)S(1)} %bitcast.27, bf16[512,3072]{1,0:T(8,128)(2,1)S(1)} %collective-permute-done.3.refs_1_, bf16[3,1536,2048]{2,1,0:T(8,128)(2,1)} %refs_2_.13, bf16[1536,512]{1,0:T(8,128)(2,1)S(1)} %collective-permute-done.9.refs_3_, ...), custom_call_target="tpu_custom_call" | custom-call | flops 3221225472 | bytes 6291456 | tf_op jit(solution)/shard_map/product/pallas_call | solution.py:165
  161.0 1.2 copy-done.11
  162.2 16.4 %product.11 = (f32[1536,512]{1,0:T(8,128)}, f32[1536,512]{1,0:T(8,128)}, f32[1536,512]{1,0:T(8,128)}, f32[1536,512]{1,0:T(8,128)}) custom-call(bf16[1536,3072]{1,0:T(8,128)(2,1)} %refs_0_.20, bf16[512,3072]{1,0:T(8,128)(2,1)} %copy-done.3, bf16[3,1536,2048]{2,1,0:T(8,128)(2,1)} %refs_2_.13, ...), custom_call_target="tpu_custom_call" | custom-call | flops 6442450944 | bytes 6291456 | tf_op jit(solution)/shard_map/product/pallas_call | solution.py:165
  178.6 3.7 copy-done
  182.3 1.4 copy-done.12
  183.7 8.2 %product.12.refs_7_ = bf16[3,1536,2048]{2,1,0:T(8,128)(2,1)} custom-call(bf16[1536,3072]{1,0:T(8,128)(2,1)S(1)} %copy-done, bf16[512,3072]{1,0:T(8,128)(2,1)} %collective-permute-done.4.refs_1_.refs_2_, bf16[3,1536,2048]{2,1,0:T(8,128)(2,1)} %refs_2_.13, bf16[1536,512]{1,0:T(8,128)(2,1)S(1)} %collective-permute-done.9.refs_3_, ...), custom_call_target="tpu_custom_call", output_to_operand_aliasing={{}: (6, {})} | custom-call | flops 3221225472 | bytes 6291456 | tf_op jit(solution)/shard_map/product/pallas_call | solution.py:165
  192.6 1.6 collective-permute-start.5
  194.2 6.3 %slice_bitcast_fusion.1 = (bf16[1536,1024]{1,0:T(8,128)(2,1)}, bf16[1536,1024]{1,0:T(8,128)(2,1)}) fusion(bf16[3,1536,2048]{2,1,0:T(8,128)(2,1)} %refs_2_.13), kind=kLoop, calls=%fused_computation.1 | loop fusion | bytes 12582912 | tf_op jit(solution)/shard_map/squeeze | solution.py:293
  200.5 1.5 collective-permute-start.7
  202.0 2.2 copy-done.9
  204.1 28.6 %product.13.refs_6_ = bf16[3,1536,2048]{2,1,0:T(8,128)(2,1)} custom-call(bf16[1536,3072]{1,0:T(8,128)(2,1)} %refs_0_.20, bf16[512,3072]{1,0:T(8,128)(2,1)S(1)} %copy-done.4, bf16[512,3072]{1,0:T(8,128)(2,1)} %collective-permute-done.4.refs_1_.refs_2_, bf16[3,1536,2048]{2,1,0:T(8,128)(2,1)} %refs_2_.13, ...), custom_call_target="tpu_custom_call", output_to_operand_aliasing={{}: (7, {})} | custom-call | flops 19327352832 | bytes 12582912 | tf_op jit(solution)/shard_map/product/pallas_call | solution.py:165
  232.7 16.5 %product.14 = (f32[1536,512]{1,0:T(8,128)}, f32[1536,512]{1,0:T(8,128)}, f32[1536,512]{1,0:T(8,128)}, f32[1536,512]{1,0:T(8,128)}) custom-call(bf16[1536,3072]{1,0:T(8,128)(2,1)} %refs_0_.20, bf16[512,3072]{1,0:T(8,128)(2,1)} %collective-permute-done.4.refs_1_.refs_2_, ...), custom_call_target="tpu_custom_call", output_to_operand_aliasing={{0}: (4, {}), {1}: (5, {}), {2}: (6, {}), {3}: (7, {})} | custom-call | flops 6442450944 | bytes 6291456 | tf_op jit(solution)/shard_map/product/pallas_call | solution.py:165
  249.2 14.0 %collective-permute-done.5.refs_1_.refs_3_ = bf16[512,3072]{1,0:T(8,128)(2,1)} collective-permute-done((bf16[512,3072]{1,0:T(8,128)(2,1)}, bf16[512,3072]{1,0:T(8,128)(2,1)}, u32[]{:S(2)}, u32[]{:S(2)}) %collective-permute-start.5) | collective-permute-done | bytes 3145760 | tf_op jit(solution)/shard_map/ppermute | solution.py:284
  263.2 3.7 copy-done.1
  266.9 1.4 copy-done.13
  268.3 8.5 %product.15.refs_6_ = bf16[3,1536,2048]{2,1,0:T(8,128)(2,1)} custom-call(bf16[1536,3072]{1,0:T(8,128)(2,1)S(1)} %copy-done.1, bf16[512,3072]{1,0:T(8,128)(2,1)} %collective-permute-done.5.refs_1_.refs_3_, bf16[3,1536,2048]{2,1,0:T(8,128)(2,1)} %refs_2_.13, bf16[1536,512]{1,0:T(8,128)(2,1)S(1)} %collective-permute-done.9.refs_3_, ...), custom_call_target="tpu_custom_call", output_to_operand_aliasing={{}: (6, {})} | custom-call | flops 3221225472 | bytes 6291456 | tf_op jit(solution)/shard_map/product/pallas_call | solution.py:165
  276.8 17.6 %product.16.refs_8_ = bf16[3,1536,2048]{2,1,0:T(8,128)(2,1)} custom-call(bf16[1536,3072]{1,0:T(8,128)(2,1)} %refs_0_.20, bf16[512,3072]{1,0:T(8,128)(2,1)} %collective-permute-done.5.refs_1_.refs_3_, bf16[3,1536,2048]{2,1,0:T(8,128)(2,1)} %refs_2_.13, bf16[1536,1536]{1,0:T(8,128)(2,1)} %collective-permute-done.8.refs_4_.refs_3_, ...), custom_call_target="tpu_custom_call", output_to_operand_aliasing={{}: (6, {})} | custom-call | flops 9663676416 | bytes 6291456 | tf_op jit(solution)/shard_map/product/pallas_call | solution.py:165
  294.5 1.5 collective-permute-start.6
  296.1 4.3 collective-permute-done.12.refs_7_
  300.4 1.7 copy-done.16
  302.1 28.6 %product.17.refs_8_ = bf16[3,1536,2048]{2,1,0:T(8,128)(2,1)} custom-call(bf16[1536,3072]{1,0:T(8,128)(2,1)} %refs_0_.20, bf16[512,3072]{1,0:T(8,128)(2,1)S(1)} %copy-done.4, bf16[512,3072]{1,0:T(8,128)(2,1)} %collective-permute-done.4.refs_1_.refs_2_, bf16[512,3072]{1,0:T(8,128)(2,1)} %collective-permute-done.5.refs_1_.refs_3_, ...), custom_call_target="tpu_custom_call", output_to_operand_aliasing={{}: (8, {})} | custom-call | flops 19327352832 | bytes 18874368 | tf_op jit(solution)/shard_map/product/pallas_call | solution.py:165
  330.7 34.3 %collective-permute-done.6.refs_5_ = bf16[1536,1024]{1,0:T(8,128)(2,1)S(1)} collective-permute-done((bf16[1536,1024]{1,0:T(8,128)(2,1)S(1)}, bf16[1536,1024]{1,0:T(8,128)(2,1)S(1)}, u32[]{:S(2)}, u32[]{:S(2)}) %collective-permute-start.6) | collective-permute-done | bytes 3145760 | tf_op jit(solution)/shard_map/ppermute | solution.py:284
  365.0 1.5 slice_bitcast_fusion.8
  366.5 1.5 collective-permute-start.2
  369.6 1.5 collective-permute-start.16
  371.1 3.7 slice_bitcast_fusion.3
  375.3 18.6 %collective-permute-done.16.refs_1_ = bf16[384,256]{1,0:T(8,128)(2,1)S(1)} collective-permute-done((bf16[384,256]{1,0:T(8,128)(2,1)S(1)}, bf16[384,256]{1,0:T(8,128)(2,1)S(1)}, u32[]{:S(2)}, u32[]{:S(2)}) %collective-permute-start.16) | collective-permute-done | bytes 196640 | tf_op jit(solution)/shard_map/ppermute | solution.py:284
  393.9 1.7 copy-done.15
  395.6 28.6 %product.18.refs_4_ = bf16[3,1536,2048]{2,1,0:T(8,128)(2,1)} custom-call(bf16[1536,3072]{1,0:T(8,128)(2,1)} %refs_0_.20, bf16[512,3072]{1,0:T(8,128)(2,1)S(1)} %copy-done.4, bf16[512,3072]{1,0:T(8,128)(2,1)} %collective-permute-done.4.refs_1_.refs_2_, bf16[512,3072]{1,0:T(8,128)(2,1)} %collective-permute-done.5.refs_1_.refs_3_, ...), custom_call_target="tpu_custom_call", output_to_operand_aliasing={{}: (8, {})} | custom-call | flops 19327352832 | bytes 18874368 | tf_op jit(solution)/shard_map/product/pallas_call | solution.py:165
  424.3 16.4 %product.19 = (f32[1536,512]{1,0:T(8,128)}, f32[1536,512]{1,0:T(8,128)}, f32[1536,512]{1,0:T(8,128)}, f32[1536,512]{1,0:T(8,128)}) custom-call(bf16[1536,3072]{1,0:T(8,128)(2,1)} %refs_0_.20, bf16[512,3072]{1,0:T(8,128)(2,1)} %collective-permute-done.5.refs_1_.refs_3_, ...), custom_call_target="tpu_custom_call", output_to_operand_aliasing={{0}: (4, {}), {1}: (5, {}), {2}: (6, {}), {3}: (7, {})} | custom-call | flops 6442450944 | bytes 6291456 | tf_op jit(solution)/shard_map/product/pallas_call | solution.py:165
  440.8 3.7 copy-done.2
  444.5 2.9 late_weights.1.refs_0_
  447.4 1.3 late.13.refs_3_
  449.6 1.5 collective-permute-start.14
  451.6 2.3 collective-permute-done.20.refs_2_
  454.0 1.7 late.16.refs_2_
  455.7 2.1 late.15.refs_2_
  457.9 6.2 %late.14.refs_4_ = bf16[3,1536,2048]{2,1,0:T(8,128)(2,1)} custom-call(bf16[2,1536,1536]{2,1,0:T(8,128)(2,1)S(1)} %late_weights.1.refs_0_, bf16[1536,512]{1,0:T(8,128)(2,1)S(1)} %collective-permute-done.15.refs_1_, bf16[1536,512]{1,0:T(8,128)(2,1)S(1)} %collective-permute-done.18.refs_2_, f32[1536,512]{1,0:T(8,128)S(1)} %copy-done.7, ...), custom_call_target="tpu_custom_call", output_to_operand_aliasing={{}: (4, {})} | custom-call | flops 4831838208 | bytes 3145728 | tf_op jit(solution)/shard_map/late/pallas_call | solution.py:266
  464.1 21.9 %collective-permute-done.14.refs_1_ = bf16[1536,512]{1,0:T(8,128)(2,1)S(1)} collective-permute-done((bf16[1536,512]{1,0:T(8,128)(2,1)S(1)}, bf16[1536,512]{1,0:T(8,128)(2,1)S(1)}, u32[]{:S(2)}, u32[]{:S(2)}) %collective-permute-start.14) | collective-permute-done | bytes 1572896 | tf_op jit(solution)/shard_map/ppermute | solution.py:284
  486.0 1.5 slice_bitcast_fusion.6
  487.5 1.5 collective-permute-start.25
  489.4 6.2 %late.17.refs_3_ = bf16[3,1536,2048]{2,1,0:T(8,128)(2,1)} custom-call(bf16[2,1536,1536]{2,1,0:T(8,128)(2,1)S(1)} %late_weights.1.refs_0_, bf16[1536,512]{1,0:T(8,128)(2,1)S(1)} %collective-permute-done.14.refs_1_, bf16[1536,512]{1,0:T(8,128)(2,1)S(1)} %collective-permute-done.21.refs_2_, f32[1536,512]{1,0:T(8,128)S(1)} %copy-done.8, ...), custom_call_target="tpu_custom_call", output_to_operand_aliasing={{}: (4, {})} | custom-call | flops 4831838208 | bytes 3145728 | tf_op jit(solution)/shard_map/late/pallas_call | solution.py:266
  495.6 11.9 %collective-permute-done.25.refs_1_ = bf16[1536,256]{1,0:T(8,128)(2,1)S(1)} collective-permute-done((bf16[1536,256]{1,0:T(8,128)(2,1)S(1)}, bf16[1536,256]{1,0:T(8,128)(2,1)S(1)}, u32[]{:S(2)}, u32[]{:S(2)}) %collective-permute-start.25) | collective-permute-done | bytes 786464 | tf_op jit(solution)/shard_map/ppermute | solution.py:284
  507.5 1.5 collective-permute-start.24
  509.0 1.7 late.18.refs_2_
  510.7 2.5 late.19.refs_3_
  513.2 14.2 %collective-permute-done.24.refs_1_ = bf16[1536,256]{1,0:T(8,128)(2,1)S(1)} collective-permute-done((bf16[1536,256]{1,0:T(8,128)(2,1)S(1)}, bf16[1536,256]{1,0:T(8,128)(2,1)S(1)}, u32[]{:S(2)}, u32[]{:S(2)}) %collective-permute-start.24) | collective-permute-done | bytes 786464 | tf_op jit(solution)/shard_map/ppermute | solution.py:284
  528.4 1.5 collective-permute-start.23
  529.9 1.7 late.20.refs_2_
  531.7 2.5 late.21.refs_3_
  534.1 3.0 collective-permute-done.23.refs_1_
  538.1 1.5 collective-permute-start.22
  540.2 1.5 late.23.refs_3_
  541.7 3.8 collective-permute-done.22.refs_1_
  546.9 1.5 late.25
  (79 shorter events, 10.1 us)
Async XLA Ops:
  1.6 14.2 %slice-start = ((s8[9437184]{0:T(1024)(128)(4,1)}), s8[4194304]{0:T(1024)(128)(4,1)S(1)}, s32[]{:S(2)}) async-start(s8[9437184]{0:T(1024)(128)(4,1)} %bitcast.26), calls=%async_computation | async-start | bytes 8388608
  3.3 12.5 %slice-start.1 = ((s8[9437184]{0:T(1024)(128)(4,1)}), s8[4194304]{0:T(1024)(128)(4,1)S(1)}, s32[]{:S(2)}) async-start(s8[9437184]{0:T(1024)(128)(4,1)} %bitcast.26), calls=%async_computation.1 | async-start | bytes 8388608
  5.5 10.3 %slice-start.2 = ((s8[9437184]{0:T(1024)(128)(4,1)}), s8[1048576]{0:T(1024)(128)(4,1)S(1)}, s32[]{:S(2)}) async-start(s8[9437184]{0:T(1024)(128)(4,1)} %bitcast.26), calls=%async_computation.2 | async-start | bytes 2097152
  5.6 148.0 %collective-permute-start = (bf16[3,1536,2048]{2,1,0:T(8,128)(2,1)}, bf16[3,1536,2048]{2,1,0:T(8,128)(2,1)}, u32[]{:S(2)}, u32[]{:S(2)}) collective-permute-start(bf16[3,1536,2048]{2,1,0:T(8,128)(2,1)} %refs_2_.13), channel_id=1, source_target_pairs={{0,1},{1,0},{2,3},{3,2},{4,5},{5,4},{6,7},{7,6}} | collective-permute-start | bytes 56623112 | tf_op jit(solution)/shard_map/ppermute | solution.py:284
  11.2 180.7 %collective-permute-start.8 = (bf16[1536,1536]{1,0:T(8,128)(2,1)}, bf16[1536,1536]{1,0:T(8,128)(2,1)}, u32[]{:S(2)}, u32[]{:S(2)}) collective-permute-start(bf16[1536,1536]{1,0:T(8,128)(2,1)} %slice_bitcast_fusion), channel_id=1, source_target_pairs={{0,4},{4,0},{1,5},{5,1},{2,6},{6,2},{3,7},{7,3}} | collective-permute-start | bytes 14155784 | tf_op jit(solution)/shard_map/ppermute | solution.py:284
  13.8 136.3 %collective-permute-start.3 = (bf16[512,3072]{1,0:T(8,128)(2,1)S(1)}, bf16[512,3072]{1,0:T(8,128)(2,1)S(1)}, u32[]{:S(2)}, u32[]{:S(2)}) collective-permute-start(bf16[512,3072]{1,0:T(8,128)(2,1)S(1)} %slice.50), channel_id=1, source_target_pairs={{0,2},{2,0},{1,3},{3,1},{4,6},{6,4},{5,7},{7,5}} | collective-permute-start | bytes 9437192 | tf_op jit(solution)/shard_map/ppermute | solution.py:284
  15.3 134.8 %collective-permute-start.9 = (bf16[1536,512]{1,0:T(8,128)(2,1)S(1)}, bf16[1536,512]{1,0:T(8,128)(2,1)S(1)}, u32[]{:S(2)}, u32[]{:S(2)}) collective-permute-start(bf16[1536,512]{1,0:T(8,128)(2,1)S(1)} %slice_bitcast_fusion.5), channel_id=1, source_target_pairs={{0,4},{4,0},{1,5},{5,1},{2,6},{6,2},{3,7},{7,3}} | collective-permute-start | bytes 4718600 | tf_op jit(solution)/shard_map/ppermute | solution.py:284
  19.0 159.6 %collective-permute-start.4 = (bf16[512,3072]{1,0:T(8,128)(2,1)}, bf16[512,3072]{1,0:T(8,128)(2,1)}, u32[]{:S(2)}, u32[]{:S(2)}) collective-permute-start(bf16[512,3072]{1,0:T(8,128)(2,1)} %get-tuple-element.160), channel_id=1, source_target_pairs={{0,2},{2,0},{1,3},{3,1},{4,6},{6,4},{5,7},{7,5}} | collective-permute-start | bytes 9437192 | tf_op jit(solution)/shard_map/ppermute | solution.py:284
  150.1 3.4 collective-permute-start.10
  150.1 10.9 %copy-start.3 = (bf16[512,3072]{1,0:T(8,128)(2,1)}, bf16[512,3072]{1,0:T(8,128)(2,1)S(1)}, u32[]{:S(2)}) copy-start(bf16[512,3072]{1,0:T(8,128)(2,1)S(1)} %collective-permute-done.3.refs_1_) | copy-start | bytes 9437188
  161.0 1.2 copy-start.11
  178.6 3.7 copy-start
  182.3 1.4 copy-start.12
  191.9 10.0 %collective-permute-start.11 = (bf16[1536,1536]{1,0:T(8,128)(2,1)}, bf16[1536,1536]{1,0:T(8,128)(2,1)S(1)}, u32[]{:S(2)}, u32[]{:S(2)}) collective-permute-start(bf16[1536,1536]{1,0:T(8,128)(2,1)} %collective-permute-done.8.refs_4_.refs_3_), channel_id=1, source_target_pairs={{0,1},{1,0},{2,3},{3,2},{4,5},{5,4},{6,7},{7,6}} | collective-permute-start | bytes 14155784 | tf_op jit(solution)/shard_map/ppermute | solution.py:284
  192.6 11.6 %copy-start.4 = (bf16[512,3072]{1,0:T(8,128)(2,1)S(1)}, bf16[512,3072]{1,0:T(8,128)(2,1)}, u32[]{:S(2)}) copy-start(bf16[512,3072]{1,0:T(8,128)(2,1)} %copy-done.3) | copy-start | bytes 9437188
  192.6 70.7 %collective-permute-start.5 = (bf16[512,3072]{1,0:T(8,128)(2,1)}, bf16[512,3072]{1,0:T(8,128)(2,1)}, u32[]{:S(2)}, u32[]{:S(2)}) collective-permute-start(bf16[512,3072]{1,0:T(8,128)(2,1)} %get-tuple-element.159), channel_id=1, source_target_pairs={{0,2},{2,0},{1,3},{3,1},{4,6},{6,4},{5,7},{7,5}} | collective-permute-start | bytes 9437192 | tf_op jit(solution)/shard_map/ppermute | solution.py:284
  200.5 94.0 %collective-permute-start.7 = (bf16[1536,1024]{1,0:T(8,128)(2,1)}, bf16[1536,1024]{1,0:T(8,128)(2,1)}, u32[]{:S(2)}, u32[]{:S(2)}) collective-permute-start(bf16[1536,1024]{1,0:T(8,128)(2,1)} %get-tuple-element.157), channel_id=1, source_target_pairs={{0,4},{4,0},{1,5},{5,1},{2,6},{6,2},{3,7},{7,3}} | collective-permute-start | bytes 9437192 | tf_op jit(solution)/shard_map/ppermute | solution.py:284
  202.0 2.2 copy-start.9
  263.2 3.7 copy-start.1
  266.9 1.4 copy-start.13
  268.3 8.5 %copy-start.10 = (bf16[1536,1536]{1,0:T(8,128)(2,1)S(1)}, bf16[1536,1536]{1,0:T(8,128)(2,1)}, u32[]{:S(2)}) copy-start(bf16[1536,1536]{1,0:T(8,128)(2,1)} %copy-done.9) | copy-start | bytes 14155780
  276.8 17.7 %copy-start.17 = (bf16[1536,1024]{1,0:T(8,128)(2,1)S(1)}, bf16[1536,1024]{1,0:T(8,128)(2,1)}, u32[]{:S(2)}) copy-start(bf16[1536,1024]{1,0:T(8,128)(2,1)} %get-tuple-element.158) | copy-start | bytes 9437188
  294.5 5.9 %collective-permute-start.12 = (bf16[1536,1024]{1,0:T(8,128)(2,1)}, bf16[1536,1024]{1,0:T(8,128)(2,1)S(1)}, u32[]{:S(2)}, u32[]{:S(2)}) collective-permute-start(bf16[1536,1024]{1,0:T(8,128)(2,1)} %collective-permute-done.7.refs_5_), channel_id=1, source_target_pairs={{0,1},{1,0},{2,3},{3,2},{4,5},{5,4},{6,7},{7,6}} | collective-permute-start | bytes 9437192 | tf_op jit(solution)/shard_map/ppermute | solution.py:284
  294.5 75.1 %copy-start.19 = (bf16[384,256]{1,0:T(8,128)(2,1)S(1)}, bf16[384,256]{1,0:T(8,128)(2,1)}, u32[]{:S(2)}) copy-start(bf16[384,256]{1,0:T(8,128)(2,1)} %slice_bitcast_fusion.12) | copy-start | bytes 589828
  294.5 70.5 %collective-permute-start.6 = (bf16[1536,1024]{1,0:T(8,128)(2,1)S(1)}, bf16[1536,1024]{1,0:T(8,128)(2,1)S(1)}, u32[]{:S(2)}, u32[]{:S(2)}) collective-permute-start(bf16[1536,1024]{1,0:T(8,128)(2,1)S(1)} %copy-done.17), channel_id=1, source_target_pairs={{0,4},{4,0},{1,5},{5,1},{2,6},{6,2},{3,7},{7,3}} | collective-permute-start | bytes 9437192 | tf_op jit(solution)/shard_map/ppermute | solution.py:284
  300.4 1.7 copy-start.16
  365.0 9.8 %copy-start.14 = (bf16[1536,1024]{1,0:T(8,128)(2,1)}, bf16[1536,1024]{1,0:T(8,128)(2,1)S(1)}, u32[]{:S(2)}) copy-start(bf16[1536,1024]{1,0:T(8,128)(2,1)S(1)} %collective-permute-done.6.refs_5_) | copy-start | bytes 9437188
  365.0 28.9 %collective-permute-start.13 = (bf16[1536,1024]{1,0:T(8,128)(2,1)S(1)}, bf16[1536,1024]{1,0:T(8,128)(2,1)S(1)}, u32[]{:S(2)}, u32[]{:S(2)}) collective-permute-start(bf16[1536,1024]{1,0:T(8,128)(2,1)S(1)} %collective-permute-done.6.refs_5_), channel_id=1, source_target_pairs={{0,1},{1,0},{2,3},{3,2},{4,5},{5,4},{6,7},{7,6}} | collective-permute-start | bytes 9437192 | tf_op jit(solution)/shard_map/ppermute | solution.py:284
  366.5 57.8 %collective-permute-start.2 = (bf16[1024,256]{1,0:T(8,128)(2,1)S(1)}, bf16[1024,256]{1,0:T(8,128)(2,1)S(1)}, u32[]{:S(2)}, u32[]{:S(2)}) collective-permute-start(bf16[1024,256]{1,0:T(8,128)(2,1)S(1)} %slice_bitcast_fusion.8), channel_id=1, source_target_pairs={{0,4},{4,0},{1,5},{5,1},{2,6},{6,2},{3,7},{7,3}} | collective-permute-start | bytes 1572872 | tf_op jit(solution)/shard_map/ppermute | solution.py:284
  369.0 55.3 %collective-permute-start.1 = (bf16[768,256]{1,0:T(8,128)(2,1)S(1)}, bf16[768,256]{1,0:T(8,128)(2,1)S(1)}, u32[]{:S(2)}, u32[]{:S(2)}) collective-permute-start(bf16[768,256]{1,0:T(8,128)(2,1)S(1)} %slice_bitcast_fusion.9), channel_id=1, source_target_pairs={{0,4},{4,0},{1,5},{5,1},{2,6},{6,2},{3,7},{7,3}} | collective-permute-start | bytes 1179656 | tf_op jit(solution)/shard_map/ppermute | solution.py:284
  369.6 24.4 %collective-permute-start.16 = (bf16[384,256]{1,0:T(8,128)(2,1)S(1)}, bf16[384,256]{1,0:T(8,128)(2,1)S(1)}, u32[]{:S(2)}, u32[]{:S(2)}) collective-permute-start(bf16[384,256]{1,0:T(8,128)(2,1)S(1)} %copy-done.19), channel_id=1, source_target_pairs={{0,4},{4,0},{1,5},{5,1},{2,6},{6,2},{3,7},{7,3}} | collective-permute-start | bytes 589832 | tf_op jit(solution)/shard_map/ppermute | solution.py:284
  374.8 73.8 %collective-permute-start.15 = (bf16[1536,512]{1,0:T(8,128)(2,1)}, bf16[1536,512]{1,0:T(8,128)(2,1)S(1)}, u32[]{:S(2)}, u32[]{:S(2)}) collective-permute-start(bf16[1536,512]{1,0:T(8,128)(2,1)} %get-tuple-element.155), channel_id=1, source_target_pairs={{0,4},{4,0},{1,5},{5,1},{2,6},{6,2},{3,7},{7,3}} | collective-permute-start | bytes 4718600 | tf_op jit(solution)/shard_map/ppermute | solution.py:284
  393.9 53.4 %collective-permute-start.17 = (bf16[384,256]{1,0:T(8,128)(2,1)S(1)}, bf16[384,256]{1,0:T(8,128)(2,1)S(1)}, u32[]{:S(2)}, u32[]{:S(2)}) collective-permute-start(bf16[384,256]{1,0:T(8,128)(2,1)S(1)} %collective-permute-done.16.refs_1_), channel_id=1, source_target_pairs={{0,1},{1,0},{2,3},{3,2},{4,5},{5,4},{6,7},{7,6}} | collective-permute-start | bytes 589832 | tf_op jit(solution)/shard_map/ppermute | solution.py:284
  393.9 1.7 copy-start.15
  440.8 3.7 copy-start.2
  444.5 2.9 copy-start.6
  447.3 2.3 copy-start.18
  448.6 9.2 %collective-permute-start.18 = (bf16[1536,512]{1,0:T(8,128)(2,1)S(1)}, bf16[1536,512]{1,0:T(8,128)(2,1)S(1)}, u32[]{:S(2)}, u32[]{:S(2)}) collective-permute-start(bf16[1536,512]{1,0:T(8,128)(2,1)S(1)} %collective-permute-done.15.refs_1_), channel_id=1, source_target_pairs={{0,1},{1,0},{2,3},{3,2},{4,5},{5,4},{6,7},{7,6}} | collective-permute-start | bytes 4718600 | tf_op jit(solution)/shard_map/ppermute | solution.py:284
  449.6 36.4 %collective-permute-start.14 = (bf16[1536,512]{1,0:T(8,128)(2,1)S(1)}, bf16[1536,512]{1,0:T(8,128)(2,1)S(1)}, u32[]{:S(2)}, u32[]{:S(2)}) collective-permute-start(bf16[1536,512]{1,0:T(8,128)(2,1)S(1)} %copy-done.18), channel_id=1, source_target_pairs={{0,4},{4,0},{1,5},{5,1},{2,6},{6,2},{3,7},{7,3}} | collective-permute-start | bytes 4718600 | tf_op jit(solution)/shard_map/ppermute | solution.py:284
  451.1 4.6 collective-permute-start.19
  451.1 2.8 collective-permute-start.20
  455.7 2.2 copy-start.7
  464.1 25.3 %copy-start.8 = (f32[1536,512]{1,0:T(8,128)S(1)}, f32[1536,512]{1,0:T(8,128)}, u32[]{:S(2)}) copy-start(f32[1536,512]{1,0:T(8,128)} %get-tuple-element.138.refs_3_) | copy-start | bytes 9437188
  486.0 3.4 collective-permute-start.21
  487.5 21.5 %copy-start.5 = (f32[1536,512]{1,0:T(8,128)S(1)}, f32[1536,512]{1,0:T(8,128)}, u32[]{:S(2)}) copy-start(f32[1536,512]{1,0:T(8,128)} %get-tuple-element.143.refs_2_) | copy-start | bytes 9437188
  487.5 20.0 %collective-permute-start.25 = (bf16[1536,256]{1,0:T(8,128)(2,1)S(1)}, bf16[1536,256]{1,0:T(8,128)(2,1)S(1)}, u32[]{:S(2)}, u32[]{:S(2)}) collective-permute-start(bf16[1536,256]{1,0:T(8,128)(2,1)S(1)} %get-tuple-element.153), channel_id=1, source_target_pairs={{0,4},{4,0},{1,5},{5,1},{2,6},{6,2},{3,7},{7,3}} | collective-permute-start | bytes 2359304 | tf_op jit(solution)/shard_map/ppermute | solution.py:284
  507.5 3.2 collective-permute-start.26
  507.5 20.0 %collective-permute-start.24 = (bf16[1536,256]{1,0:T(8,128)(2,1)S(1)}, bf16[1536,256]{1,0:T(8,128)(2,1)S(1)}, u32[]{:S(2)}, u32[]{:S(2)}) collective-permute-start(bf16[1536,256]{1,0:T(8,128)(2,1)S(1)} %get-tuple-element.154), channel_id=1, source_target_pairs={{0,4},{4,0},{1,5},{5,1},{2,6},{6,2},{3,7},{7,3}} | collective-permute-start | bytes 2359304 | tf_op jit(solution)/shard_map/ppermute | solution.py:284
  527.4 4.2 collective-permute-start.27
  528.4 8.7 %collective-permute-start.23 = (bf16[512,256]{1,0:T(8,128)(2,1)S(1)}, bf16[512,256]{1,0:T(8,128)(2,1)S(1)}, u32[]{:S(2)}, u32[]{:S(2)}) collective-permute-start(bf16[512,256]{1,0:T(8,128)(2,1)S(1)} %slice_bitcast_fusion.10), channel_id=1, source_target_pairs={{0,4},{4,0},{1,5},{5,1},{2,6},{6,2},{3,7},{7,3}} | collective-permute-start | bytes 786440 | tf_op jit(solution)/shard_map/ppermute | solution.py:284
  537.1 3.0 collective-permute-start.28
  538.1 7.3 %collective-permute-start.22 = (bf16[384,256]{1,0:T(8,128)(2,1)S(1)}, bf16[384,256]{1,0:T(8,128)(2,1)S(1)}, u32[]{:S(2)}, u32[]{:S(2)}) collective-permute-start(bf16[384,256]{1,0:T(8,128)(2,1)S(1)} %slice_bitcast_fusion.11), channel_id=1, source_target_pairs={{0,4},{4,0},{1,5},{5,1},{2,6},{6,2},{3,7},{7,3}} | collective-permute-start | bytes 589832 | tf_op jit(solution)/shard_map/ppermute | solution.py:284
  545.4 1.4 collective-permute-start.29

commit v6 on v4

--- a/solution.py
+++ b/solution.py
@@ -216,9 +216,12 @@
     k_rows, width = pieces[0].shape
     cross = lax.rem(lax.axis_index("col") + lax.axis_index("row"), 2)
     k_range = pl.ds(k_start, k_rows)
-    tiles = weights.shape[1] // tile_rows
+    unrolled = isinstance(tile_rows, tuple)
+    tiles = len(tile_rows) if unrolled else weights.shape[1] // tile_rows
 
     def rows_of(tile):
+        if unrolled:
+            return pl.ds(sum(tile_rows[:tile]), tile_rows[tile])
         return pl.ds(pl.multiple_of(tile * tile_rows, tile_rows), tile_rows)
 
     def out_copy(tile):
@@ -240,7 +243,11 @@
             out_copy(tile).start()
         return carry
 
-    lax.fori_loop(0, tiles, row_tile, 0)
+    if unrolled:
+        for tile in range(tiles):
+            row_tile(tile, 0)
+    else:
+        lax.fori_loop(0, tiles, row_tile, 0)
     if target is not None:
         for tile in range(tiles):
             out_copy(tile).wait()
@@ -261,7 +268,7 @@
         aliases = {len(operands): 0}
         operands.append(prev)
         in_specs.append(any_spec)
-        scratch = [pltpu.VMEM((rows, width), jnp.bfloat16), pltpu.SemaphoreType.DMA((rows // tile_rows,))]
+        scratch = [pltpu.VMEM((rows, width), jnp.bfloat16), pltpu.SemaphoreType.DMA((len(tile_rows) if isinstance(tile_rows, tuple) else rows // tile_rows,))]
     return pl.pallas_call(
         functools.partial(late_kernel, k_start, base_start, target, flips, tile_rows),
         out_shape=out_shape,
@@ -355,7 +362,7 @@
             piece, relay, y = relay_after(y, name)
             rhs_idx, start, _, k_start, _ = CHUNKS[name]
             part = late_product(weights, (piece,), (0,), part, part_start, k_start, tile_rows=tile_rows)
-            return late_product(weights, (relay,), (1,), part, 0, k_start, prev=y, target=(rhs_idx, start), tile_rows=tile_rows)
+            return late_product(weights, (relay,), (1,), part, 0, k_start, prev=y, target=(rhs_idx, start), tile_rows=(256,) * 6 if tile_rows == SMALL_ROWS else tile_rows)
 
         part_j = early_part("j0", deep["j0"], relay_j0, *base_of("j0"))
         y, part_j = lax.optimization_barrier((y, part_j))

time: 545 us -> 545 us (level)
  no operation moved by 1% of the time
where the time goes in v6:
time: 545 us; the launch traced here: 544 us
  waiting for transfers between devices  264 us (48%)
  Pallas kernels  205 us (38%)
  local copies, waits for them, and re-layouts  50.1 us (9%)
  starting transfers between devices  24 us (4%)
    ppermute x30, waiting for transfers between devices, permute(): return lax.ppermute(value, axis, SWAP)  264 us
    pallas_call x10, Pallas kernels, product(): pl.pallas_call(functools.partial(product_kernel, plan), grid=(len(tiles),...  172 us
    pallas_call x13, Pallas kernels, late_product(): pl.pallas_call(functools.partial(late_kernel, k_start, base_start, target...  29.7 us
    ppermute x30, starting transfers between devices, permute(): return lax.ppermute(value, axis, SWAP)  24 us
    squeeze x10, local copies, waits for them, and re-layouts, piece_of(): return x[rhs_idx, k_start:k_start + k_rows, start:start + width]  23.9 us
    unnamed x46, local copies, waits for them, and re-layouts  20.7 us
  transfers between devices with their start and end apart: 30, of which 14 were waited for; matrix products, arithmetic and copies ran while one was open for 4% of the time, Pallas kernels for 37%

profile of v6, /device:TPU:0, one launch (start us, length us, event | category | flops | bytes accessed | tf_op | source)
XLA Modules:
  0.0 544.3 jit_solution(8521807523524888283)
XLA Ops:
  0.0 1.6 slice_bitcast_fusion.12
  1.6 1.7 slice_bitcast_fusion.5
  3.3 2.2 slice.50
  6.4 4.8 slice_bitcast_fusion
  11.2 2.6 collective-permute-start.8
  13.8 1.5 collective-permute-start.3
  15.8 3.2 fusion
  19.1 131.0 %collective-permute-done.9.refs_3_ = bf16[1536,512]{1,0:T(8,128)(2,1)S(1)} collective-permute-done((bf16[1536,512]{1,0:T(8,128)(2,1)S(1)}, bf16[1536,512]{1,0:T(8,128)(2,1)S(1)}, u32[]{:S(2)}, u32[]{:S(2)}) %collective-permute-start.9) | collective-permute-done | bytes 1572896 | tf_op jit(solution)/shard_map/ppermute | solution.py:290
  150.1 3.4 collective-permute-done.10.refs_5_
  153.5 7.5 %product.10.refs_6_ = bf16[3,1536,2048]{2,1,0:T(8,128)(2,1)} custom-call(bf16[1536,3072]{1,0:T(8,128)(2,1)S(1)} %bitcast.27, bf16[512,3072]{1,0:T(8,128)(2,1)S(1)} %collective-permute-done.3.refs_1_, bf16[3,1536,2048]{2,1,0:T(8,128)(2,1)} %refs_2_.13, bf16[1536,512]{1,0:T(8,128)(2,1)S(1)} %collective-permute-done.9.refs_3_, ...), custom_call_target="tpu_custom_call" | custom-call | flops 3221225472 | bytes 6291456 | tf_op jit(solution)/shard_map/product/pallas_call | solution.py:164
  161.0 1.2 copy-done.11
  162.2 14.6 %product.11 = (f32[1536,512]{1,0:T(8,128)}, f32[1536,512]{1,0:T(8,128)}, f32[1536,512]{1,0:T(8,128)}, f32[1536,512]{1,0:T(8,128)}) custom-call(bf16[1536,3072]{1,0:T(8,128)(2,1)} %refs_0_.20, bf16[512,3072]{1,0:T(8,128)(2,1)} %copy-done.3, bf16[3,1536,2048]{2,1,0:T(8,128)(2,1)} %refs_2_.13, ...), custom_call_target="tpu_custom_call" | custom-call | flops 6442450944 | bytes 6291456 | tf_op jit(solution)/shard_map/product/pallas_call | solution.py:164
  176.8 3.7 copy-done
  180.5 1.4 copy-done.12
  181.9 8.2 %product.12.refs_7_ = bf16[3,1536,2048]{2,1,0:T(8,128)(2,1)} custom-call(bf16[1536,3072]{1,0:T(8,128)(2,1)S(1)} %copy-done, bf16[512,3072]{1,0:T(8,128)(2,1)} %collective-permute-done.4.refs_1_.refs_2_, bf16[3,1536,2048]{2,1,0:T(8,128)(2,1)} %refs_2_.13, bf16[1536,512]{1,0:T(8,128)(2,1)S(1)} %collective-permute-done.9.refs_3_, ...), custom_call_target="tpu_custom_call", output_to_operand_aliasing={{}: (6, {})} | custom-call | flops 3221225472 | bytes 6291456 | tf_op jit(solution)/shard_map/product/pallas_call | solution.py:164
  190.2 1.8 collective-permute-start.5
  192.0 6.3 %slice_bitcast_fusion.1 = (bf16[1536,1024]{1,0:T(8,128)(2,1)}, bf16[1536,1024]{1,0:T(8,128)(2,1)}) fusion(bf16[3,1536,2048]{2,1,0:T(8,128)(2,1)} %refs_2_.13), kind=kLoop, calls=%fused_computation.1 | loop fusion | bytes 12582912 | tf_op jit(solution)/shard_map/squeeze | solution.py:299
  198.3 1.5 collective-permute-start.7
  199.9 2.2 copy-done.9
  202.0 28.8 %product.13.refs_6_ = bf16[3,1536,2048]{2,1,0:T(8,128)(2,1)} custom-call(bf16[1536,3072]{1,0:T(8,128)(2,1)} %refs_0_.20, bf16[512,3072]{1,0:T(8,128)(2,1)S(1)} %copy-done.4, bf16[512,3072]{1,0:T(8,128)(2,1)} %collective-permute-done.4.refs_1_.refs_2_, bf16[3,1536,2048]{2,1,0:T(8,128)(2,1)} %refs_2_.13, ...), custom_call_target="tpu_custom_call", output_to_operand_aliasing={{}: (7, {})} | custom-call | flops 19327352832 | bytes 12582912 | tf_op jit(solution)/shard_map/product/pallas_call | solution.py:164
  230.8 14.7 %product.14 = (f32[1536,512]{1,0:T(8,128)}, f32[1536,512]{1,0:T(8,128)}, f32[1536,512]{1,0:T(8,128)}, f32[1536,512]{1,0:T(8,128)}) custom-call(bf16[1536,3072]{1,0:T(8,128)(2,1)} %refs_0_.20, bf16[512,3072]{1,0:T(8,128)(2,1)} %collective-permute-done.4.refs_1_.refs_2_, ...), custom_call_target="tpu_custom_call", output_to_operand_aliasing={{0}: (4, {}), {1}: (5, {}), {2}: (6, {}), {3}: (7, {})} | custom-call | flops 6442450944 | bytes 6291456 | tf_op jit(solution)/shard_map/product/pallas_call | solution.py:164
  245.5 15.5 %collective-permute-done.5.refs_1_.refs_3_ = bf16[512,3072]{1,0:T(8,128)(2,1)} collective-permute-done((bf16[512,3072]{1,0:T(8,128)(2,1)}, bf16[512,3072]{1,0:T(8,128)(2,1)}, u32[]{:S(2)}, u32[]{:S(2)}) %collective-permute-start.5) | collective-permute-done | bytes 3145760 | tf_op jit(solution)/shard_map/ppermute | solution.py:290
  261.0 3.7 copy-done.1
  264.7 1.4 copy-done.13
  266.1 8.5 %product.15.refs_6_ = bf16[3,1536,2048]{2,1,0:T(8,128)(2,1)} custom-call(bf16[1536,3072]{1,0:T(8,128)(2,1)S(1)} %copy-done.1, bf16[512,3072]{1,0:T(8,128)(2,1)} %collective-permute-done.5.refs_1_.refs_3_, bf16[3,1536,2048]{2,1,0:T(8,128)(2,1)} %refs_2_.13, bf16[1536,512]{1,0:T(8,128)(2,1)S(1)} %collective-permute-done.9.refs_3_, ...), custom_call_target="tpu_custom_call", output_to_operand_aliasing={{}: (6, {})} | custom-call | flops 3221225472 | bytes 6291456 | tf_op jit(solution)/shard_map/product/pallas_call | solution.py:164
  274.6 17.9 %product.16.refs_8_ = bf16[3,1536,2048]{2,1,0:T(8,128)(2,1)} custom-call(bf16[1536,3072]{1,0:T(8,128)(2,1)} %refs_0_.20, bf16[512,3072]{1,0:T(8,128)(2,1)} %collective-permute-done.5.refs_1_.refs_3_, bf16[3,1536,2048]{2,1,0:T(8,128)(2,1)} %refs_2_.13, bf16[1536,1536]{1,0:T(8,128)(2,1)} %collective-permute-done.8.refs_4_.refs_3_, ...), custom_call_target="tpu_custom_call", output_to_operand_aliasing={{}: (6, {})} | custom-call | flops 9663676416 | bytes 6291456 | tf_op jit(solution)/shard_map/product/pallas_call | solution.py:164
  292.6 1.8 collective-permute-start.6
  294.4 4.1 collective-permute-done.12.refs_7_
  298.4 1.7 copy-done.16
  300.1 28.8 %product.17.refs_8_ = bf16[3,1536,2048]{2,1,0:T(8,128)(2,1)} custom-call(bf16[1536,3072]{1,0:T(8,128)(2,1)} %refs_0_.20, bf16[512,3072]{1,0:T(8,128)(2,1)S(1)} %copy-done.4, bf16[512,3072]{1,0:T(8,128)(2,1)} %collective-permute-done.4.refs_1_.refs_2_, bf16[512,3072]{1,0:T(8,128)(2,1)} %collective-permute-done.5.refs_1_.refs_3_, ...), custom_call_target="tpu_custom_call", output_to_operand_aliasing={{}: (8, {})} | custom-call | flops 19327352832 | bytes 18874368 | tf_op jit(solution)/shard_map/product/pallas_call | solution.py:164
  328.9 34.1 %collective-permute-done.6.refs_5_ = bf16[1536,1024]{1,0:T(8,128)(2,1)S(1)} collective-permute-done((bf16[1536,1024]{1,0:T(8,128)(2,1)S(1)}, bf16[1536,1024]{1,0:T(8,128)(2,1)S(1)}, u32[]{:S(2)}, u32[]{:S(2)}) %collective-permute-start.6) | collective-permute-done | bytes 3145760 | tf_op jit(solution)/shard_map/ppermute | solution.py:290
  363.1 1.5 slice_bitcast_fusion.8
  364.5 1.8 collective-permute-start.2
  367.6 1.7 collective-permute-start.16
  369.4 3.7 slice_bitcast_fusion.3
  373.4 18.6 %collective-permute-done.16.refs_1_ = bf16[384,256]{1,0:T(8,128)(2,1)S(1)} collective-permute-done((bf16[384,256]{1,0:T(8,128)(2,1)S(1)}, bf16[384,256]{1,0:T(8,128)(2,1)S(1)}, u32[]{:S(2)}, u32[]{:S(2)}) %collective-permute-start.16) | collective-permute-done | bytes 196640 | tf_op jit(solution)/shard_map/ppermute | solution.py:290
  392.0 1.7 copy-done.15
  393.7 28.8 %product.18.refs_4_ = bf16[3,1536,2048]{2,1,0:T(8,128)(2,1)} custom-call(bf16[1536,3072]{1,0:T(8,128)(2,1)} %refs_0_.20, bf16[512,3072]{1,0:T(8,128)(2,1)S(1)} %copy-done.4, bf16[512,3072]{1,0:T(8,128)(2,1)} %collective-permute-done.4.refs_1_.refs_2_, bf16[512,3072]{1,0:T(8,128)(2,1)} %collective-permute-done.5.refs_1_.refs_3_, ...), custom_call_target="tpu_custom_call", output_to_operand_aliasing={{}: (8, {})} | custom-call | flops 19327352832 | bytes 18874368 | tf_op jit(solution)/shard_map/product/pallas_call | solution.py:164
  422.6 14.7 %product.19 = (f32[1536,512]{1,0:T(8,128)}, f32[1536,512]{1,0:T(8,128)}, f32[1536,512]{1,0:T(8,128)}, f32[1536,512]{1,0:T(8,128)}) custom-call(bf16[1536,3072]{1,0:T(8,128)(2,1)} %refs_0_.20, bf16[512,3072]{1,0:T(8,128)(2,1)} %collective-permute-done.5.refs_1_.refs_3_, ...), custom_call_target="tpu_custom_call", output_to_operand_aliasing={{0}: (4, {}), {1}: (5, {}), {2}: (6, {}), {3}: (7, {})} | custom-call | flops 6442450944 | bytes 6291456 | tf_op jit(solution)/shard_map/product/pallas_call | solution.py:164
  437.2 3.7 copy-done.2
  440.9 2.9 late_weights.1.refs_0_
  443.8 1.3 late.13.refs_3_
  445.2 1.7 collective-permute-start.14
  447.4 2.4 collective-permute-done.20.refs_2_
  449.9 1.7 late.16.refs_2_
  451.6 2.1 late.15.refs_2_
  453.8 6.2 %late.14.refs_4_ = bf16[3,1536,2048]{2,1,0:T(8,128)(2,1)} custom-call(bf16[2,1536,1536]{2,1,0:T(8,128)(2,1)S(1)} %late_weights.1.refs_0_, bf16[1536,512]{1,0:T(8,128)(2,1)S(1)} %collective-permute-done.15.refs_1_, bf16[1536,512]{1,0:T(8,128)(2,1)S(1)} %collective-permute-done.18.refs_2_, f32[1536,512]{1,0:T(8,128)S(1)} %copy-done.7, ...), custom_call_target="tpu_custom_call", output_to_operand_aliasing={{}: (4, {})} | custom-call | flops 4831838208 | bytes 3145728 | tf_op jit(solution)/shard_map/late/pallas_call | solution.py:272
  460.0 21.9 %collective-permute-done.14.refs_1_ = bf16[1536,512]{1,0:T(8,128)(2,1)S(1)} collective-permute-done((bf16[1536,512]{1,0:T(8,128)(2,1)S(1)}, bf16[1536,512]{1,0:T(8,128)(2,1)S(1)}, u32[]{:S(2)}, u32[]{:S(2)}) %collective-permute-start.14) | collective-permute-done | bytes 1572896 | tf_op jit(solution)/shard_map/ppermute | solution.py:290
  482.0 1.5 slice_bitcast_fusion.6
  483.5 1.7 collective-permute-start.25
  485.4 6.2 %late.17.refs_3_ = bf16[3,1536,2048]{2,1,0:T(8,128)(2,1)} custom-call(bf16[2,1536,1536]{2,1,0:T(8,128)(2,1)S(1)} %late_weights.1.refs_0_, bf16[1536,512]{1,0:T(8,128)(2,1)S(1)} %collective-permute-done.14.refs_1_, bf16[1536,512]{1,0:T(8,128)(2,1)S(1)} %collective-permute-done.21.refs_2_, f32[1536,512]{1,0:T(8,128)S(1)} %copy-done.8, ...), custom_call_target="tpu_custom_call", output_to_operand_aliasing={{}: (4, {})} | custom-call | flops 4831838208 | bytes 3145728 | tf_op jit(solution)/shard_map/late/pallas_call | solution.py:272
  491.6 11.9 %collective-permute-done.25.refs_1_ = bf16[1536,256]{1,0:T(8,128)(2,1)S(1)} collective-permute-done((bf16[1536,256]{1,0:T(8,128)(2,1)S(1)}, bf16[1536,256]{1,0:T(8,128)(2,1)S(1)}, u32[]{:S(2)}, u32[]{:S(2)}) %collective-permute-start.25) | collective-permute-done | bytes 786464 | tf_op jit(solution)/shard_map/ppermute | solution.py:290
  503.4 1.7 collective-permute-start.24
  505.2 1.7 late.18.refs_2_
  506.9 2.5 late.19.refs_3_
  509.4 14.0 %collective-permute-done.24.refs_1_ = bf16[1536,256]{1,0:T(8,128)(2,1)S(1)} collective-permute-done((bf16[1536,256]{1,0:T(8,128)(2,1)S(1)}, bf16[1536,256]{1,0:T(8,128)(2,1)S(1)}, u32[]{:S(2)}, u32[]{:S(2)}) %collective-permute-start.24) | collective-permute-done | bytes 786464 | tf_op jit(solution)/shard_map/ppermute | solution.py:290
  524.4 1.7 collective-permute-start.23
  526.1 1.7 late.20.refs_2_
  527.9 2.5 late.21.refs_3_
  530.3 2.8 collective-permute-done.23.refs_1_
  534.0 1.7 collective-permute-start.22
  536.4 1.3 late.23.refs_3_
  537.7 3.7 collective-permute-done.22.refs_1_
  542.8 1.3 late.25
  (79 shorter events, 7.9 us)
Async XLA Ops:
  1.6 14.2 %slice-start = ((s8[9437184]{0:T(1024)(128)(4,1)}), s8[4194304]{0:T(1024)(128)(4,1)S(1)}, s32[]{:S(2)}) async-start(s8[9437184]{0:T(1024)(128)(4,1)} %bitcast.26), calls=%async_computation | async-start | bytes 8388608
  3.3 12.5 %slice-start.1 = ((s8[9437184]{0:T(1024)(128)(4,1)}), s8[4194304]{0:T(1024)(128)(4,1)S(1)}, s32[]{:S(2)}) async-start(s8[9437184]{0:T(1024)(128)(4,1)} %bitcast.26), calls=%async_computation.1 | async-start | bytes 8388608
  5.5 10.3 %slice-start.2 = ((s8[9437184]{0:T(1024)(128)(4,1)}), s8[1048576]{0:T(1024)(128)(4,1)S(1)}, s32[]{:S(2)}) async-start(s8[9437184]{0:T(1024)(128)(4,1)} %bitcast.26), calls=%async_computation.2 | async-start | bytes 2097152
  5.6 148.0 %collective-permute-start = (bf16[3,1536,2048]{2,1,0:T(8,128)(2,1)}, bf16[3,1536,2048]{2,1,0:T(8,128)(2,1)}, u32[]{:S(2)}, u32[]{:S(2)}) collective-permute-start(bf16[3,1536,2048]{2,1,0:T(8,128)(2,1)} %refs_2_.13), channel_id=1, source_target_pairs={{0,1},{1,0},{2,3},{3,2},{4,5},{5,4},{6,7},{7,6}} | collective-permute-start | bytes 56623112 | tf_op jit(solution)/shard_map/ppermute | solution.py:290
  11.2 179.0 %collective-permute-start.8 = (bf16[1536,1536]{1,0:T(8,128)(2,1)}, bf16[1536,1536]{1,0:T(8,128)(2,1)}, u32[]{:S(2)}, u32[]{:S(2)}) collective-permute-start(bf16[1536,1536]{1,0:T(8,128)(2,1)} %slice_bitcast_fusion), channel_id=1, source_target_pairs={{0,4},{4,0},{1,5},{5,1},{2,6},{6,2},{3,7},{7,3}} | collective-permute-start | bytes 14155784 | tf_op jit(solution)/shard_map/ppermute | solution.py:290
  13.8 136.3 %collective-permute-start.3 = (bf16[512,3072]{1,0:T(8,128)(2,1)S(1)}, bf16[512,3072]{1,0:T(8,128)(2,1)S(1)}, u32[]{:S(2)}, u32[]{:S(2)}) collective-permute-start(bf16[512,3072]{1,0:T(8,128)(2,1)S(1)} %slice.50), channel_id=1, source_target_pairs={{0,2},{2,0},{1,3},{3,1},{4,6},{6,4},{5,7},{7,5}} | collective-permute-start | bytes 9437192 | tf_op jit(solution)/shard_map/ppermute | solution.py:290
  15.3 134.8 %collective-permute-start.9 = (bf16[1536,512]{1,0:T(8,128)(2,1)S(1)}, bf16[1536,512]{1,0:T(8,128)(2,1)S(1)}, u32[]{:S(2)}, u32[]{:S(2)}) collective-permute-start(bf16[1536,512]{1,0:T(8,128)(2,1)S(1)} %slice_bitcast_fusion.5), channel_id=1, source_target_pairs={{0,4},{4,0},{1,5},{5,1},{2,6},{6,2},{3,7},{7,3}} | collective-permute-start | bytes 4718600 | tf_op jit(solution)/shard_map/ppermute | solution.py:290
  19.0 157.8 %collective-permute-start.4 = (bf16[512,3072]{1,0:T(8,128)(2,1)}, bf16[512,3072]{1,0:T(8,128)(2,1)}, u32[]{:S(2)}, u32[]{:S(2)}) collective-permute-start(bf16[512,3072]{1,0:T(8,128)(2,1)} %get-tuple-element.160), channel_id=1, source_target_pairs={{0,2},{2,0},{1,3},{3,1},{4,6},{6,4},{5,7},{7,5}} | collective-permute-start | bytes 9437192 | tf_op jit(solution)/shard_map/ppermute | solution.py:290
  150.1 3.4 collective-permute-start.10
  150.1 10.9 %copy-start.3 = (bf16[512,3072]{1,0:T(8,128)(2,1)}, bf16[512,3072]{1,0:T(8,128)(2,1)S(1)}, u32[]{:S(2)}) copy-start(bf16[512,3072]{1,0:T(8,128)(2,1)S(1)} %collective-permute-done.3.refs_1_) | copy-start | bytes 9437188
  161.0 1.2 copy-start.11
  176.8 3.7 copy-start
  180.5 1.4 copy-start.12
  190.2 9.7 %collective-permute-start.11 = (bf16[1536,1536]{1,0:T(8,128)(2,1)}, bf16[1536,1536]{1,0:T(8,128)(2,1)S(1)}, u32[]{:S(2)}, u32[]{:S(2)}) collective-permute-start(bf16[1536,1536]{1,0:T(8,128)(2,1)} %collective-permute-done.8.refs_4_.refs_3_), channel_id=1, source_target_pairs={{0,1},{1,0},{2,3},{3,2},{4,5},{5,4},{6,7},{7,6}} | collective-permute-start | bytes 14155784 | tf_op jit(solution)/shard_map/ppermute | solution.py:290
  190.2 11.8 %copy-start.4 = (bf16[512,3072]{1,0:T(8,128)(2,1)S(1)}, bf16[512,3072]{1,0:T(8,128)(2,1)}, u32[]{:S(2)}) copy-start(bf16[512,3072]{1,0:T(8,128)(2,1)} %copy-done.3) | copy-start | bytes 9437188
  190.2 70.8 %collective-permute-start.5 = (bf16[512,3072]{1,0:T(8,128)(2,1)}, bf16[512,3072]{1,0:T(8,128)(2,1)}, u32[]{:S(2)}, u32[]{:S(2)}) collective-permute-start(bf16[512,3072]{1,0:T(8,128)(2,1)} %get-tuple-element.159), channel_id=1, source_target_pairs={{0,2},{2,0},{1,3},{3,1},{4,6},{6,4},{5,7},{7,5}} | collective-permute-start | bytes 9437192 | tf_op jit(solution)/shard_map/ppermute | solution.py:290
  198.3 94.2 %collective-permute-start.7 = (bf16[1536,1024]{1,0:T(8,128)(2,1)}, bf16[1536,1024]{1,0:T(8,128)(2,1)}, u32[]{:S(2)}, u32[]{:S(2)}) collective-permute-start(bf16[1536,1024]{1,0:T(8,128)(2,1)} %get-tuple-element.157), channel_id=1, source_target_pairs={{0,4},{4,0},{1,5},{5,1},{2,6},{6,2},{3,7},{7,3}} | collective-permute-start | bytes 9437192 | tf_op jit(solution)/shard_map/ppermute | solution.py:290
  199.8 2.2 copy-start.9
  261.0 3.7 copy-start.1
  264.7 1.4 copy-start.13
  266.1 8.5 %copy-start.10 = (bf16[1536,1536]{1,0:T(8,128)(2,1)S(1)}, bf16[1536,1536]{1,0:T(8,128)(2,1)}, u32[]{:S(2)}) copy-start(bf16[1536,1536]{1,0:T(8,128)(2,1)} %copy-done.9) | copy-start | bytes 14155780
  274.6 17.9 %copy-start.17 = (bf16[1536,1024]{1,0:T(8,128)(2,1)S(1)}, bf16[1536,1024]{1,0:T(8,128)(2,1)}, u32[]{:S(2)}) copy-start(bf16[1536,1024]{1,0:T(8,128)(2,1)} %get-tuple-element.158) | copy-start | bytes 9437188
  292.5 5.9 %collective-permute-start.12 = (bf16[1536,1024]{1,0:T(8,128)(2,1)}, bf16[1536,1024]{1,0:T(8,128)(2,1)S(1)}, u32[]{:S(2)}, u32[]{:S(2)}) collective-permute-start(bf16[1536,1024]{1,0:T(8,128)(2,1)} %collective-permute-done.7.refs_5_), channel_id=1, source_target_pairs={{0,1},{1,0},{2,3},{3,2},{4,5},{5,4},{6,7},{7,6}} | collective-permute-start | bytes 9437192 | tf_op jit(solution)/shard_map/ppermute | solution.py:290
  292.6 75.1 %copy-start.19 = (bf16[384,256]{1,0:T(8,128)(2,1)S(1)}, bf16[384,256]{1,0:T(8,128)(2,1)}, u32[]{:S(2)}) copy-start(bf16[384,256]{1,0:T(8,128)(2,1)} %slice_bitcast_fusion.12) | copy-start | bytes 589828
  292.6 70.5 %collective-permute-start.6 = (bf16[1536,1024]{1,0:T(8,128)(2,1)S(1)}, bf16[1536,1024]{1,0:T(8,128)(2,1)S(1)}, u32[]{:S(2)}, u32[]{:S(2)}) collective-permute-start(bf16[1536,1024]{1,0:T(8,128)(2,1)S(1)} %copy-done.17), channel_id=1, source_target_pairs={{0,4},{4,0},{1,5},{5,1},{2,6},{6,2},{3,7},{7,3}} | collective-permute-start | bytes 9437192 | tf_op jit(solution)/shard_map/ppermute | solution.py:290
  298.4 1.7 copy-start.16
  363.1 10.0 %copy-start.14 = (bf16[1536,1024]{1,0:T(8,128)(2,1)}, bf16[1536,1024]{1,0:T(8,128)(2,1)S(1)}, u32[]{:S(2)}) copy-start(bf16[1536,1024]{1,0:T(8,128)(2,1)S(1)} %collective-permute-done.6.refs_5_) | copy-start | bytes 9437188
  363.1 28.9 %collective-permute-start.13 = (bf16[1536,1024]{1,0:T(8,128)(2,1)S(1)}, bf16[1536,1024]{1,0:T(8,128)(2,1)S(1)}, u32[]{:S(2)}, u32[]{:S(2)}) collective-permute-start(bf16[1536,1024]{1,0:T(8,128)(2,1)S(1)} %collective-permute-done.6.refs_5_), channel_id=1, source_target_pairs={{0,1},{1,0},{2,3},{3,2},{4,5},{5,4},{6,7},{7,6}} | collective-permute-start | bytes 9437192 | tf_op jit(solution)/shard_map/ppermute | solution.py:290
  364.5 58.0 %collective-permute-start.2 = (bf16[1024,256]{1,0:T(8,128)(2,1)S(1)}, bf16[1024,256]{1,0:T(8,128)(2,1)S(1)}, u32[]{:S(2)}, u32[]{:S(2)}) collective-permute-start(bf16[1024,256]{1,0:T(8,128)(2,1)S(1)} %slice_bitcast_fusion.8), channel_id=1, source_target_pairs={{0,4},{4,0},{1,5},{5,1},{2,6},{6,2},{3,7},{7,3}} | collective-permute-start | bytes 1572872 | tf_op jit(solution)/shard_map/ppermute | solution.py:290
  367.3 55.2 %collective-permute-start.1 = (bf16[768,256]{1,0:T(8,128)(2,1)S(1)}, bf16[768,256]{1,0:T(8,128)(2,1)S(1)}, u32[]{:S(2)}, u32[]{:S(2)}) collective-permute-start(bf16[768,256]{1,0:T(8,128)(2,1)S(1)} %slice_bitcast_fusion.9), channel_id=1, source_target_pairs={{0,4},{4,0},{1,5},{5,1},{2,6},{6,2},{3,7},{7,3}} | collective-permute-start | bytes 1179656 | tf_op jit(solution)/shard_map/ppermute | solution.py:290
  367.6 24.4 %collective-permute-start.16 = (bf16[384,256]{1,0:T(8,128)(2,1)S(1)}, bf16[384,256]{1,0:T(8,128)(2,1)S(1)}, u32[]{:S(2)}, u32[]{:S(2)}) collective-permute-start(bf16[384,256]{1,0:T(8,128)(2,1)S(1)} %copy-done.19), channel_id=1, source_target_pairs={{0,4},{4,0},{1,5},{5,1},{2,6},{6,2},{3,7},{7,3}} | collective-permute-start | bytes 589832 | tf_op jit(solution)/shard_map/ppermute | solution.py:290
  373.1 72.0 %collective-permute-start.15 = (bf16[1536,512]{1,0:T(8,128)(2,1)}, bf16[1536,512]{1,0:T(8,128)(2,1)S(1)}, u32[]{:S(2)}, u32[]{:S(2)}) collective-permute-start(bf16[1536,512]{1,0:T(8,128)(2,1)} %get-tuple-element.155), channel_id=1, source_target_pairs={{0,4},{4,0},{1,5},{5,1},{2,6},{6,2},{3,7},{7,3}} | collective-permute-start | bytes 4718600 | tf_op jit(solution)/shard_map/ppermute | solution.py:290
  392.0 51.8 %collective-permute-start.17 = (bf16[384,256]{1,0:T(8,128)(2,1)S(1)}, bf16[384,256]{1,0:T(8,128)(2,1)S(1)}, u32[]{:S(2)}, u32[]{:S(2)}) collective-permute-start(bf16[384,256]{1,0:T(8,128)(2,1)S(1)} %collective-permute-done.16.refs_1_), channel_id=1, source_target_pairs={{0,1},{1,0},{2,3},{3,2},{4,5},{5,4},{6,7},{7,6}} | collective-permute-start | bytes 589832 | tf_op jit(solution)/shard_map/ppermute | solution.py:290
  392.0 1.7 copy-start.15
  437.2 3.7 copy-start.2
  440.9 2.9 copy-start.6
  443.8 1.4 copy-start.18
  445.1 8.6 %collective-permute-start.18 = (bf16[1536,512]{1,0:T(8,128)(2,1)S(1)}, bf16[1536,512]{1,0:T(8,128)(2,1)S(1)}, u32[]{:S(2)}, u32[]{:S(2)}) collective-permute-start(bf16[1536,512]{1,0:T(8,128)(2,1)S(1)} %collective-permute-done.15.refs_1_), channel_id=1, source_target_pairs={{0,1},{1,0},{2,3},{3,2},{4,5},{5,4},{6,7},{7,6}} | collective-permute-start | bytes 4718600 | tf_op jit(solution)/shard_map/ppermute | solution.py:290
  445.2 36.8 %collective-permute-start.14 = (bf16[1536,512]{1,0:T(8,128)(2,1)S(1)}, bf16[1536,512]{1,0:T(8,128)(2,1)S(1)}, u32[]{:S(2)}, u32[]{:S(2)}) collective-permute-start(bf16[1536,512]{1,0:T(8,128)(2,1)S(1)} %copy-done.18), channel_id=1, source_target_pairs={{0,4},{4,0},{1,5},{5,1},{2,6},{6,2},{3,7},{7,3}} | collective-permute-start | bytes 4718600 | tf_op jit(solution)/shard_map/ppermute | solution.py:290
  446.9 4.7 collective-permute-start.19
  447.1 2.8 collective-permute-start.20
  451.6 2.2 copy-start.7
  460.0 25.4 %copy-start.8 = (f32[1536,512]{1,0:T(8,128)S(1)}, f32[1536,512]{1,0:T(8,128)}, u32[]{:S(2)}) copy-start(f32[1536,512]{1,0:T(8,128)} %get-tuple-element.138.refs_3_) | copy-start | bytes 9437188
  481.9 3.4 collective-permute-start.21
  483.4 21.7 %copy-start.5 = (f32[1536,512]{1,0:T(8,128)S(1)}, f32[1536,512]{1,0:T(8,128)}, u32[]{:S(2)}) copy-start(f32[1536,512]{1,0:T(8,128)} %get-tuple-element.143.refs_2_) | copy-start | bytes 9437188
  483.5 20.0 %collective-permute-start.25 = (bf16[1536,256]{1,0:T(8,128)(2,1)S(1)}, bf16[1536,256]{1,0:T(8,128)(2,1)S(1)}, u32[]{:S(2)}, u32[]{:S(2)}) collective-permute-start(bf16[1536,256]{1,0:T(8,128)(2,1)S(1)} %get-tuple-element.153), channel_id=1, source_target_pairs={{0,4},{4,0},{1,5},{5,1},{2,6},{6,2},{3,7},{7,3}} | collective-permute-start | bytes 2359304 | tf_op jit(solution)/shard_map/ppermute | solution.py:290
  503.4 3.5 collective-permute-start.26
  503.4 20.0 %collective-permute-start.24 = (bf16[1536,256]{1,0:T(8,128)(2,1)S(1)}, bf16[1536,256]{1,0:T(8,128)(2,1)S(1)}, u32[]{:S(2)}, u32[]{:S(2)}) collective-permute-start(bf16[1536,256]{1,0:T(8,128)(2,1)S(1)} %get-tuple-element.154), channel_id=1, source_target_pairs={{0,4},{4,0},{1,5},{5,1},{2,6},{6,2},{3,7},{7,3}} | collective-permute-start | bytes 2359304 | tf_op jit(solution)/shard_map/ppermute | solution.py:290
  523.4 4.5 collective-permute-start.27
  524.4 8.7 %collective-permute-start.23 = (bf16[512,256]{1,0:T(8,128)(2,1)S(1)}, bf16[512,256]{1,0:T(8,128)(2,1)S(1)}, u32[]{:S(2)}, u32[]{:S(2)}) collective-permute-start(bf16[512,256]{1,0:T(8,128)(2,1)S(1)} %slice_bitcast_fusion.10), channel_id=1, source_target_pairs={{0,4},{4,0},{1,5},{5,1},{2,6},{6,2},{3,7},{7,3}} | collective-permute-start | bytes 786440 | tf_op jit(solution)/shard_map/ppermute | solution.py:290
  533.1 3.3 collective-permute-start.28
  534.0 7.3 %collective-permute-start.22 = (bf16[384,256]{1,0:T(8,128)(2,1)S(1)}, bf16[384,256]{1,0:T(8,128)(2,1)S(1)}, u32[]{:S(2)}, u32[]{:S(2)}) collective-permute-start(bf16[384,256]{1,0:T(8,128)(2,1)S(1)} %slice_bitcast_fusion.11), channel_id=1, source_target_pairs={{0,4},{4,0},{1,5},{5,1},{2,6},{6,2},{3,7},{7,3}} | collective-permute-start | bytes 589832 | tf_op jit(solution)/shard_map/ppermute | solution.py:290
  541.4 1.4 collective-permute-start.29
